TPU v7x, 128 devices: a whole 4x4x4 slice. The times are simulated.
128 devices in a mesh: gx: 8 (over x, z_lo), gy: 16 (over z_hi, y, core).
Axes of the slice: x: 4, y: 4, z: 4 (z_hi: 2, z_lo: 2; z = z_hi * 2 + z_lo), core: 2. Of those that a mesh axis runs over, the one named last changes fastest.
Arguments:
- position: float32 [2, 48, 96, 128], P(None, 'gx', 'gy'), may hold values from 0 to 1
- velocity: float32 [2, 48, 96, 128], P(None, 'gx', 'gy'), may hold values from -3 to 3
- other_accel: float32 [2, 48, 96, 128], P(None, 'gx', 'gy'), may hold values from -5 to 5
- phase_ids: int32 [48, 96, 128], P('gx', 'gy'), may hold values from 0 to 1, as said below
- counts: int32 [48, 96], P('gx', 'gy'), may hold values from 48 to 128, as said below
Outputs:
- new_position: float32 [2, 48, 96, 128], P(None, 'gx', 'gy')
- new_velocity: float32 [2, 48, 96, 128], P(None, 'gx', 'gy')
- pressure: float32 [48, 96, 128], P('gx', 'gy')
- monitor: float32 [4, 4], replicated
Inputs may be any that keep to these rules, and one draw needn't show every extreme that they name: `counts`: each entry is the number of live slots of its cell; the live slots are the first ones of the cell; some cell holds 128. `phase_ids`: both phases occur among the live slots.
All inputs are finite; a program needn't handle non-finite values.
Results may differ from a plain program's by a relative error of at most 0.0001.
Values sent between devices are 32-bit elements; how exact they have to be, the bound alone decides.
No kernel may reach another device: no remote copies, remote signals or barrier semaphores. Data moves between devices by JAX's collectives and lax.ppermute only.
A program may use at most 64 MiB of HBM per device.

v0:
```python
import jax
import jax.numpy as jnp
from jax import lax
from jax.sharding import Mesh
from jax.sharding import PartitionSpec as P

ITERS = 4
GX_GY = ("gx_0", "gx_1", "gy_0", "gy_1", "gy_2")
GX = ("gx_0", "gx_1")
GY = ("gy_0", "gy_1", "gy_2")


TIME_STEP = 0.05
KERNEL_NORM = 4.0 / (3.141592653589793 * 64.0)
REST_LIGHT = 1.2
REST_HEAVY = 1.5
STIFF_LIGHT = 100.0
STIFF_HEAVY = 200.0
MASS_LIGHT = 1.0
MASS_HEAVY = 1.5
SENTINEL = 1e30


def one_axis_at_a_time(value, axes):
    for axis in axes:
        value = lax.pmax(value, axis)
    return value


def padded(block, sides, width):
    for axis, dim in sides:
        count = lax.axis_size(axis)
        forward = [(i, i + 1) for i in range(count - 1)]
        forward.append((count - 1, 0))
        backward = [(target, source) for source, target in forward]
        low = lax.ppermute(
            lax.slice_in_dim(block, block.shape[dim] - width, None, axis=dim), axis, forward
        )
        high = lax.ppermute(lax.slice_in_dim(block, 0, width, axis=dim), axis, backward)
        block = jnp.concatenate([low, block, high], axis=dim)
    return block


def window_of(source, off_x, off_y, row_count, col_count):
    return source[1 + off_x : 1 + off_x + row_count, 1 + off_y : 1 + off_y + col_count]


def pair_sums(centers, padded_list, with_force):
    center_x, center_y = (centers[0], centers[1])
    near_x, near_y, near_live = (padded_list[0], padded_list[1], padded_list[2])
    row_count, col_count = (center_x.shape[0], center_x.shape[1])
    total_a = jnp.zeros_like(center_x)
    total_b = jnp.zeros_like(center_x)
    for off_x in (-1, 0, 1):
        for off_y in (-1, 0, 1):
            other_x = window_of(near_x, off_x, off_y, row_count, col_count)
            other_y = window_of(near_y, off_x, off_y, row_count, col_count)
            other_live = window_of(near_live, off_x, off_y, row_count, col_count)
            diff_x = center_x[..., :, None] - (other_x[..., None, :] + off_x)
            diff_y = center_y[..., :, None] - (other_y[..., None, :] + off_y)
            intersection = (
                jnp.maximum(1.0 - diff_x * diff_x - diff_y * diff_y, 0.0) * other_live[..., None, :]
            )
            if with_force:
                other_term = window_of(padded_list[3], off_x, off_y, row_count, col_count)
                pair_coef = (
                    intersection
                    * intersection
                    * (centers[2][..., :, None] + other_term[..., None, :])
                )
                total_a = total_a + jnp.sum(pair_coef * diff_x, axis=-1)
                total_b = total_b + jnp.sum(pair_coef * diff_y, axis=-1)
            else:
                total_a = total_a + jnp.sum(intersection * intersection * intersection, axis=-1)
    if with_force:
        return (total_a, total_b)
    return (total_a,)


def blocked(with_force, centers, padded_list, row_count):
    block_count = row_count // 2

    def one_block(block_index):
        first_row = block_index * 2
        center_part = tuple(
            (lax.dynamic_slice_in_dim(source, first_row, 2, 0) for source in centers)
        )
        padded_part = tuple(
            (lax.dynamic_slice_in_dim(source, first_row, 4, 0) for source in padded_list)
        )
        return pair_sums(center_part, padded_part, with_force)

    results = lax.map(one_block, jnp.arange(block_count, dtype=jnp.int32))
    return tuple((source.reshape((row_count,) + source.shape[2:]) for source in results))


def global_bounds(density_ratio, live_bool, heavy_bool):
    light_sel = live_bool & jnp.logical_not(heavy_bool)
    heavy_sel = live_bool & heavy_bool
    top_local = jnp.stack(
        [
            jnp.max(jnp.where(light_sel, density_ratio, -SENTINEL)),
            jnp.max(jnp.where(heavy_sel, density_ratio, -SENTINEL)),
        ]
    )
    low_local = jnp.stack(
        [
            jnp.min(jnp.where(light_sel, density_ratio, SENTINEL)),
            jnp.min(jnp.where(heavy_sel, density_ratio, SENTINEL)),
        ]
    )
    bounds = one_axis_at_a_time(jnp.concatenate([top_local, -low_local]), GX_GY)
    top_ratio = bounds[:2]
    low_ratio = -bounds[2:]
    return (top_ratio, low_ratio)


def phase_params(heavy_bool):
    rest_density = jnp.where(heavy_bool, REST_HEAVY, REST_LIGHT).astype(jnp.float32)
    stiffness = jnp.where(heavy_bool, STIFF_HEAVY, STIFF_LIGHT).astype(jnp.float32)
    return (rest_density, stiffness)


def pressure_update(pressure, density_sum, live_bool, heavy_bool, own_live, own_heavy, trim):
    live_mask = live_bool.astype(jnp.float32)
    rest_density, stiffness = phase_params(heavy_bool)
    density = KERNEL_NORM * density_sum
    density_ratio = density / rest_density
    own_ratio = density_ratio[
        trim : density_ratio.shape[0] - trim, trim : density_ratio.shape[1] - trim
    ]
    top_ratio, low_ratio = global_bounds(own_ratio, own_live, own_heavy)
    relaxation = 1.0 / (1.0 + top_ratio - low_ratio)
    particle_relax = jnp.where(heavy_bool, relaxation[1], relaxation[0])
    pressure = live_mask * (pressure + stiffness * particle_relax * (density_ratio - 1.0))
    safe_density = jnp.where(live_bool, density, 1.0)
    press_term = jnp.where(live_bool, pressure / (safe_density * safe_density), 0.0)
    return (pressure, press_term, jnp.concatenate([top_ratio, low_ratio]))


def local(position, velocity, other_accel, phase_ids, counts):
    tile_rows, tile_cols, slot_count = phase_ids.shape
    slot_index = jnp.arange(slot_count, dtype=jnp.int32)
    live_bool = slot_index[None, None, :] < counts[:, :, None]
    heavy_bool = phase_ids == 1
    live_mask = live_bool.astype(jnp.float32)
    particle_mass = jnp.where(heavy_bool, MASS_HEAVY, MASS_LIGHT).astype(jnp.float32)
    slot_codes = jnp.where(live_bool, phase_ids + 1, 0)
    padded_codes = padded(slot_codes, ((GX, 0), (GY, 1)), 2)
    cycle_codes = padded_codes[1:-1, 1:-1]
    cycle_live = cycle_codes > 0
    cycle_heavy = cycle_codes == 2
    cycle_mask = cycle_live.astype(jnp.float32)
    accel_x = jnp.zeros_like(live_mask)
    accel_y = jnp.zeros_like(live_mask)
    monitor_rows = []
    far_mask = (padded_codes > 0).astype(jnp.float32)
    cycle_pressure = jnp.zeros_like(cycle_mask)
    for iteration in range(ITERS):
        vel_x = velocity[0] + TIME_STEP * (other_accel[0] + accel_x)
        vel_y = velocity[1] + TIME_STEP * (other_accel[1] + accel_y)
        pos_x = position[0] + TIME_STEP * vel_x
        pos_y = position[1] + TIME_STEP * vel_y
        moved = padded(jnp.stack([pos_x, pos_y]), ((GX, 1), (GY, 2)), 2)
        cycle_x = moved[0, 1:-1, 1:-1]
        cycle_y = moved[1, 1:-1, 1:-1]
        (density_sum,) = blocked(
            False, (cycle_x, cycle_y), (moved[0], moved[1], far_mask), tile_rows + 2
        )
        cycle_pressure, cycle_term, monitor_row = pressure_update(
            cycle_pressure, density_sum, cycle_live, cycle_heavy, live_bool, heavy_bool, 1
        )
        force_x, force_y = blocked(
            True,
            (pos_x, pos_y, cycle_term[1:-1, 1:-1]),
            (cycle_x, cycle_y, cycle_mask, cycle_term),
            tile_rows,
        )
        accel_x = live_mask * (6.0 * KERNEL_NORM / particle_mass) * force_x
        accel_y = live_mask * (6.0 * KERNEL_NORM / particle_mass) * force_y
        monitor_rows.append(monitor_row)
    pressure = cycle_pressure[1:-1, 1:-1]
    new_vel_x = live_mask * (velocity[0] + TIME_STEP * (other_accel[0] + accel_x))
    new_vel_y = live_mask * (velocity[1] + TIME_STEP * (other_accel[1] + accel_y))
    new_pos_x = live_mask * (position[0] + TIME_STEP * new_vel_x)
    new_pos_y = live_mask * (position[1] + TIME_STEP * new_vel_y)
    return (
        jnp.stack([new_pos_x, new_pos_y]),
        jnp.stack([new_vel_x, new_vel_y]),
        pressure,
        jnp.stack(monitor_rows),
    )


def solution(mesh):
    torus = Mesh(mesh.devices.reshape(4, 2, 2, 4, 2), ("gx_0", "gx_1", "gy_0", "gy_1", "gy_2"))
    in_specs = (
        P(None, GX, GY, None),
        P(None, GX, GY, None),
        P(None, GX, GY, None),
        P(GX, GY, None),
        P(GX, GY),
    )
    out_specs = (P(None, GX, GY, None), P(None, GX, GY, None), P(GX, GY, None), P())
    return jax.shard_map(local, mesh=torus, in_specs=in_specs, out_specs=out_specs, check_vma=False)
```

profile of v0, /device:TPU:103, one launch (start us, length us, event | category | flops | bytes accessed | tf_op | source)
XLA Modules:
  0.0 435.1 jit_solution(13213212542423151397)
XLA Ops:
  6.3 3.3 collective-permute-start.6
  10.9 3.9 collective-permute-start.2
  18.4 27.3 %while.88 = (s32[]{:T(128)}, f32[4,2,8,128]{3,2,1,0:T(8,128)S(1)}, s32[4]{0:T(128)S(1)}, f32[8,8,128]{2,1,0:T(8,128)S(1)}, f32[10,10,128]{2,1,0:T(8,128)S(1)}, /...) while((s32[]{:T(128)}, f32[4,2,8,128]{3,2,1,0:T(8,128)S(1)}, ...), condition=%wide.region_10.11_spmd, body=%wide.region_0.10_spmd.sunk | while | flops 25974796 | bytes 885060 | solution.py:93
  49.9 5.7 %pmax.140 = f32[4]{0:T(128)S(1)} all-reduce(f32[4]{0:T(128)S(1)} %pad_maximum_fusion.31), channel_id=1, replica_groups=mesh['gx_0'=4,'gx_1'=2,'gy_0'=2,'gy_1'=4,'gy_2'=2] {'gx_0'}, use_global_device_ids=true, to_apply=%region_15.16 | all-reduce | flops 4 | bytes 32 | tf_op jit(solution)/shard_map/pmax | solution.py:26
  55.6 3.8 pmax.141
  59.4 5.3 %pmax.142 = f32[4]{0:T(128)S(1)} all-reduce(f32[4]{0:T(128)S(1)} %pmax.141), channel_id=1, replica_groups=mesh['gx_0'=4,'gx_1'=2,'gy_0'=2,'gy_1'=4,'gy_2'=2] {'gy_0'}, use_global_device_ids=true, to_apply=%region_17.18 | all-reduce | flops 4 | bytes 32 | tf_op jit(solution)/shard_map/pmax | solution.py:26
  64.7 12.3 %pmax.143 = f32[4]{0:T(128)S(1)} all-reduce(f32[4]{0:T(128)S(1)} %pmax.142), channel_id=1, replica_groups=mesh['gx_0'=4,'gx_1'=2,'gy_0'=2,'gy_1'=4,'gy_2'=2] {'gy_1'}, use_global_device_ids=true, to_apply=%region_18.19 | all-reduce | flops 4 | bytes 32 | tf_op jit(solution)/shard_map/pmax | solution.py:26
  77.0 5.0 %pmax.144 = f32[4]{0:T(128)S(1)} all-reduce(f32[4]{0:T(128)S(1)} %pmax.143), channel_id=1, replica_groups=mesh['gx_0'=4,'gx_1'=2,'gy_0'=2,'gy_1'=4,'gy_2'=2] {'gy_2'}, use_global_device_ids=true, to_apply=%region_19.20 | all-reduce | flops 4 | bytes 32 | tf_op jit(solution)/shard_map/pmax | solution.py:26
  84.1 26.8 %while.89 = (s32[]{:T(128)}, f32[3,2,6,128]{3,2,1,0:T(8,128)S(1)}, f32[3,2,6,128]{3,2,1,0:T(8,128)S(1)}, s32[3]{0:T(128)S(1)}, f32[6,6,128]{2,1,0:T(8,128)S(1)},...) while((s32[]{:T(128)}, f32[3,2,6,128]{3,2,1,0:T(8,128)S(1)}, ...), condition=%wide.region_39.40_spmd, body=%wide.region_20.39_spmd.sunk | while | flops 26557452 | bytes 1030516 | solution.py:93
  86.7 3.1 fusion.501
  95.7 3.1 fusion.501
  104.6 3.1 fusion.501
  114.7 3.8 collective-permute-done.9
  118.6 3.5 collective-permute-start.10
  125.6 27.3 %while.90 = (s32[]{:T(128)}, f32[4,2,8,128]{3,2,1,0:T(8,128)S(1)}, s32[4]{0:T(128)S(1)}, f32[8,8,128]{2,1,0:T(8,128)S(1)}, f32[10,10,128]{2,1,0:T(8,128)S(1)}, /...) while((s32[]{:T(128)}, f32[4,2,8,128]{3,2,1,0:T(8,128)S(1)}, ...), condition=%wide.region_50.51_spmd, body=%wide.region_40.50_spmd.sunk | while | flops 25974796 | bytes 885060 | solution.py:93
  156.4 5.7 %pmax.145 = f32[4]{0:T(128)S(1)} all-reduce(f32[4]{0:T(128)S(1)} %pad_maximum_fusion.32), channel_id=1, replica_groups=mesh['gx_0'=4,'gx_1'=2,'gy_0'=2,'gy_1'=4,'gy_2'=2] {'gx_0'}, use_global_device_ids=true, to_apply=%region_55.56 | all-reduce | flops 4 | bytes 32 | tf_op jit(solution)/shard_map/pmax | solution.py:26
  162.1 3.8 pmax.146
  165.9 5.3 %pmax.147 = f32[4]{0:T(128)S(1)} all-reduce(f32[4]{0:T(128)S(1)} %pmax.146), channel_id=1, replica_groups=mesh['gx_0'=4,'gx_1'=2,'gy_0'=2,'gy_1'=4,'gy_2'=2] {'gy_0'}, use_global_device_ids=true, to_apply=%region_57.58 | all-reduce | flops 4 | bytes 32 | tf_op jit(solution)/shard_map/pmax | solution.py:26
  171.1 10.4 %pmax.148 = f32[4]{0:T(128)S(1)} all-reduce(f32[4]{0:T(128)S(1)} %pmax.147), channel_id=1, replica_groups=mesh['gx_0'=4,'gx_1'=2,'gy_0'=2,'gy_1'=4,'gy_2'=2] {'gy_1'}, use_global_device_ids=true, to_apply=%region_58.59 | all-reduce | flops 4 | bytes 32 | tf_op jit(solution)/shard_map/pmax | solution.py:26
  181.6 5.1 %pmax.149 = f32[4]{0:T(128)S(1)} all-reduce(f32[4]{0:T(128)S(1)} %pmax.148), channel_id=1, replica_groups=mesh['gx_0'=4,'gx_1'=2,'gy_0'=2,'gy_1'=4,'gy_2'=2] {'gy_2'}, use_global_device_ids=true, to_apply=%region_59.60 | all-reduce | flops 4 | bytes 32 | tf_op jit(solution)/shard_map/pmax | solution.py:26
  190.1 26.5 %while.91 = (s32[]{:T(128)}, f32[3,2,6,128]{3,2,1,0:T(8,128)S(1)}, f32[3,2,6,128]{3,2,1,0:T(8,128)S(1)}, s32[3]{0:T(128)S(1)}, f32[6,6,128]{2,1,0:T(8,128)S(1)},...) while((s32[]{:T(128)}, f32[3,2,6,128]{3,2,1,0:T(8,128)S(1)}, ...), condition=%wide.region_79.80_spmd, body=%wide.region_60.79_spmd.sunk | while | flops 26557452 | bytes 1030516 | solution.py:93
  192.7 3.1 fusion.508
  201.5 3.1 fusion.508
  210.4 3.1 fusion.508
  220.3 3.8 collective-permute-done.13
  224.2 3.5 collective-permute-start.14
  231.3 26.9 %while.92 = (s32[]{:T(128)}, f32[4,2,8,128]{3,2,1,0:T(8,128)S(1)}, s32[4]{0:T(128)S(1)}, f32[8,8,128]{2,1,0:T(8,128)S(1)}, f32[10,10,128]{2,1,0:T(8,128)S(1)}, /...) while((s32[]{:T(128)}, f32[4,2,8,128]{3,2,1,0:T(8,128)S(1)}, ...), condition=%wide.region_90.91_spmd, body=%wide.region_80.90_spmd.sunk | while | flops 25974796 | bytes 885060 | solution.py:93
  261.6 5.7 %pmax.150 = f32[4]{0:T(128)S(1)} all-reduce(f32[4]{0:T(128)S(1)} %pad_maximum_fusion.33), channel_id=1, replica_groups=mesh['gx_0'=4,'gx_1'=2,'gy_0'=2,'gy_1'=4,'gy_2'=2] {'gx_0'}, use_global_device_ids=true, to_apply=%region_95.96 | all-reduce | flops 4 | bytes 32 | tf_op jit(solution)/shard_map/pmax | solution.py:26
  267.3 3.8 pmax.151
  271.0 5.3 %pmax.152 = f32[4]{0:T(128)S(1)} all-reduce(f32[4]{0:T(128)S(1)} %pmax.151), channel_id=1, replica_groups=mesh['gx_0'=4,'gx_1'=2,'gy_0'=2,'gy_1'=4,'gy_2'=2] {'gy_0'}, use_global_device_ids=true, to_apply=%region_97.98 | all-reduce | flops 4 | bytes 32 | tf_op jit(solution)/shard_map/pmax | solution.py:26
  276.3 10.4 %pmax.153 = f32[4]{0:T(128)S(1)} all-reduce(f32[4]{0:T(128)S(1)} %pmax.152), channel_id=1, replica_groups=mesh['gx_0'=4,'gx_1'=2,'gy_0'=2,'gy_1'=4,'gy_2'=2] {'gy_1'}, use_global_device_ids=true, to_apply=%region_98.99 | all-reduce | flops 4 | bytes 32 | tf_op jit(solution)/shard_map/pmax | solution.py:26
  286.7 5.4 %pmax.154 = f32[4]{0:T(128)S(1)} all-reduce(f32[4]{0:T(128)S(1)} %pmax.153), channel_id=1, replica_groups=mesh['gx_0'=4,'gx_1'=2,'gy_0'=2,'gy_1'=4,'gy_2'=2] {'gy_2'}, use_global_device_ids=true, to_apply=%region_99.100 | all-reduce | flops 4 | bytes 32 | tf_op jit(solution)/shard_map/pmax | solution.py:26
  292.8 3.9 fusion.388
  296.7 27.0 %while.93 = (s32[]{:T(128)}, f32[3,2,6,128]{3,2,1,0:T(8,128)S(1)}, f32[3,2,6,128]{3,2,1,0:T(8,128)S(1)}, s32[3]{0:T(128)S(1)}, f32[6,6,128]{2,1,0:T(8,128)S(1)},...) while((s32[]{:T(128)}, f32[3,2,6,128]{3,2,1,0:T(8,128)S(1)}, ...), condition=%wide.region_119.120_spmd, body=%wide.region_100.119_spmd.sunk | while | flops 26557452 | bytes 1030516 | solution.py:93
  299.4 3.1 fusion.515
  308.4 3.1 fusion.515
  317.4 3.1 fusion.515
  327.3 3.8 collective-permute-done.17
  331.2 3.5 collective-permute-start.18
  338.3 27.5 %while.94 = (s32[]{:T(128)}, f32[4,2,8,128]{3,2,1,0:T(8,128)S(1)}, s32[4]{0:T(128)S(1)}, f32[8,8,128]{2,1,0:T(8,128)S(1)}, f32[10,10,128]{2,1,0:T(8,128)S(1)}, /...) while((s32[]{:T(128)}, f32[4,2,8,128]{3,2,1,0:T(8,128)S(1)}, ...), condition=%wide.region_130.131_spmd, body=%wide.region_120.130_spmd.sunk | while | flops 25974796 | bytes 885060 | solution.py:93
  369.1 5.7 %pmax.155 = f32[4]{0:T(128)S(1)} all-reduce(f32[4]{0:T(128)S(1)} %pad_maximum_fusion.34), channel_id=1, replica_groups=mesh['gx_0'=4,'gx_1'=2,'gy_0'=2,'gy_1'=4,'gy_2'=2] {'gx_0'}, use_global_device_ids=true, to_apply=%region_135.136 | all-reduce | flops 4 | bytes 32 | tf_op jit(solution)/shard_map/pmax | solution.py:26
  374.9 3.8 pmax.156
  378.7 5.3 %pmax.157 = f32[4]{0:T(128)S(1)} all-reduce(f32[4]{0:T(128)S(1)} %pmax.156), channel_id=1, replica_groups=mesh['gx_0'=4,'gx_1'=2,'gy_0'=2,'gy_1'=4,'gy_2'=2] {'gy_0'}, use_global_device_ids=true, to_apply=%region_137.138 | all-reduce | flops 4 | bytes 32 | tf_op jit(solution)/shard_map/pmax | solution.py:26
  384.0 10.4 %pmax.158 = f32[4]{0:T(128)S(1)} all-reduce(f32[4]{0:T(128)S(1)} %pmax.157), channel_id=1, replica_groups=mesh['gx_0'=4,'gx_1'=2,'gy_0'=2,'gy_1'=4,'gy_2'=2] {'gy_1'}, use_global_device_ids=true, to_apply=%region_138.139 | all-reduce | flops 4 | bytes 32 | tf_op jit(solution)/shard_map/pmax | solution.py:26
  394.5 5.2 %pmax.159 = f32[4]{0:T(128)S(1)} all-reduce(f32[4]{0:T(128)S(1)} %pmax.158), channel_id=1, replica_groups=mesh['gx_0'=4,'gx_1'=2,'gy_0'=2,'gy_1'=4,'gy_2'=2] {'gy_2'}, use_global_device_ids=true, to_apply=%region_139.140 | all-reduce | flops 4 | bytes 32 | tf_op jit(solution)/shard_map/pmax | solution.py:26
  400.4 5.1 %fusion.385 = (f32[8,8,128]{2,1,0:T(8,128)S(1)}, f32[8,8,128]{2,1,0:T(8,128)S(1)}) fusion(pred[8,8,128]{2,1,0:T(8,128)(4,1)S(1)} %get-tuple-element.763, f32[4,2,8,128]{3,2,1,0:T(8,128)S(1)} %broadcast_multiply_fusion, pred[8,8,128]{2,1,0:T(8,128)(4,1)S(1)} %get-tuple-element.768, f32[]{:T(128)} %bitcast.81, f32[]{:T(128)} %bitcast.80, ...), kind=kLoop, calls=%fused_computation.882 | loop fusion | flops 270336 | bytes 213024 | tf_op jit(solution)/shard_map/jit(_where)/select_n | solution.py:137
  405.6 26.8 %while.95 = (s32[]{:T(128)}, f32[3,2,6,128]{3,2,1,0:T(8,128)S(1)}, f32[3,2,6,128]{3,2,1,0:T(8,128)S(1)}, s32[3]{0:T(128)S(1)}, f32[6,6,128]{2,1,0:T(8,128)S(1)},...) while((s32[]{:T(128)}, f32[3,2,6,128]{3,2,1,0:T(8,128)S(1)}, ...), condition=%wide.region_159.160_spmd, body=%wide.region_140.159_spmd.sunk | while | flops 26557452 | bytes 1030516 | solution.py:93
  411.3 3.1 fusion.521
  (363 shorter events, 221.4 us)
Async XLA Ops:
  0.6 2.4 copy-start.2
  1.5 4.7 %collective-permute-start.4 = (s32[2,6,128]{2,1,0:T(8,128)S(1)}, s32[2,6,128]{2,1,0:T(8,128)S(1)}, u32[]{:S(2)}, u32[]{:S(2)}) collective-permute-start(s32[2,6,128]{2,1,0:T(8,128)S(1)} %get-tuple-element.1149), channel_id=1, source_target_pairs={{0,16},{16,32},{32,48},{48,64},{64,80},{80,96},{96,112},{112,0},{1... | collective-permute-start | bytes 18440 | tf_op jit(solution)/shard_map/ppermute | solution.py:36
  1.6 1.5 copy-start.3
  1.6 4.7 %collective-permute-start.5 = (s32[2,6,128]{2,1,0:T(8,128)S(1)}, s32[2,6,128]{2,1,0:T(8,128)S(1)}, u32[]{:S(2)}, u32[]{:S(2)}) collective-permute-start(s32[2,6,128]{2,1,0:T(8,128)S(1)} %get-tuple-element.1150), channel_id=1, source_target_pairs={{16,0},{32,16},{48,32},{64,48},{80,64},{96,80},{112,96},{0,112},{1... | collective-permute-start | bytes 18440 | tf_op jit(solution)/shard_map/ppermute | solution.py:39
  3.1 0.8 copy-start.4
  3.9 5.7 %collective-permute-start = (f32[2,2,6,128]{3,2,1,0:T(8,128)S(1)}, f32[2,2,6,128]{3,2,1,0:T(8,128)S(1)}, u32[]{:S(2)}, u32[]{:S(2)}) collective-permute-start(f32[2,2,6,128]{3,2,1,0:T(8,128)S(1)} %get-tuple-element.1139), channel_id=1, source_target_pairs={{0,16},{16,32},{32,48},{48,64},{64,80},{80,96},{96,112},{112,0},{1... | collective-permute-start | bytes 36872 | tf_op jit(solution)/shard_map/ppermute | solution.py:36
  6.2 4.7 %collective-permute-start.1 = (f32[2,2,6,128]{3,2,1,0:T(8,128)S(1)}, f32[2,2,6,128]{3,2,1,0:T(8,128)S(1)}, u32[]{:S(2)}, u32[]{:S(2)}) collective-permute-start(f32[2,2,6,128]{3,2,1,0:T(8,128)S(1)} %get-tuple-element.1140), channel_id=1, source_target_pairs={{16,0},{32,16},{48,32},{64,48},{80,64},{96,80},{112,96},{0,112},{1... | collective-permute-start | bytes 36872 | tf_op jit(solution)/shard_map/ppermute | solution.py:39
  6.3 8.5 %collective-permute-start.6 = (s32[10,2,128]{2,1,0:T(2,128)S(1)}, s32[10,2,128]{2,1,0:T(2,128)S(1)}, u32[]{:S(2)}, u32[]{:S(2)}) collective-permute-start(s32[10,2,128]{2,1,0:T(2,128)S(1)} %get-tuple-element.1141), channel_id=1, source_target_pairs={{0,1},{1,2},{2,3},{3,4},{4,5},{5,6},{6,7},{7,8},{8,9},{9,10},{10,1... | collective-permute-start | bytes 30728 | tf_op jit(solution)/shard_map/ppermute | solution.py:36
  9.6 5.2 %collective-permute-start.7 = (s32[10,2,128]{2,1,0:T(2,128)S(1)}, s32[10,2,128]{2,1,0:T(2,128)S(1)}, u32[]{:S(2)}, u32[]{:S(2)}) collective-permute-start(s32[10,2,128]{2,1,0:T(2,128)S(1)} %get-tuple-element.1142), channel_id=1, source_target_pairs={{1,0},{2,1},{3,2},{4,3},{5,4},{6,5},{7,6},{8,7},{9,8},{10,9},{11,1... | collective-permute-start | bytes 30728 | tf_op jit(solution)/shard_map/ppermute | solution.py:39
  10.9 4.8 %collective-permute-start.2 = (f32[2,10,2,128]{3,2,1,0:T(2,128)S(1)}, f32[2,10,2,128]{3,2,1,0:T(2,128)S(1)}, u32[]{:S(2)}, u32[]{:S(2)}) collective-permute-start(f32[2,10,2,128]{3,2,1,0:T(2,128)S(1)} %get-tuple-element.1131), channel_id=1, source_target_pairs={{0,1},{1,2},{2,3},{3,4},{4,5},{5,6},{6,7},{7,8},{8,9},{9,10},{10,1... | collective-permute-start | bytes 61448 | tf_op jit(solution)/shard_map/ppermute | solution.py:36
  14.7 3.5 collective-permute-start.3
  45.7 0.7 copy-start
  45.7 0.7 copy-start.1
  111.0 3.7 collective-permute-start.8
  113.8 4.7 %collective-permute-start.9 = (f32[2,2,6,128]{3,2,1,0:T(8,128)S(1)}, f32[2,2,6,128]{3,2,1,0:T(8,128)S(1)}, u32[]{:S(2)}, u32[]{:S(2)}) collective-permute-start(f32[2,2,6,128]{3,2,1,0:T(8,128)S(1)} %get-tuple-element.1138), channel_id=1, source_target_pairs={{16,0},{32,16},{48,32},{64,48},{80,64},{96,80},{112,96},{0,112},{1... | collective-permute-start | bytes 36872 | tf_op jit(solution)/shard_map/ppermute | solution.py:39
  118.6 4.4 %collective-permute-start.10 = (f32[2,10,2,128]{3,2,1,0:T(2,128)S(1)}, f32[2,10,2,128]{3,2,1,0:T(2,128)S(1)}, u32[]{:S(2)}, u32[]{:S(2)}) collective-permute-start(f32[2,10,2,128]{3,2,1,0:T(2,128)S(1)} %get-tuple-element.1129), channel_id=1, source_target_pairs={{0,1},{1,2},{2,3},{3,4},{4,5},{5,6},{6,7},{7,8},{8,9},{9,10},{10,1... | collective-permute-start | bytes 61448 | tf_op jit(solution)/shard_map/ppermute | solution.py:36
  122.0 3.5 collective-permute-start.11
  216.8 3.6 collective-permute-start.12
  219.5 4.7 %collective-permute-start.13 = (f32[2,2,6,128]{3,2,1,0:T(8,128)S(1)}, f32[2,2,6,128]{3,2,1,0:T(8,128)S(1)}, u32[]{:S(2)}, u32[]{:S(2)}) collective-permute-start(f32[2,2,6,128]{3,2,1,0:T(8,128)S(1)} %get-tuple-element.1136), channel_id=1, source_target_pairs={{16,0},{32,16},{48,32},{64,48},{80,64},{96,80},{112,96},{0,112},{1... | collective-permute-start | bytes 36872 | tf_op jit(solution)/shard_map/ppermute | solution.py:39
  224.2 4.4 %collective-permute-start.14 = (f32[2,10,2,128]{3,2,1,0:T(2,128)S(1)}, f32[2,10,2,128]{3,2,1,0:T(2,128)S(1)}, u32[]{:S(2)}, u32[]{:S(2)}) collective-permute-start(f32[2,10,2,128]{3,2,1,0:T(2,128)S(1)} %get-tuple-element.1127), channel_id=1, source_target_pairs={{0,1},{1,2},{2,3},{3,4},{4,5},{5,6},{6,7},{7,8},{8,9},{9,10},{10,1... | collective-permute-start | bytes 61448 | tf_op jit(solution)/shard_map/ppermute | solution.py:36
  227.6 3.5 collective-permute-start.15
  323.8 3.6 collective-permute-start.16
  326.5 4.7 %collective-permute-start.17 = (f32[2,2,6,128]{3,2,1,0:T(8,128)S(1)}, f32[2,2,6,128]{3,2,1,0:T(8,128)S(1)}, u32[]{:S(2)}, u32[]{:S(2)}) collective-permute-start(f32[2,2,6,128]{3,2,1,0:T(8,128)S(1)} %get-tuple-element.1134), channel_id=1, source_target_pairs={{16,0},{32,16},{48,32},{64,48},{80,64},{96,80},{112,96},{0,112},{1... | collective-permute-start | bytes 36872 | tf_op jit(solution)/shard_map/ppermute | solution.py:39
  331.2 4.4 %collective-permute-start.18 = (f32[2,10,2,128]{3,2,1,0:T(2,128)S(1)}, f32[2,10,2,128]{3,2,1,0:T(2,128)S(1)}, u32[]{:S(2)}, u32[]{:S(2)}) collective-permute-start(f32[2,10,2,128]{3,2,1,0:T(2,128)S(1)} %get-tuple-element.1125), channel_id=1, source_target_pairs={{0,1},{1,2},{2,3},{3,4},{4,5},{5,6},{6,7},{7,8},{8,9},{9,10},{10,1... | collective-permute-start | bytes 61448 | tf_op jit(solution)/shard_map/ppermute | solution.py:36
  334.6 3.5 collective-permute-start.19
where the time goes:
time: 440 us; the launch traced here: 435 us
  other arithmetic  208 us (47%)
  blocking collectives  123 us (28%)
  starting transfers between devices  29.6 us (7%)
  waiting for transfers between devices  29.4 us (7%)
  local copies, waits for them, and re-layouts  24 us (5%)
  loops' own time  19.9 us (5%)
    pmax x20, blocking collectives, one_axis_at_a_time(): value = lax.pmax(value, axis)  123 us
    reduce_sum x36, other arithmetic, pair_sums(): total_b = total_b + jnp.sum(pair_coef * diff_y, axis=-1)  89.8 us
    reduce_sum x32, other arithmetic, pair_sums(): jnp.sum(intersection * intersection * intersection, axis=-1)  86.5 us
    ppermute x10, starting transfers between devices, padded(): lax.ppermute(lax.slice_in_dim(block, block.shape[dim] - width, None, axis...  28.1 us
    ppermute x10, waiting for transfers between devices, padded(): lax.ppermute(lax.slice_in_dim(block, 0, width, axis=dim), axis, backward)  23.2 us
    another operation x8, loops' own time, blocked(): results = lax.map(one_block, jnp.arange(block_count, dtype=jnp.int32))  19.9 us
    dynamic_slice x28, local copies, waits for them, and re-layouts, blocked(): results = lax.map(one_block, jnp.arange(block_count, dtype=jnp.int32))  16.9 us
    select_n x4, other arithmetic, pressure_update(): jnp.where(live_bool, pressure / (safe_density * safe_density), 0.0)  13 us
  transfers between devices with their start and end apart: 20, of which 16 were waited for; matrix products, arithmetic and copies ran while one was open for 0% of the time, Pallas kernels for 0%

commit v1 on v0

v1 whole, which is shorter than its diff:
```python
import jax
import jax.numpy as jnp
import numpy as np
from jax import lax
from jax.experimental import pallas as pl
from jax.experimental.pallas import tpu as pltpu
from jax.sharding import Mesh
from jax.sharding import PartitionSpec as P

ITERS = 4
GX = ("gx_0", "gx_1")
GY = ("gy_0", "gy_1", "gy_2")

F32, BF16 = jnp.float32, jnp.bfloat16
OFFS = tuple((ox, oy) for ox in (-1, 0, 1) for oy in (-1, 0, 1))


def offset_masks():
    out = np.ones((9, 32, 128), np.float32)
    for k, (ox, oy) in enumerate(OFFS):
        for row in (6, 7, 12, 13, 14, 15, 18, 19, 20, 21, 22, 23):
            out[k, row] = (ox, oy)[row % 2]
        out[k, 31] = ox * ox + oy * oy
    return out


def rnd(v):
    return v.astype(BF16).astype(F32)


def row_iota():
    return lax.broadcasted_iota(jnp.int32, (8, 128), 0)


def cell_slabs(pos_ref, r, c, want_l=True, want_r=True):
    row = row_iota()
    x = jnp.broadcast_to(pos_ref[r, c, 0:1, :], (8, 128))
    y = jnp.broadcast_to(pos_ref[r, c, 1:2, :], (8, 128))
    v = jnp.where((row & 1) == 1, y, x)
    v1 = rnd(v)
    rest = v - v1
    v2 = rnd(rest)
    v3 = rest - v2
    n = x * x + y * y
    n1 = rnd(n)
    nrest = n - n1
    n2 = rnd(nrest)
    n3 = nrest - n2
    left = right = None
    if want_l:
        la = v1
        lb = jnp.where((row == 4) | (row == 5), 1.0, v2)
        lc = jnp.where((row >= 2) & (row <= 5), 1.0, v3)
        ld = jnp.where(row == 0, n1, jnp.where(row == 1, n2, jnp.where(row == 2, n3, 1.0)))
        left = jnp.concatenate([la, lb, lc, ld], axis=0)
    if want_r:
        t1, t2, t3 = 2.0 * v1, 2.0 * v2, 2.0 * v3
        ra = jnp.where(row < 2, t1, jnp.where(row < 4, t2, jnp.where(row < 6, t3, -2.0)))
        rb = ra
        rc = jnp.where(row < 4, t1, jnp.where(row < 6, t2, -2.0))
        rd = jnp.where(row < 3, -1.0, jnp.where(row == 3, -n1, jnp.where(row == 4, -n2, jnp.where(row == 5, -n3, jnp.where(row == 6, 1.0, -1.0)))))
        right = jnp.concatenate([ra, rb, rc, rd], axis=0)
    return left, right


def pair_rhs(r1, r2, mask):
    zero = jnp.zeros((32, 128), BF16)
    return jnp.concatenate(
        [jnp.concatenate([r1 * mask, zero], axis=1), jnp.concatenate([zero, r2 * mask], axis=1)], axis=0)


def pair_s(left_t, rhs):
    return jnp.dot(left_t, rhs, preferred_element_type=F32)


def fill_slabs(pos_ref, ls, rs, lo, hi, rlo, rhi):
    def body(r, carry):
        for c in range(lo, hi):
            left, right = cell_slabs(pos_ref, r, c)
            ls[r, c] = left
            if rlo <= c < rhi:
                rs[r, c] = right.astype(BF16)
        return carry
    lax.fori_loop(lo, hi, body, 0)


def fill_pairs(ls, lt, start, rows, cols, dr, dc, rbase, cbase):
    def body(i, carry):
        for j in range(cols):
            both = jnp.concatenate([ls[rbase + i, cbase + j], ls[rbase + i + dr, cbase + j + dc]], axis=0)
            lt[start + i * cols + j] = both.T.astype(BF16)
        return carry
    lax.fori_loop(0, rows, body, 0)


def density_pair(rs, lt, masks_ref, i1, i2, first, stride):
    r1, r2 = rs[i1[0], i1[1]], rs[i2[0], i2[1]]
    acc = jnp.zeros((8, 256), F32)
    for k, (ox, oy) in enumerate(OFFS):
        s = pair_s(lt[first + ox * stride + oy], pair_rhs(r1, r2, masks_ref[k]))
        w = jnp.maximum(s, 0.0)
        w3 = w * w * w
        acc = acc + w3.reshape(16, 8, 256).sum(axis=0)
    return acc.sum(axis=0, keepdims=True)

TIME_STEP = 0.05
KERNEL_NORM = 4.0 / (3.141592653589793 * 64.0)
SENTINEL = 1.0e30


def density_own(pos_ref, masks_ref, ls, rs, lt, store):
    fill_slabs(pos_ref, ls, rs, 1, 9, 2, 8)
    fill_pairs(ls, lt, 0, 5, 8, 3, 0, 1, 1)
    def body(b, carry):
        for a in range(3):
            row = density_pair(rs, lt, masks_ref, (a + 2, b + 2), (a + 5, b + 2), (a + 1) * 8 + b + 1, 8)
            store(a, b, row[:, :128])
            store(a + 3, b, row[:, 128:])
        return carry
    lax.fori_loop(0, 6, body, 0)


def kd_kernel(pos_ref, code_ref, masks_ref, dens_ref, bnd_ref, ls, rs, lt):
    def store(a, b, row):
        dens_ref[a, pl.ds(b, 1), :] = row
    density_own(pos_ref, masks_ref, ls, rs, lt, store)
    code = code_ref[...]
    ratio = dens_ref[...] * jnp.where(code == 2.0, KERNEL_NORM / 1.5, KERNEL_NORM / 1.2)
    picks = []
    for phase in (1.0, 2.0):
        picks.append(jnp.where(code == phase, ratio, -SENTINEL))
    for phase in (1.0, 2.0):
        picks.append(jnp.where(code == phase, -ratio, -SENTINEL))
    lane = lax.broadcasted_iota(jnp.int32, (1, 128), 1)
    out = jnp.zeros((1, 128), F32)
    for k, pick in enumerate(picks):
        top = pick.max(axis=0).max(axis=0, keepdims=True).max(axis=1, keepdims=True)
        out = jnp.where(lane == k, top, out)
    bnd_ref[...] = jnp.broadcast_to(out, (128, 128))


def term_rows(t_ref, r, c):
    row = row_iota() & 3
    a, b0, b1 = (jnp.broadcast_to(t_ref[k, r, pl.ds(c, 1), :], (8, 128)) for k in range(3))
    return jnp.where(row == 0, 1.0, jnp.where(row == 1, a, jnp.where(row == 2, b0, b1)))


def hi_lo(v):
    hi = rnd(v)
    return jnp.where(row_iota() < 4, hi, v - hi)


def cell_moments(pos_ref, t_ref, r, c):
    t = term_rows(t_ref, r, c)
    x = jnp.broadcast_to(pos_ref[r + 1, c + 1, 0:1, :], (8, 128))
    y = jnp.broadcast_to(pos_ref[r + 1, c + 1, 1:2, :], (8, 128))
    groups = [hi_lo(t)]
    for q in (x, y):
        for o in (-1.0, 0.0, 1.0):
            groups.append(hi_lo(t * (q + o)))
    return groups


def kf_kernel(pos_ref, dens_ref, code_ref, p_ref, masks_ref, s_ref, q_ref, ls, rs, lt, dn, tt, gt):
    fill_slabs(pos_ref, ls, rs, 0, 10, 1, 9)
    fill_pairs(ls, lt, 0, 5, 8, 3, 0, 1, 1)
    fill_pairs(ls, lt, 40, 3, 10, 7, 0, 0, 0)
    fill_pairs(ls, lt, 70, 8, 3, 0, 7, 1, 0)
    def top_bottom(h, carry):
        for u in range(2):
            c = h * 2 + u
            row = density_pair(rs, lt, masks_ref, (1, c + 1), (8, c + 1), 50 + c + 1, 10)
            dn[0, pl.ds(c, 1), :] = row[:, :128]
            dn[7, pl.ds(c, 1), :] = row[:, 128:]
        return carry
    lax.fori_loop(0, 4, top_bottom, 0)
    def left_right(h, carry):
        for u in range(2):
            a = h * 2 + u + 1
            row = density_pair(rs, lt, masks_ref, (a + 1, 1), (a + 1, 8), 70 + a * 3 + 1, 3)
            dn[a, pl.ds(0, 1), :] = row[:, :128]
            dn[a, pl.ds(7, 1), :] = row[:, 128:]
        return carry
    lax.fori_loop(0, 3, left_right, 0)
    for a in range(6):
        dn[a + 1, pl.ds(1, 6), :] = dens_ref[a]
    code = code_ref[...]
    live = code > 0.0
    heavy = code == 2.0
    density = KERNEL_NORM * dn[...]
    ratio = density * jnp.where(heavy, 1.0 / 1.5, 1.0 / 1.2)
    q = jnp.where(live, jnp.where(heavy, 200.0, 100.0) * (ratio - 1.0), 0.0)
    q_ref[...] = q
    safe = jnp.where(live, density, 1.0)
    inv = jnp.where(live, 1.0 / (safe * safe), 0.0)
    b = q * inv
    tt[0] = p_ref[...] * inv
    tt[1] = jnp.where(heavy, 0.0, b)
    tt[2] = jnp.where(heavy, b, 0.0)
    def moments(i, carry):
        for j in range(8):
            one = cell_moments(pos_ref, tt, i, j)
            two = cell_moments(pos_ref, tt, i + 3, j)
            tiles = [jnp.concatenate([g, h], axis=0) for g, h in zip(one, two)]
            gt[i * 8 + j] = jnp.concatenate(tiles, axis=0).astype(BF16)
        return carry
    lax.fori_loop(0, 5, moments, 0)
    row = row_iota()
    def forces(bcol, carry):
        for a in range(3):
            r1, r2 = rs[a + 2, bcol + 2], rs[a + 5, bcol + 2]
            acc = jnp.zeros((48, 256), F32)
            for k, (ox, oy) in enumerate(OFFS):
                p = (a + 1 + ox) * 8 + bcol + 1 + oy
                s = pair_s(lt[p], pair_rhs(r1, r2, masks_ref[k]))
                w = jnp.maximum(s, 0.0)
                w2 = w * w
                hi = w2.astype(BF16)
                lo = (w2 - hi.astype(F32)).astype(BF16)
                g = jnp.concatenate([gt[p, 0:16], gt[p, 32 + 16 * ox:48 + 16 * ox], gt[p, 80 + 16 * oy:96 + 16 * oy]], axis=0)
                acc = acc + jnp.dot(jnp.concatenate([g, g], axis=1), jnp.concatenate([hi, lo], axis=0), preferred_element_type=F32)
            for h in range(2):
                aa = a + 3 * h
                lanes = slice(128 * h, 128 * h + 128)
                sums = []
                for t in range(3):
                    m = acc[16 * t + 8 * h:16 * t + 8 * h + 8, lanes]
                    sums.append(m + jnp.concatenate([m[4:8], m[0:4]], axis=0))
                x = jnp.broadcast_to(pos_ref[aa + 2, bcol + 2, 0:1, :], (8, 128))
                y = jnp.broadcast_to(pos_ref[aa + 2, bcol + 2, 1:2, :], (8, 128))
                ex = x * sums[0] - sums[1]
                ey = y * sums[0] - sums[2]
                e = jnp.where(row < 4, ex, ey)
                e0 = jnp.where(row < 4, jnp.broadcast_to(ex[0:1], (8, 128)), jnp.broadcast_to(ey[0:1], (8, 128)))
                code_row = jnp.broadcast_to(code_ref[aa + 1, pl.ds(bcol + 1, 1), :], (8, 128))
                scale = 6.0 * KERNEL_NORM * TIME_STEP * TIME_STEP
                coef = jnp.where(code_row == 2.0, scale / 1.5, jnp.where(code_row == 1.0, scale, 0.0))
                s_ref[aa, bcol] = coef * (term_rows(tt, aa + 1, bcol + 1) * e0 + e)
        return carry
    lax.fori_loop(0, 6, forces, 0)


VM = pl.BlockSpec(memory_space=pltpu.VMEM)
LIMIT = 40 * 1024 * 1024


def call_kd(pos, code, masks, **kw):
    return pl.pallas_call(
        kd_kernel,
        out_shape=(jax.ShapeDtypeStruct((6, 6, 128), F32), jax.ShapeDtypeStruct((128, 128), F32)),
        in_specs=[VM] * 3, out_specs=(VM, VM),
        scratch_shapes=[pltpu.VMEM((10, 10, 32, 128), F32), pltpu.VMEM((10, 10, 32, 128), BF16), pltpu.VMEM((40, 128, 64), BF16)],
        compiler_params=pltpu.CompilerParams(vmem_limit_bytes=LIMIT),
        cost_estimate=pl.CostEstimate(flops=4_000_000_0, bytes_accessed=200_000, transcendentals=0),
        name="density", **kw)(pos, code, masks)


def call_kf(pos, dens, code8, p8, masks, **kw):
    return pl.pallas_call(
        kf_kernel,
        out_shape=(jax.ShapeDtypeStruct((6, 6, 8, 128), F32), jax.ShapeDtypeStruct((8, 8, 128), F32)),
        in_specs=[VM] * 5, out_specs=(VM, VM),
        scratch_shapes=[pltpu.VMEM((10, 10, 32, 128), F32), pltpu.VMEM((10, 10, 32, 128), BF16), pltpu.VMEM((94, 128, 64), BF16),
                        pltpu.VMEM((8, 8, 128), F32), pltpu.VMEM((3, 8, 8, 128), F32), pltpu.VMEM((40, 112, 128), BF16)],
        compiler_params=pltpu.CompilerParams(vmem_limit_bytes=LIMIT),
        cost_estimate=pl.CostEstimate(flops=8_000_000_00, bytes_accessed=400_000, transcendentals=0),
        name="force", **kw)(pos, dens, code8, p8, masks)


FAR = 2.0 ** 20


def padded(block, sides, width):
    for axis, dim in sides:
        count = lax.axis_size(axis)
        forward = [(i, (i + 1) % count) for i in range(count)]
        backward = [(target, source) for source, target in forward]
        low = lax.ppermute(lax.slice_in_dim(block, block.shape[dim] - width, None, axis=dim), axis, forward)
        high = lax.ppermute(lax.slice_in_dim(block, 0, width, axis=dim), axis, backward)
        block = jnp.concatenate([low, block, high], axis=dim)
    return block


def local(position, velocity, other_accel, phase_ids, counts):
    slot_index = jnp.arange(128, dtype=jnp.int32)
    live = slot_index[None, None, :] < counts[:, :, None]
    code = jnp.where(live, phase_ids + 1, 0).astype(F32)
    masks = jnp.asarray(offset_masks(), BF16)
    rest = position - 0.5 + TIME_STEP * (velocity + TIME_STEP * other_accel)
    base = jnp.stack([jnp.where(live, rest[0], FAR), jnp.where(live, rest[1], 0.0)], axis=2)
    first = padded(jnp.concatenate([base, code[:, :, None, :]], axis=2), ((GX, 0), (GY, 1)), 2)
    near = first[:, :, :2]
    code8 = first[1:9, 1:9, 2]
    pressure = jnp.zeros((8, 8, 128), F32)
    rows = []
    for iteration in range(ITERS):
        dens, bounds = call_kd(near, code, masks)
        seen = lax.all_to_all(bounds, GX + GY, 0, 0, tiled=True)
        sums, gain = call_kf(near, dens, code8, pressure, masks)
        top = seen.max(axis=0)
        row = jnp.concatenate([top[:2], -top[2:4]])
        relax = 1.0 / (1.0 + row[:2] - row[2:])
        pressure = pressure + jnp.where(code8 == 2.0, relax[1], relax[0]) * gain
        parts = sums.reshape(6, 6, 2, 4, 128)
        delta = parts[:, :, :, 1] + relax[0] * parts[:, :, :, 2] + relax[1] * parts[:, :, :, 3]
        rows.append(row)
        if iteration < ITERS - 1:
            near = padded(base + delta, ((GX, 0), (GY, 1)), 2)
    change = jnp.stack([delta[:, :, 0], delta[:, :, 1]]) * (1.0 / TIME_STEP)
    new_velocity = jnp.where(live, velocity + TIME_STEP * other_accel + change, 0.0)
    new_position = jnp.where(live, position + TIME_STEP * new_velocity, 0.0)
    return new_position, new_velocity, pressure[1:7, 1:7], jnp.stack(rows)


def solution(mesh):
    torus = Mesh(mesh.devices.reshape(4, 2, 2, 4, 2), ("gx_0", "gx_1", "gy_0", "gy_1", "gy_2"))
    in_specs = (
        P(None, GX, GY, None),
        P(None, GX, GY, None),
        P(None, GX, GY, None),
        P(GX, GY, None),
        P(GX, GY),
    )
    out_specs = (P(None, GX, GY, None), P(None, GX, GY, None), P(GX, GY, None), P())
    return jax.shard_map(local, mesh=torus, in_specs=in_specs, out_specs=out_specs, check_vma=False)
```

time: 440 us -> 195 us (0.44)
  other arithmetic: 208 us -> 16.2 us
  blocking collectives: 123 us -> 0 us
  Pallas kernels: 0 us -> 82.1 us
  starting transfers between devices: 29.6 us -> 65.5 us
  loops' own time: 19.9 us -> 0 us
  local copies, waits for them, and re-layouts: 24 us -> 5.92 us
  waiting for transfers between devices: 29.4 us -> 22.5 us
    reduce_sum x68 -> x0, other arithmetic: 176 us -> none  [the longest x36 89.8 us: pair_sums(): total_b = total_b + jnp.sum(pair_coef * diff_y, axis=-1)]
    pmax x20 -> x0, blocking collectives: 123 us -> none  [one_axis_at_a_time(): value = lax.pmax(value, axis)]
    pallas_call x0 -> x8, Pallas kernels: none -> 82.1 us  [the longest x4 59.7 us: call_kf(): pl.pallas_call(kf_kernel, out_shape=(jax.ShapeDtypeStruct((6, 6, 8, 128),...]
    all_to_all x0 -> x4, starting transfers between devices: none -> 46.8 us  [local(): seen = lax.all_to_all(bounds, GX + GY, 0, 0, tiled=True)]
    another operation x8 -> x0, loops' own time: 19.9 us -> none  [blocked(): results = lax.map(one_block, jnp.arange(block_count, dtype=jnp.int32))]
    dynamic_slice x56 -> x0, local copies, waits for them, and re-layouts: 17.1 us -> none  [the longest x28 16.9 us: blocked(): results = lax.map(one_block, jnp.arange(block_count, dtype=jnp.int32))]
    ppermute x10 -> x8, starting transfers between devices: 28.1 us -> 13.6 us  [padded(): lax.ppermute(lax.slice_in_dim(block, block.shape[dim] - width, None, axis...]
    select_n x5 -> x2, other arithmetic: 13.8 us -> 0.11 us  [the longest x1 0.08 us: local(): jnp.where(live, rest[0], FAR)]
  transfers between devices with their start and end apart: 20 -> 20, of which waited for: 16 -> 13; matrix products, arithmetic and copies ran while one was open for 0% -> 3% of each run, Pallas kernels for 0% -> 31%
where the time goes in v1:
time: 195 us; the launch traced here: 193 us
  Pallas kernels  82.1 us (42%)
  starting transfers between devices  65.5 us (34%)
  waiting for transfers between devices  22.5 us (12%)
  other arithmetic  16.2 us (8%)
  local copies, waits for them, and re-layouts  5.92 us (3%)
    pallas_call x4, Pallas kernels, call_kf(): pl.pallas_call(kf_kernel, out_shape=(jax.ShapeDtypeStruct((6, 6, 8, 128),...  59.7 us
    all_to_all x4, starting transfers between devices, local(): seen = lax.all_to_all(bounds, GX + GY, 0, 0, tiled=True)  46.8 us
    pallas_call x4, Pallas kernels, call_kd(): pl.pallas_call(kd_kernel, out_shape=(jax.ShapeDtypeStruct((6, 6, 128), F3...  22.4 us
    ppermute x8, waiting for transfers between devices, padded(): lax.ppermute(lax.slice_in_dim(block, 0, width, axis=dim), axis, backward)  17.2 us
    ppermute x8, starting transfers between devices, padded(): lax.ppermute(lax.slice_in_dim(block, block.shape[dim] - width, None, axis...  13.6 us
    add x3, other arithmetic, local(): pressure = pressure + jnp.where(code8 == 2.0, relax[1], relax[0]) * gain  5.81 us
    ppermute x8, waiting for transfers between devices, padded(): lax.ppermute(lax.slice_in_dim(block, block.shape[dim] - width, None, axis...  5.36 us
    ppermute x8, starting transfers between devices, padded(): lax.ppermute(lax.slice_in_dim(block, 0, width, axis=dim), axis, backward)  5.06 us
  transfers between devices with their start and end apart: 20, of which 13 were waited for; matrix products, arithmetic and copies ran while one was open for 3% of the time, Pallas kernels for 31%

profile of v1, /device:TPU:103, one launch (start us, length us, event | category | flops | bytes accessed | tf_op | source)
XLA Modules:
  0.0 193.3 jit_solution(15670463333676460675)
XLA Ops:
  0.6 0.8 fusion.37
  1.5 0.8 fusion.1
  2.5 1.4 collective-permute-start.1
  3.9 1.2 collective-permute-done
  5.1 2.2 %collective-permute-done.1 = f32[2,6,3,128]{3,1,0,2:T(8,128)S(1)} collective-permute-done((f32[2,6,3,128]{3,1,0,2:T(8,128)S(1)}, f32[2,6,3,128]{3,1,0,2:T(8,128)S(1)}, u32[]{:S(2)}, u32[]{:S(2)}) %collective-permute-start.1) | collective-permute-done | bytes 18464 | tf_op jit(solution)/shard_map/ppermute | solution.py:279
  7.4 3.3 %collective-permute-start.2 = (f32[10,2,3,128]{3,1,0,2:T(2,128)S(1)}, f32[10,2,3,128]{3,1,0,2:T(2,128)S(1)}, u32[]{:S(2)}, u32[]{:S(2)}) collective-permute-start(f32[10,2,3,128]{3,1,0,2:T(2,128)S(1)} %get-tuple-element.64), channel_id=1, source_target_pairs={{0,1},{1,2},{2,3},{3,4},{4,5},{5,6},{6,7},{7,8},{8,9},{9,10},{10,1... | collective-permute-start | bytes 92168 | tf_op jit(solution)/shard_map/ppermute | solution.py:278
  10.8 0.9 collective-permute-done.2
  11.7 2.6 %collective-permute-done.3 = f32[10,2,3,128]{3,1,0,2:T(2,128)S(1)} collective-permute-done((f32[10,2,3,128]{3,1,0,2:T(2,128)S(1)}, f32[10,2,3,128]{3,1,0,2:T(2,128)S(1)}, u32[]{:S(2)}, u32[]{:S(2)}) %collective-permute-start.3) | collective-permute-done | bytes 30752 | tf_op jit(solution)/shard_map/ppermute | solution.py:279
  14.5 0.8 copy-done
  15.2 5.6 %density.4 = (f32[6,6,128]{2,1,0:T(8,128)S(1)}, f32[128,128]{1,0:T(8,128)}) custom-call(f32[10,10,2,128]{3,2,1,0:T(2,128)S(1)} %copy.54.pos_ref, f32[6,6,128]{2,1,0:T(8,128)S(1)} %select_convert_fusion.code_ref, bf16[9,32,128]{2,1,0:T(8,128)(2,1)S(1)} %copy-done), custom_call_target="tpu_custom_call" | custom-call | flops 40000000 | bytes 200000 | tf_op jit(solution)/shard_map/density/pallas_call | solution.py:248
  20.8 11.4 %all-to-all-start = ((f32[128,1,128]{2,1,0:T(1,128)}), f32[128,1,128]{2,1,0:T(1,128)S(1)}, u32[]{:S(2)}, u32[]{:S(2)}) async-start(f32[128,1,128]{2,1,0:T(1,128)} %bitcast.6), calls=%async_computation | async-start | bytes 131072 | tf_op jit(solution)/shard_map/all_to_all | solution.py:298
  32.3 14.9 %force.4 = (f32[6,6,8,128]{3,2,1,0:T(8,128)S(1)}, f32[8,8,128]{2,1,0:T(8,128)S(1)}) custom-call(f32[10,10,2,128]{3,2,1,0:T(2,128)S(1)} %copy.54.pos_ref, f32[6,6,128]{2,1,0:T(8,128)S(1)} %get-tuple-element.20.dens_ref, f32[8,8,128]{2,1,0:T(8,128)S(1)} %maximum_bitcast_fusion.code_ref, f32[8,8,128]{2,1,0:T(8,128)S(1)} %broadcast_in_dim.60.p_ref, ...), custom_call_target="tpu_custom_call" | custom-call | flops 800000000 | bytes 400000 | tf_op jit(solution)/shard_map/force/pallas_call | solution.py:259
  48.1 1.3 fusion.17
  49.8 1.2 collective-permute-start.5
  51.0 1.1 collective-permute-done.4
  52.1 2.4 %collective-permute-done.5 = f32[2,6,2,128]{3,1,0,2:T(8,128)S(1)} collective-permute-done((f32[2,6,2,128]{3,1,0,2:T(8,128)S(1)}, f32[2,6,2,128]{3,1,0,2:T(8,128)S(1)}, u32[]{:S(2)}, u32[]{:S(2)}) %collective-permute-start.5) | collective-permute-done | bytes 12320 | tf_op jit(solution)/shard_map/ppermute | solution.py:279
  54.5 3.0 %collective-permute-start.6 = (f32[10,2,2,128]{3,1,0,2:T(2,128)S(1)}, f32[10,2,2,128]{3,1,0,2:T(2,128)S(1)}, u32[]{:S(2)}, u32[]{:S(2)}) collective-permute-start(f32[10,2,2,128]{3,1,0,2:T(2,128)S(1)} %get-tuple-element.70), channel_id=1, source_target_pairs={{0,1},{1,2},{2,3},{3,4},{4,5},{5,6},{6,7},{7,8},{8,9},{9,10},{10,1... | collective-permute-start | bytes 61448 | tf_op jit(solution)/shard_map/ppermute | solution.py:278
  57.5 1.3 select_multiply_fusion
  58.8 2.2 %collective-permute-done.7 = f32[10,2,2,128]{3,1,0,2:T(2,128)S(1)} collective-permute-done((f32[10,2,2,128]{3,1,0,2:T(2,128)S(1)}, f32[10,2,2,128]{3,1,0,2:T(2,128)S(1)}, u32[]{:S(2)}, u32[]{:S(2)}) %collective-permute-start.7) | collective-permute-done | bytes 20512 | tf_op jit(solution)/shard_map/ppermute | solution.py:279
  61.1 5.6 %density.5 = (f32[6,6,128]{2,1,0:T(8,128)S(1)}, f32[128,128]{1,0:T(8,128)}) custom-call(f32[10,10,2,128]{3,2,1,0:T(2,128)S(1)} %copy.60.pos_ref, f32[6,6,128]{2,1,0:T(8,128)S(1)} %select_convert_fusion.code_ref, bf16[9,32,128]{2,1,0:T(8,128)(2,1)S(1)} %copy-done), custom_call_target="tpu_custom_call" | custom-call | flops 40000000 | bytes 200000 | tf_op jit(solution)/shard_map/density/pallas_call | solution.py:248
  66.7 11.8 %all-to-all-start.1 = ((f32[128,1,128]{2,1,0:T(1,128)}), f32[128,1,128]{2,1,0:T(1,128)S(1)}, u32[]{:S(2)}, u32[]{:S(2)}) async-start(f32[128,1,128]{2,1,0:T(1,128)} %bitcast.12), calls=%async_computation.1 | async-start | bytes 131072 | tf_op jit(solution)/shard_map/all_to_all | solution.py:298
  78.6 14.9 %force.5 = (f32[6,6,8,128]{3,2,1,0:T(8,128)S(1)}, f32[8,8,128]{2,1,0:T(8,128)S(1)}) custom-call(f32[10,10,2,128]{3,2,1,0:T(2,128)S(1)} %copy.60.pos_ref, f32[6,6,128]{2,1,0:T(8,128)S(1)} %get-tuple-element.23.dens_ref, f32[8,8,128]{2,1,0:T(8,128)S(1)} %maximum_bitcast_fusion.code_ref, f32[8,8,128]{2,1,0:T(8,128)S(1)} %get-tuple-element.50.p_ref, ...), custom_call_target="tpu_custom_call" | custom-call | flops 800000000 | bytes 400000 | tf_op jit(solution)/shard_map/force/pallas_call | solution.py:259
  94.4 1.3 fusion.13
  96.3 1.2 collective-permute-start.9
  97.6 1.0 collective-permute-done.8
  98.6 2.4 %collective-permute-done.9 = f32[2,6,2,128]{3,1,0,2:T(8,128)S(1)} collective-permute-done((f32[2,6,2,128]{3,1,0,2:T(8,128)S(1)}, f32[2,6,2,128]{3,1,0,2:T(8,128)S(1)}, u32[]{:S(2)}, u32[]{:S(2)}) %collective-permute-start.9) | collective-permute-done | bytes 12320 | tf_op jit(solution)/shard_map/ppermute | solution.py:279
  101.0 3.0 %collective-permute-start.10 = (f32[10,2,2,128]{3,1,0,2:T(2,128)S(1)}, f32[10,2,2,128]{3,1,0,2:T(2,128)S(1)}, u32[]{:S(2)}, u32[]{:S(2)}) collective-permute-start(f32[10,2,2,128]{3,1,0,2:T(2,128)S(1)} %get-tuple-element.68), channel_id=1, source_target_pairs={{0,1},{1,2},{2,3},{3,4},{4,5},{5,6},{6,7},{7,8},{8,9},{9,10},{10,1... | collective-permute-start | bytes 61448 | tf_op jit(solution)/shard_map/ppermute | solution.py:278
  104.0 2.6 %multiply_add_fusion.1.p_ref = f32[8,8,128]{2,1,0:T(8,128)S(1)} fusion(f32[8,8,128]{2,1,0:T(8,128)S(1)} %get-tuple-element.28, pred[8,8,128]{2,1,0:T(8,128)(4,1)S(1)} %get-tuple-element.51, f32[]{:T(128)} %bitcast.13, f32[]{:T(128)} %bitcast.14, f32[8,8,128]{2,1,0:T(8,128)S(1)} %get-tuple-element.24, f32[]{:T(128)} %bitcast.7, f32[]{:T(128)} %bitcast.8), kind=kLoop, calls=%fused_computation.39 | loop fusion | flops 40960 | bytes 106512 | tf_op jit(solution)/shard_map/add | solution.py:303
  106.6 0.9 collective-permute-done.11
  107.6 5.6 %density.6 = (f32[6,6,128]{2,1,0:T(8,128)S(1)}, f32[128,128]{1,0:T(8,128)}) custom-call(f32[10,10,2,128]{3,2,1,0:T(2,128)S(1)} %copy.66.pos_ref, f32[6,6,128]{2,1,0:T(8,128)S(1)} %select_convert_fusion.code_ref, bf16[9,32,128]{2,1,0:T(8,128)(2,1)S(1)} %copy-done), custom_call_target="tpu_custom_call" | custom-call | flops 40000000 | bytes 200000 | tf_op jit(solution)/shard_map/density/pallas_call | solution.py:248
  113.2 11.8 %all-to-all-start.2 = ((f32[128,1,128]{2,1,0:T(1,128)}), f32[128,1,128]{2,1,0:T(1,128)S(1)}, u32[]{:S(2)}, u32[]{:S(2)}) async-start(f32[128,1,128]{2,1,0:T(1,128)} %bitcast.18), calls=%async_computation.2 | async-start | bytes 131072 | tf_op jit(solution)/shard_map/all_to_all | solution.py:298
  125.1 14.9 %force.6 = (f32[6,6,8,128]{3,2,1,0:T(8,128)S(1)}, f32[8,8,128]{2,1,0:T(8,128)S(1)}) custom-call(f32[10,10,2,128]{3,2,1,0:T(2,128)S(1)} %copy.66.pos_ref, f32[6,6,128]{2,1,0:T(8,128)S(1)} %get-tuple-element.27.dens_ref, f32[8,8,128]{2,1,0:T(8,128)S(1)} %maximum_bitcast_fusion.code_ref, f32[8,8,128]{2,1,0:T(8,128)S(1)} %multiply_add_fusion.1.p_ref, ...), custom_call_target="tpu_custom_call" | custom-call | flops 800000000 | bytes 400000 | tf_op jit(solution)/shard_map/force/pallas_call | solution.py:259
  140.9 1.3 fusion.9
  142.6 1.2 collective-permute-start.13
  143.9 1.0 collective-permute-done.12
  144.9 2.4 %collective-permute-done.13 = f32[2,6,2,128]{3,1,0,2:T(8,128)S(1)} collective-permute-done((f32[2,6,2,128]{3,1,0,2:T(8,128)S(1)}, f32[2,6,2,128]{3,1,0,2:T(8,128)S(1)}, u32[]{:S(2)}, u32[]{:S(2)}) %collective-permute-start.13) | collective-permute-done | bytes 12320 | tf_op jit(solution)/shard_map/ppermute | solution.py:279
  147.3 3.0 %collective-permute-start.14 = (f32[10,2,2,128]{3,1,0,2:T(2,128)S(1)}, f32[10,2,2,128]{3,1,0,2:T(2,128)S(1)}, u32[]{:S(2)}, u32[]{:S(2)}) collective-permute-start(f32[10,2,2,128]{3,1,0,2:T(2,128)S(1)} %get-tuple-element.66), channel_id=1, source_target_pairs={{0,1},{1,2},{2,3},{3,4},{4,5},{5,6},{6,7},{7,8},{8,9},{9,10},{10,1... | collective-permute-start | bytes 61448 | tf_op jit(solution)/shard_map/ppermute | solution.py:278
  150.3 1.3 multiply_add_fusion.p_ref
  151.7 2.2 %collective-permute-done.15 = f32[10,2,2,128]{3,1,0,2:T(2,128)S(1)} collective-permute-done((f32[10,2,2,128]{3,1,0,2:T(2,128)S(1)}, f32[10,2,2,128]{3,1,0,2:T(2,128)S(1)}, u32[]{:S(2)}, u32[]{:S(2)}) %collective-permute-start.15) | collective-permute-done | bytes 20512 | tf_op jit(solution)/shard_map/ppermute | solution.py:279
  154.0 5.6 %density.7 = (f32[6,6,128]{2,1,0:T(8,128)S(1)}, f32[128,128]{1,0:T(8,128)}) custom-call(f32[10,10,2,128]{3,2,1,0:T(2,128)S(1)} %copy.72.pos_ref, f32[6,6,128]{2,1,0:T(8,128)S(1)} %select_convert_fusion.code_ref, bf16[9,32,128]{2,1,0:T(8,128)(2,1)S(1)} %copy-done), custom_call_target="tpu_custom_call" | custom-call | flops 40000000 | bytes 200000 | tf_op jit(solution)/shard_map/density/pallas_call | solution.py:248
  159.6 11.8 %all-to-all-start.3 = ((f32[128,1,128]{2,1,0:T(1,128)}), f32[128,1,128]{2,1,0:T(1,128)S(1)}, u32[]{:S(2)}, u32[]{:S(2)}) async-start(f32[128,1,128]{2,1,0:T(1,128)} %bitcast.24), calls=%async_computation.3 | async-start | bytes 131072 | tf_op jit(solution)/shard_map/all_to_all | solution.py:298
  171.4 14.9 %force.7 = (f32[6,6,8,128]{3,2,1,0:T(8,128)S(1)}, f32[8,8,128]{2,1,0:T(8,128)S(1)}) custom-call(f32[10,10,2,128]{3,2,1,0:T(2,128)S(1)} %copy.72.pos_ref, f32[6,6,128]{2,1,0:T(8,128)S(1)} %get-tuple-element.31.dens_ref, f32[8,8,128]{2,1,0:T(8,128)S(1)} %maximum_bitcast_fusion.code_ref, f32[8,8,128]{2,1,0:T(8,128)S(1)} %multiply_add_fusion.p_ref, ...), custom_call_target="tpu_custom_call" | custom-call | flops 800000000 | bytes 400000 | tf_op jit(solution)/shard_map/force/pallas_call | solution.py:259
  187.3 1.9 slice_add_fusion
  189.2 1.3 fusion.5
  190.5 0.7 copy-done.2
  191.3 0.6 copy.78
  192.0 0.6 copy.79
  192.7 0.6 pad_maximum_fusion.22
  (67 shorter events, 6.0 us)
Async XLA Ops:
  0.6 0.8 copy-start.1
  1.5 0.8 copy-start.5
  2.4 2.7 %collective-permute-start = (f32[2,6,3,128]{3,1,0,2:T(8,128)S(1)}, f32[2,6,3,128]{3,1,0,2:T(8,128)S(1)}, u32[]{:S(2)}, u32[]{:S(2)}) collective-permute-start(f32[2,6,3,128]{3,1,0,2:T(8,128)S(1)} %get-tuple-element.72), channel_id=1, source_target_pairs={{0,16},{16,32},{32,48},{48,64},{64,80},{80,96},{96,112},{112,0},{1... | collective-permute-start | bytes 55304 | tf_op jit(solution)/shard_map/ppermute | solution.py:278
  2.5 8.2 %copy-start.4 = (s32[6,6,128]{2,1,0:T(8,128)S(1)}, s32[6,6,128]{2,1,0:T(8,128)}, u32[]{:S(2)}) copy-start(s32[6,6,128]{2,1,0:T(8,128)} %param.9) | copy-start | bytes 55300
  2.5 4.8 %collective-permute-start.1 = (f32[2,6,3,128]{3,1,0,2:T(8,128)S(1)}, f32[2,6,3,128]{3,1,0,2:T(8,128)S(1)}, u32[]{:S(2)}, u32[]{:S(2)}) collective-permute-start(f32[2,6,3,128]{3,1,0,2:T(8,128)S(1)} %get-tuple-element.73), channel_id=1, source_target_pairs={{16,0},{32,16},{48,32},{64,48},{80,64},{96,80},{112,96},{0,112},{1... | collective-permute-start | bytes 55304 | tf_op jit(solution)/shard_map/ppermute | solution.py:279
  7.4 4.3 %collective-permute-start.2 = (f32[10,2,3,128]{3,1,0,2:T(2,128)S(1)}, f32[10,2,3,128]{3,1,0,2:T(2,128)S(1)}, u32[]{:S(2)}, u32[]{:S(2)}) collective-permute-start(f32[10,2,3,128]{3,1,0,2:T(2,128)S(1)} %get-tuple-element.64), channel_id=1, source_target_pairs={{0,1},{1,2},{2,3},{3,4},{4,5},{5,6},{6,7},{7,8},{8,9},{9,10},{10,1... | collective-permute-start | bytes 92168 | tf_op jit(solution)/shard_map/ppermute | solution.py:278
  10.7 3.6 %collective-permute-start.3 = (f32[10,2,3,128]{3,1,0,2:T(2,128)S(1)}, f32[10,2,3,128]{3,1,0,2:T(2,128)S(1)}, u32[]{:S(2)}, u32[]{:S(2)}) collective-permute-start(f32[10,2,3,128]{3,1,0,2:T(2,128)S(1)} %get-tuple-element.65), channel_id=1, source_target_pairs={{1,0},{2,1},{3,2},{4,3},{5,4},{6,5},{7,6},{8,7},{9,8},{10,9},{11,1... | collective-permute-start | bytes 92168 | tf_op jit(solution)/shard_map/ppermute | solution.py:279
  14.4 0.9 copy-start
  20.8 26.4 %all-to-all-start = ((f32[128,1,128]{2,1,0:T(1,128)}), f32[128,1,128]{2,1,0:T(1,128)S(1)}, u32[]{:S(2)}, u32[]{:S(2)}) async-start(f32[128,1,128]{2,1,0:T(1,128)} %bitcast.6), calls=%async_computation | async-start | bytes 131072 | tf_op jit(solution)/shard_map/all_to_all | solution.py:298
  49.4 2.7 %collective-permute-start.4 = (f32[2,6,2,128]{3,1,0,2:T(8,128)S(1)}, f32[2,6,2,128]{3,1,0,2:T(8,128)S(1)}, u32[]{:S(2)}, u32[]{:S(2)}) collective-permute-start(f32[2,6,2,128]{3,1,0,2:T(8,128)S(1)} %get-tuple-element.82), channel_id=1, source_target_pairs={{0,16},{16,32},{32,48},{48,64},{64,80},{80,96},{96,112},{112,0},{1... | collective-permute-start | bytes 36872 | tf_op jit(solution)/shard_map/ppermute | solution.py:278
  49.8 4.7 %collective-permute-start.5 = (f32[2,6,2,128]{3,1,0,2:T(8,128)S(1)}, f32[2,6,2,128]{3,1,0,2:T(8,128)S(1)}, u32[]{:S(2)}, u32[]{:S(2)}) collective-permute-start(f32[2,6,2,128]{3,1,0,2:T(8,128)S(1)} %get-tuple-element.83), channel_id=1, source_target_pairs={{16,0},{32,16},{48,32},{64,48},{80,64},{96,80},{112,96},{0,112},{1... | collective-permute-start | bytes 36872 | tf_op jit(solution)/shard_map/ppermute | solution.py:279
  54.5 4.3 %collective-permute-start.6 = (f32[10,2,2,128]{3,1,0,2:T(2,128)S(1)}, f32[10,2,2,128]{3,1,0,2:T(2,128)S(1)}, u32[]{:S(2)}, u32[]{:S(2)}) collective-permute-start(f32[10,2,2,128]{3,1,0,2:T(2,128)S(1)} %get-tuple-element.70), channel_id=1, source_target_pairs={{0,1},{1,2},{2,3},{3,4},{4,5},{5,6},{6,7},{7,8},{8,9},{9,10},{10,1... | collective-permute-start | bytes 61448 | tf_op jit(solution)/shard_map/ppermute | solution.py:278
  57.5 3.5 %collective-permute-start.7 = (f32[10,2,2,128]{3,1,0,2:T(2,128)S(1)}, f32[10,2,2,128]{3,1,0,2:T(2,128)S(1)}, u32[]{:S(2)}, u32[]{:S(2)}) collective-permute-start(f32[10,2,2,128]{3,1,0,2:T(2,128)S(1)} %get-tuple-element.71), channel_id=1, source_target_pairs={{1,0},{2,1},{3,2},{4,3},{5,4},{6,5},{7,6},{8,7},{9,8},{10,9},{11,1... | collective-permute-start | bytes 61448 | tf_op jit(solution)/shard_map/ppermute | solution.py:279
  66.7 26.9 %all-to-all-start.1 = ((f32[128,1,128]{2,1,0:T(1,128)}), f32[128,1,128]{2,1,0:T(1,128)S(1)}, u32[]{:S(2)}, u32[]{:S(2)}) async-start(f32[128,1,128]{2,1,0:T(1,128)} %bitcast.12), calls=%async_computation.1 | async-start | bytes 131072 | tf_op jit(solution)/shard_map/all_to_all | solution.py:298
  95.8 2.8 %collective-permute-start.8 = (f32[2,6,2,128]{3,1,0,2:T(8,128)S(1)}, f32[2,6,2,128]{3,1,0,2:T(8,128)S(1)}, u32[]{:S(2)}, u32[]{:S(2)}) collective-permute-start(f32[2,6,2,128]{3,1,0,2:T(8,128)S(1)} %get-tuple-element.80), channel_id=1, source_target_pairs={{0,16},{16,32},{32,48},{48,64},{64,80},{80,96},{96,112},{112,0},{1... | collective-permute-start | bytes 36872 | tf_op jit(solution)/shard_map/ppermute | solution.py:278
  96.3 4.7 %collective-permute-start.9 = (f32[2,6,2,128]{3,1,0,2:T(8,128)S(1)}, f32[2,6,2,128]{3,1,0,2:T(8,128)S(1)}, u32[]{:S(2)}, u32[]{:S(2)}) collective-permute-start(f32[2,6,2,128]{3,1,0,2:T(8,128)S(1)} %get-tuple-element.81), channel_id=1, source_target_pairs={{16,0},{32,16},{48,32},{64,48},{80,64},{96,80},{112,96},{0,112},{1... | collective-permute-start | bytes 36872 | tf_op jit(solution)/shard_map/ppermute | solution.py:279
  101.0 5.6 %collective-permute-start.10 = (f32[10,2,2,128]{3,1,0,2:T(2,128)S(1)}, f32[10,2,2,128]{3,1,0,2:T(2,128)S(1)}, u32[]{:S(2)}, u32[]{:S(2)}) collective-permute-start(f32[10,2,2,128]{3,1,0,2:T(2,128)S(1)} %get-tuple-element.68), channel_id=1, source_target_pairs={{0,1},{1,2},{2,3},{3,4},{4,5},{5,6},{6,7},{7,8},{8,9},{9,10},{10,1... | collective-permute-start | bytes 61448 | tf_op jit(solution)/shard_map/ppermute | solution.py:278
  104.0 3.5 %collective-permute-start.11 = (f32[10,2,2,128]{3,1,0,2:T(2,128)S(1)}, f32[10,2,2,128]{3,1,0,2:T(2,128)S(1)}, u32[]{:S(2)}, u32[]{:S(2)}) collective-permute-start(f32[10,2,2,128]{3,1,0,2:T(2,128)S(1)} %get-tuple-element.69), channel_id=1, source_target_pairs={{1,0},{2,1},{3,2},{4,3},{5,4},{6,5},{7,6},{8,7},{9,8},{10,9},{11,1... | collective-permute-start | bytes 61448 | tf_op jit(solution)/shard_map/ppermute | solution.py:279
  113.2 26.9 %all-to-all-start.2 = ((f32[128,1,128]{2,1,0:T(1,128)}), f32[128,1,128]{2,1,0:T(1,128)S(1)}, u32[]{:S(2)}, u32[]{:S(2)}) async-start(f32[128,1,128]{2,1,0:T(1,128)} %bitcast.18), calls=%async_computation.2 | async-start | bytes 131072 | tf_op jit(solution)/shard_map/all_to_all | solution.py:298
  142.3 2.7 %collective-permute-start.12 = (f32[2,6,2,128]{3,1,0,2:T(8,128)S(1)}, f32[2,6,2,128]{3,1,0,2:T(8,128)S(1)}, u32[]{:S(2)}, u32[]{:S(2)}) collective-permute-start(f32[2,6,2,128]{3,1,0,2:T(8,128)S(1)} %get-tuple-element.78), channel_id=1, source_target_pairs={{0,16},{16,32},{32,48},{48,64},{64,80},{80,96},{96,112},{112,0},{1... | collective-permute-start | bytes 36872 | tf_op jit(solution)/shard_map/ppermute | solution.py:278
  142.6 4.7 %collective-permute-start.13 = (f32[2,6,2,128]{3,1,0,2:T(8,128)S(1)}, f32[2,6,2,128]{3,1,0,2:T(8,128)S(1)}, u32[]{:S(2)}, u32[]{:S(2)}) collective-permute-start(f32[2,6,2,128]{3,1,0,2:T(8,128)S(1)} %get-tuple-element.79), channel_id=1, source_target_pairs={{16,0},{32,16},{48,32},{64,48},{80,64},{96,80},{112,96},{0,112},{1... | collective-permute-start | bytes 36872 | tf_op jit(solution)/shard_map/ppermute | solution.py:279
  147.3 4.3 %collective-permute-start.14 = (f32[10,2,2,128]{3,1,0,2:T(2,128)S(1)}, f32[10,2,2,128]{3,1,0,2:T(2,128)S(1)}, u32[]{:S(2)}, u32[]{:S(2)}) collective-permute-start(f32[10,2,2,128]{3,1,0,2:T(2,128)S(1)} %get-tuple-element.66), channel_id=1, source_target_pairs={{0,1},{1,2},{2,3},{3,4},{4,5},{5,6},{6,7},{7,8},{8,9},{9,10},{10,1... | collective-permute-start | bytes 61448 | tf_op jit(solution)/shard_map/ppermute | solution.py:278
  150.3 3.5 %collective-permute-start.15 = (f32[10,2,2,128]{3,1,0,2:T(2,128)S(1)}, f32[10,2,2,128]{3,1,0,2:T(2,128)S(1)}, u32[]{:S(2)}, u32[]{:S(2)}) collective-permute-start(f32[10,2,2,128]{3,1,0,2:T(2,128)S(1)} %get-tuple-element.67), channel_id=1, source_target_pairs={{1,0},{2,1},{3,2},{4,3},{5,4},{6,5},{7,6},{8,7},{9,8},{10,9},{11,1... | collective-permute-start | bytes 61448 | tf_op jit(solution)/shard_map/ppermute | solution.py:279
  159.6 26.9 %all-to-all-start.3 = ((f32[128,1,128]{2,1,0:T(1,128)}), f32[128,1,128]{2,1,0:T(1,128)S(1)}, u32[]{:S(2)}, u32[]{:S(2)}) async-start(f32[128,1,128]{2,1,0:T(1,128)} %bitcast.24), calls=%async_computation.3 | async-start | bytes 131072 | tf_op jit(solution)/shard_map/all_to_all | solution.py:298
  190.5 0.8 copy-start.2
  190.5 0.8 copy-start.3

commit v2 on v1

--- a/solution.py
+++ b/solution.py
@@ -10,6 +10,7 @@
 ITERS = 4
 GX = ("gx_0", "gx_1")
 GY = ("gy_0", "gy_1", "gy_2")
+ALL = GX + GY
 
 F32, BF16 = jnp.float32, jnp.bfloat16
 OFFS = tuple((ox, oy) for ox in (-1, 0, 1) for oy in (-1, 0, 1))
@@ -76,7 +77,7 @@
 def fill_slabs(pos_ref, ls, rs, lo, hi, rlo, rhi):
     def body(r, carry):
         for c in range(lo, hi):
-            left, right = cell_slabs(pos_ref, r, c)
+            left, right = cell_slabs(pos_ref, r, c, True, rlo <= c < rhi)
             ls[r, c] = left
             if rlo <= c < rhi:
                 rs[r, c] = right.astype(BF16)
@@ -85,12 +86,10 @@
 
 
 def fill_pairs(ls, lt, start, rows, cols, dr, dc, rbase, cbase):
-    def body(i, carry):
+    for i in range(rows):
         for j in range(cols):
             both = jnp.concatenate([ls[rbase + i, cbase + j], ls[rbase + i + dr, cbase + j + dc]], axis=0)
             lt[start + i * cols + j] = both.T.astype(BF16)
-        return carry
-    lax.fori_loop(0, rows, body, 0)
 
 
 def density_pair(rs, lt, masks_ref, i1, i2, first, stride):
@@ -109,7 +108,7 @@
 
 
 def density_own(pos_ref, masks_ref, ls, rs, lt, store):
-    fill_slabs(pos_ref, ls, rs, 1, 9, 2, 8)
+    fill_slabs(pos_ref, ls, rs, 1, 9, 1, 9)
     fill_pairs(ls, lt, 0, 5, 8, 3, 0, 1, 1)
     def body(b, carry):
         for a in range(3):
@@ -120,7 +119,7 @@
     lax.fori_loop(0, 6, body, 0)
 
 
-def kd_kernel(pos_ref, code_ref, masks_ref, dens_ref, bnd_ref, ls, rs, lt):
+def kd_kernel(pos_ref, code_ref, masks_ref, dens_ref, bnd_ref, lt, rs, ls):
     def store(a, b, row):
         dens_ref[a, pl.ds(b, 1), :] = row
     density_own(pos_ref, masks_ref, ls, rs, lt, store)
@@ -161,15 +160,14 @@
     return groups
 
 
-def kf_kernel(pos_ref, dens_ref, code_ref, p_ref, masks_ref, s_ref, q_ref, ls, rs, lt, dn, tt, gt):
-    fill_slabs(pos_ref, ls, rs, 0, 10, 1, 9)
-    fill_pairs(ls, lt, 0, 5, 8, 3, 0, 1, 1)
-    fill_pairs(ls, lt, 40, 3, 10, 7, 0, 0, 0)
-    fill_pairs(ls, lt, 70, 8, 3, 0, 7, 1, 0)
+def kf_kernel(pos_ref, dens_ref, code_ref, p_ref, masks_ref, lt0, rs, s_ref, q_ref, ls, lt, dn, tt, gt):
+    fill_slabs(pos_ref, ls, None, 0, 10, 0, 0)
+    fill_pairs(ls, lt, 0, 3, 10, 7, 0, 0, 0)
+    fill_pairs(ls, lt, 30, 8, 3, 0, 7, 1, 0)
     def top_bottom(h, carry):
         for u in range(2):
             c = h * 2 + u
-            row = density_pair(rs, lt, masks_ref, (1, c + 1), (8, c + 1), 50 + c + 1, 10)
+            row = density_pair(rs, lt, masks_ref, (1, c + 1), (8, c + 1), 10 + c + 1, 10)
             dn[0, pl.ds(c, 1), :] = row[:, :128]
             dn[7, pl.ds(c, 1), :] = row[:, 128:]
         return carry
@@ -177,7 +175,7 @@
     def left_right(h, carry):
         for u in range(2):
             a = h * 2 + u + 1
-            row = density_pair(rs, lt, masks_ref, (a + 1, 1), (a + 1, 8), 70 + a * 3 + 1, 3)
+            row = density_pair(rs, lt, masks_ref, (a + 1, 1), (a + 1, 8), 30 + a * 3 + 1, 3)
             dn[a, pl.ds(0, 1), :] = row[:, :128]
             dn[a, pl.ds(7, 1), :] = row[:, 128:]
         return carry
@@ -212,7 +210,7 @@
             acc = jnp.zeros((48, 256), F32)
             for k, (ox, oy) in enumerate(OFFS):
                 p = (a + 1 + ox) * 8 + bcol + 1 + oy
-                s = pair_s(lt[p], pair_rhs(r1, r2, masks_ref[k]))
+                s = pair_s(lt0[p], pair_rhs(r1, r2, masks_ref[k]))
                 w = jnp.maximum(s, 0.0)
                 w2 = w * w
                 hi = w2.astype(BF16)
@@ -235,50 +233,118 @@
                 code_row = jnp.broadcast_to(code_ref[aa + 1, pl.ds(bcol + 1, 1), :], (8, 128))
                 scale = 6.0 * KERNEL_NORM * TIME_STEP * TIME_STEP
                 coef = jnp.where(code_row == 2.0, scale / 1.5, jnp.where(code_row == 1.0, scale, 0.0))
-                s_ref[aa, bcol] = coef * (term_rows(tt, aa + 1, bcol + 1) * e0 + e)
+                out = coef * (term_rows(tt, aa + 1, bcol + 1) * e0 + e)
+                for t in range(3):
+                    s_ref[t, aa, bcol, 0:1, :] = out[t + 1:t + 2]
+                    s_ref[t, aa, bcol, 1:2, :] = out[t + 5:t + 6]
         return carry
     lax.fori_loop(0, 6, forces, 0)
 
 
+def kc_kernel(absolute, seen_ref, s_ref, base_ref, code_ref, p_ref, q_ref, pos_ref, pout_ref, row_ref):
+    top = seen_ref[...].max(axis=0, keepdims=True)
+    lane = lax.broadcasted_iota(jnp.int32, (1, 128), 1)
+    top0, top1, neg0, neg1 = (jnp.sum(jnp.where(lane == k, top, 0.0), axis=1, keepdims=True) for k in range(4))
+    row_ref[...] = jnp.where(lane < 2, top, -top)
+    r0 = 1.0 / (1.0 + top0 + neg0)
+    r1 = 1.0 / (1.0 + top1 + neg1)
+    for a in range(8):
+        pout_ref[a] = p_ref[a] + jnp.where(code_ref[a] == 2.0, r1, r0) * q_ref[a]
+    for a in range(6):
+        delta = s_ref[0, a] + r0[None] * s_ref[1, a] + r1[None] * s_ref[2, a]
+        pos_ref[a] = base_ref[a] + delta if absolute else delta
+
+
 VM = pl.BlockSpec(memory_space=pltpu.VMEM)
-LIMIT = 40 * 1024 * 1024
-
-
-def call_kd(pos, code, masks, **kw):
+LIMIT = 20 * 1024 * 1024
+
+
+def shaped(shape, dtype=F32):
+    return jax.ShapeDtypeStruct(shape, dtype)
+
+
+def call_kd(pos, code, masks):
     return pl.pallas_call(
         kd_kernel,
-        out_shape=(jax.ShapeDtypeStruct((6, 6, 128), F32), jax.ShapeDtypeStruct((128, 128), F32)),
-        in_specs=[VM] * 3, out_specs=(VM, VM),
-        scratch_shapes=[pltpu.VMEM((10, 10, 32, 128), F32), pltpu.VMEM((10, 10, 32, 128), BF16), pltpu.VMEM((40, 128, 64), BF16)],
+        out_shape=(shaped((6, 6, 128)), shaped((128, 128)), shaped((40, 128, 64), BF16), shaped((10, 10, 32, 128), BF16)),
+        in_specs=[VM] * 3, out_specs=(VM,) * 4,
+        scratch_shapes=[pltpu.VMEM((10, 10, 32, 128), F32)],
         compiler_params=pltpu.CompilerParams(vmem_limit_bytes=LIMIT),
-        cost_estimate=pl.CostEstimate(flops=4_000_000_0, bytes_accessed=200_000, transcendentals=0),
-        name="density", **kw)(pos, code, masks)
-
-
-def call_kf(pos, dens, code8, p8, masks, **kw):
+        cost_estimate=pl.CostEstimate(flops=40_000_000, bytes_accessed=200_000, transcendentals=0),
+        name="density")(pos, code, masks)
+
+
+def call_kf(pos, dens, code8, p8, masks, pairs, rights):
     return pl.pallas_call(
         kf_kernel,
-        out_shape=(jax.ShapeDtypeStruct((6, 6, 8, 128), F32), jax.ShapeDtypeStruct((8, 8, 128), F32)),
-        in_specs=[VM] * 5, out_specs=(VM, VM),
-        scratch_shapes=[pltpu.VMEM((10, 10, 32, 128), F32), pltpu.VMEM((10, 10, 32, 128), BF16), pltpu.VMEM((94, 128, 64), BF16),
+        out_shape=(shaped((3, 6, 6, 2, 128)), shaped((8, 8, 128))),
+        in_specs=[VM] * 7, out_specs=(VM, VM),
+        scratch_shapes=[pltpu.VMEM((10, 10, 32, 128), F32), pltpu.VMEM((54, 128, 64), BF16),
                         pltpu.VMEM((8, 8, 128), F32), pltpu.VMEM((3, 8, 8, 128), F32), pltpu.VMEM((40, 112, 128), BF16)],
         compiler_params=pltpu.CompilerParams(vmem_limit_bytes=LIMIT),
-        cost_estimate=pl.CostEstimate(flops=8_000_000_00, bytes_accessed=400_000, transcendentals=0),
-        name="force", **kw)(pos, dens, code8, p8, masks)
+        cost_estimate=pl.CostEstimate(flops=800_000_000, bytes_accessed=400_000, transcendentals=0),
+        name="force")(pos, dens, code8, p8, masks, pairs, rights)
+
+
+def call_kc(seen, sums, base, code8, p8, gain, absolute):
+    def kernel(*refs):
+        kc_kernel(absolute, *refs)
+    return pl.pallas_call(
+        kernel,
+        out_shape=(shaped((6, 6, 2, 128)), shaped((8, 8, 128)), shaped((1, 128))),
+        in_specs=[VM] * 6, out_specs=(VM,) * 3,
+        compiler_params=pltpu.CompilerParams(vmem_limit_bytes=LIMIT),
+        cost_estimate=pl.CostEstimate(flops=1_000_000, bytes_accessed=400_000, transcendentals=0),
+        name="combine")(seen.reshape(128, 128), sums, base, code8, p8, gain)
 
 
 FAR = 2.0 ** 20
-
-
-def padded(block, sides, width):
-    for axis, dim in sides:
-        count = lax.axis_size(axis)
-        forward = [(i, (i + 1) % count) for i in range(count)]
-        backward = [(target, source) for source, target in forward]
-        low = lax.ppermute(lax.slice_in_dim(block, block.shape[dim] - width, None, axis=dim), axis, forward)
-        high = lax.ppermute(lax.slice_in_dim(block, 0, width, axis=dim), axis, backward)
-        block = jnp.concatenate([low, block, high], axis=dim)
-    return block
+TILES = [(gx, gy) for gx in range(8) for gy in range(16)]
+
+
+def home_of(gx, gy):
+    return gx * 16 + gy
+
+
+def work_of(gx, gy):
+    x, flip = (gx, 0) if gx < 4 else (7 - gx, 1)
+    chip = gy >> 1
+    high = chip >> 2
+    y = chip & 3 if high == 0 else 3 - (chip & 3)
+    return ((x * 2 + (flip ^ high)) * 2 + high) * 8 + y * 2 + ((gx + gy) & 1)
+
+
+def to_work(block):
+    return lax.ppermute(block, ALL, [(home_of(gx, gy), work_of(gx, gy)) for gx, gy in TILES])
+
+
+def to_home(block):
+    return lax.ppermute(block, ALL, [(work_of(gx, gy), home_of(gx, gy)) for gx, gy in TILES])
+
+
+def partners(dim, near):
+    pairs = []
+    for gx, gy in TILES:
+        place, count = ((gx, 8), (gy, 16))[dim]
+        other = (place + (1 if (place % 2 == 0) == near else -1)) % count
+        pairs.append((work_of(gx, gy), work_of(*((other, gy) if dim == 0 else (gx, other)))))
+    return pairs
+
+
+def swapped(block, even, dim):
+    first = lax.slice_in_dim(block, 0, 2, axis=dim)
+    last = lax.slice_in_dim(block, 4, 6, axis=dim)
+    far = lax.ppermute(jnp.where(even, first, last), ALL, partners(dim, False))
+    near = lax.ppermute(jnp.where(even, last, first), ALL, partners(dim, True))
+    low = jnp.where(even, far, near)
+    high = jnp.where(even, near, far)
+    return jnp.concatenate([low, block, high], axis=dim)
+
+
+def padded(block):
+    odd_x = lax.axis_index("gx_0") + lax.axis_index("gx_1") + lax.axis_index("gy_0")
+    odd_y = odd_x + lax.axis_index("gy_2")
+    return swapped(swapped(block, odd_x % 2 == 0, 0), odd_y % 2 == 0, 1)
 
 
 def local(position, velocity, other_accel, phase_ids, counts):
@@ -288,28 +354,26 @@
     masks = jnp.asarray(offset_masks(), BF16)
     rest = position - 0.5 + TIME_STEP * (velocity + TIME_STEP * other_accel)
     base = jnp.stack([jnp.where(live, rest[0], FAR), jnp.where(live, rest[1], 0.0)], axis=2)
-    first = padded(jnp.concatenate([base, code[:, :, None, :]], axis=2), ((GX, 0), (GY, 1)), 2)
+    packed = to_work(jnp.concatenate([base, code[:, :, None, :]], axis=2))
+    base, code = packed[:, :, :2], packed[:, :, 2]
+    first = padded(packed)
     near = first[:, :, :2]
     code8 = first[1:9, 1:9, 2]
     pressure = jnp.zeros((8, 8, 128), F32)
     rows = []
     for iteration in range(ITERS):
-        dens, bounds = call_kd(near, code, masks)
-        seen = lax.all_to_all(bounds, GX + GY, 0, 0, tiled=True)
-        sums, gain = call_kf(near, dens, code8, pressure, masks)
-        top = seen.max(axis=0)
-        row = jnp.concatenate([top[:2], -top[2:4]])
-        relax = 1.0 / (1.0 + row[:2] - row[2:])
-        pressure = pressure + jnp.where(code8 == 2.0, relax[1], relax[0]) * gain
-        parts = sums.reshape(6, 6, 2, 4, 128)
-        delta = parts[:, :, :, 1] + relax[0] * parts[:, :, :, 2] + relax[1] * parts[:, :, :, 3]
-        rows.append(row)
+        dens, bounds, pairs, rights = call_kd(near, code, masks)
+        seen = lax.all_to_all(bounds, ALL, 0, 0, tiled=True)
+        sums, gain = call_kf(near, dens, code8, pressure, masks, pairs, rights)
+        delta, pressure, row = call_kc(seen, sums, base, code8, pressure, gain, iteration < ITERS - 1)
+        rows.append(row[0, :4])
         if iteration < ITERS - 1:
-            near = padded(base + delta, ((GX, 0), (GY, 1)), 2)
-    change = jnp.stack([delta[:, :, 0], delta[:, :, 1]]) * (1.0 / TIME_STEP)
+            near = padded(delta)
+    result = to_home(jnp.concatenate([delta, pressure[1:7, 1:7, None]], axis=2))
+    change = jnp.stack([result[:, :, 0], result[:, :, 1]]) * (1.0 / TIME_STEP)
     new_velocity = jnp.where(live, velocity + TIME_STEP * other_accel + change, 0.0)
     new_position = jnp.where(live, position + TIME_STEP * new_velocity, 0.0)
-    return new_position, new_velocity, pressure[1:7, 1:7], jnp.stack(rows)
+    return new_position, new_velocity, result[:, :, 2], jnp.stack(rows)
 
 
 def solution(mesh):

time: 195 us -> 174 us (0.89)
  other arithmetic: 16.2 us -> 3.62 us
  waiting for transfers between devices: 22.5 us -> 30.5 us
  Pallas kernels: 82.1 us -> 75.4 us
  starting transfers between devices: 65.5 us -> 60.7 us
  local copies, waits for them, and re-layouts: 5.92 us -> 2.06 us
    add x7 -> x0, other arithmetic: 11.1 us -> none  [the longest x3 5.81 us: local(): pressure = pressure + jnp.where(code8 == 2.0, relax[1], relax[0]) * gain]
    ppermute x16 -> x18, waiting for transfers between devices: 22.5 us -> 30.5 us  [the longest x8 18.4 us: swapped(): far = lax.ppermute(jnp.where(even, first, last), ALL, partners(dim, False))]
    pallas_call x8 -> x12, Pallas kernels: 82.1 us -> 75.4 us  [the longest x4 53.5 us: call_kf(): pl.pallas_call(kf_kernel, out_shape=(shaped((3, 6, 6, 2, 128)), shaped((8...]
    all_to_all x4, starting transfers between devices: 46.8 us -> 41.7 us  [local(): seen = lax.all_to_all(bounds, ALL, 0, 0, tiled=True)]
    slice x11 -> x2, local copies, waits for them, and re-layouts: 2.74 us -> 0.03 us  [local(): base, code = (packed[:, :, :2], packed[:, :, 2])]
    ppermute x16 -> x18, starting transfers between devices: 18.7 us -> 19 us  [the longest x8 6.25 us: swapped(): far = lax.ppermute(jnp.where(even, first, last), ALL, partners(dim, False))]
  transfers between devices with their start and end apart: 20 -> 22, of which waited for: 13 -> 14; matrix products, arithmetic and copies ran while one was open for 3% -> 0% of each run, Pallas kernels for 31% -> 31%
where the time goes in v2:
time: 174 us; the launch traced here: 173 us
  Pallas kernels  75.4 us (43%)
  starting transfers between devices  60.7 us (35%)
  waiting for transfers between devices  30.5 us (18%)
  other arithmetic  3.62 us (2%)
  local copies, waits for them, and re-layouts  2.06 us (1%)
    pallas_call x4, Pallas kernels, call_kf(): pl.pallas_call(kf_kernel, out_shape=(shaped((3, 6, 6, 2, 128)), shaped((8...  53.5 us
    all_to_all x4, starting transfers between devices, local(): seen = lax.all_to_all(bounds, ALL, 0, 0, tiled=True)  41.7 us
    pallas_call x4, Pallas kernels, call_kd(): pl.pallas_call(kd_kernel, out_shape=(shaped((6, 6, 128)), shaped((128, 12...  21.4 us
    ppermute x8, waiting for transfers between devices, swapped(): far = lax.ppermute(jnp.where(even, first, last), ALL, partners(dim, False))  18.4 us
    ppermute x8, starting transfers between devices, swapped(): far = lax.ppermute(jnp.where(even, first, last), ALL, partners(dim, False))  6.25 us
    ppermute x1, starting transfers between devices, to_home(): lax.ppermute(block, ALL, [(work_of(gx, gy), home_of(gx, gy)) for gx, gy i...  5.64 us
    ppermute x1, waiting for transfers between devices, to_work(): lax.ppermute(block, ALL, [(home_of(gx, gy), work_of(gx, gy)) for gx, gy i...  5.36 us
    ppermute x1, waiting for transfers between devices, to_home(): lax.ppermute(block, ALL, [(work_of(gx, gy), home_of(gx, gy)) for gx, gy i...  5.19 us
  transfers between devices with their start and end apart: 22, of which 14 were waited for; matrix products, arithmetic and copies ran while one was open for 0% of the time, Pallas kernels for 31%

profile of v2, /device:TPU:103, one launch (start us, length us, event | category | flops | bytes accessed | tf_op | source)
XLA Modules:
  0.0 173.4 jit_solution(15669026784280846584)
XLA Ops:
  0.6 0.8 convert_bitcast_fusion
  1.5 0.8 fusion.1
  2.3 0.8 fusion.5
  3.1 5.0 %collective-permute-start = (f32[6,6,3,128]{3,1,0,2:T(8,128)S(1)}, f32[6,6,3,128]{3,1,0,2:T(8,128)S(1)}, u32[]{:S(2)}, u32[]{:S(2)}) collective-permute-start(f32[6,6,3,128]{3,1,0,2:T(8,128)S(1)} %pad_maximum_fusion.4), channel_id=1, source_target_pairs={{0,0},{1,1},{2,2},{3,3},{4,4},{5,5},{6,6},{7,7},{8,30},{9,31},{10,... | collective-permute-start | bytes 165896 | tf_op jit(solution)/shard_map/ppermute | solution.py:318
  8.1 5.4 %collective-permute-done = f32[6,6,3,128]{3,1,0,2:T(8,128)S(1)} collective-permute-done((f32[6,6,3,128]{3,1,0,2:T(8,128)S(1)}, f32[6,6,3,128]{3,1,0,2:T(8,128)S(1)}, u32[]{:S(2)}, u32[]{:S(2)}) %collective-permute-start) | collective-permute-done | bytes 55328 | tf_op jit(solution)/shard_map/ppermute | solution.py:318
  13.6 3.2 %collective-permute-done.1 = f32[2,6,3,128]{3,1,0,2:T(8,128)S(1)} collective-permute-done((f32[2,6,3,128]{3,1,0,2:T(8,128)S(1)}, f32[2,6,3,128]{3,1,0,2:T(8,128)S(1)}, u32[]{:S(2)}, u32[]{:S(2)}) %collective-permute-start.1) | collective-permute-done | bytes 18464 | tf_op jit(solution)/shard_map/ppermute | solution.py:337
  16.9 0.5 collective-permute-start.4
  17.5 0.7 collective-permute-done.4
  18.2 2.5 %collective-permute-done.3 = f32[10,2,3,128]{3,1,0,2:T(2,128)S(1)} collective-permute-done((f32[10,2,3,128]{3,1,0,2:T(2,128)S(1)}, f32[10,2,3,128]{3,1,0,2:T(2,128)S(1)}, u32[]{:S(2)}, u32[]{:S(2)}) %collective-permute-start.3) | collective-permute-done | bytes 30752 | tf_op jit(solution)/shard_map/ppermute | solution.py:337
  20.8 5.4 %density.4 = (f32[6,6,128]{2,1,0:T(8,128)S(1)}, f32[128,128]{1,0:T(8,128)}, bf16[40,128,64]{2,1,0:T(8,128)(2,1)S(1)}, bf16[10,10,32,128]{3,2,1,0:T(8,128)(2,1)S(1)}) custom-call(f32[10,10,2,128]{3,2,1,0:T(2,128)S(1)} %copy.26.pos_ref, f32[6,6,128]{2,1,0:T(8,128)S(1)} %slice_bitcast_fusion.3.code_ref, bf16[9,32,128]{2,1,0:T(8,128)(2,1)S(1)} %copy-done), custom_call_target="tpu_custom_call" | custom-call | flops 40000000 | bytes 200000 | tf_op jit(solution)/shard_map/density/pallas_call | solution.py:267
  26.2 10.5 %all-to-all-start = ((f32[128,1,128]{2,1,0:T(1,128)}), f32[128,1,128]{2,1,0:T(1,128)S(1)}, u32[]{:S(2)}, u32[]{:S(2)}) async-start(f32[128,1,128]{2,1,0:T(1,128)} %bitcast.5), calls=%async_computation | async-start | bytes 131072 | tf_op jit(solution)/shard_map/all_to_all | solution.py:366
  36.8 13.5 %force.4 = (f32[3,6,6,2,128]{4,3,2,1,0:T(2,128)S(1)}, f32[8,8,128]{2,1,0:T(8,128)S(1)}) custom-call(f32[10,10,2,128]{3,2,1,0:T(2,128)S(1)} %copy.26.pos_ref, f32[6,6,128]{2,1,0:T(8,128)S(1)} %get-tuple-element.41.dens_ref, f32[8,8,128]{2,1,0:T(8,128)S(1)} %maximum_bitcast_fusion.code_ref.refs_3_, f32[8,8,128]{2,1,0:T(8,128)S(1)} %broadcast_in_dim.37.p_ref.refs_4_, ...), custom_call_target="tpu_custom_call" | custom-call | flops 800000000 | bytes 400000 | tf_op jit(solution)/shard_map/force/pallas_call | solution.py:278
  50.2 0.1 combine.4
  50.4 0.6 collective-permute-start.5
  51.0 0.5 collective-permute-start.6
  51.6 2.3 %collective-permute-done.5 = f32[2,6,2,128]{3,2,1,0:T(2,128)S(1)} collective-permute-done((f32[2,6,2,128]{3,2,1,0:T(2,128)S(1)}, f32[2,6,2,128]{3,2,1,0:T(2,128)S(1)}, u32[]{:S(2)}, u32[]{:S(2)}) %collective-permute-start.5) | collective-permute-done | bytes 12320 | tf_op jit(solution)/shard_map/ppermute | solution.py:337
  53.9 0.3 collective-permute-done.6
  54.2 1.3 collective-permute-start.7
  55.6 1.9 %collective-permute-done.7 = f32[10,2,2,128]{3,2,1,0:T(2,128)S(1)} collective-permute-done((f32[10,2,2,128]{3,2,1,0:T(2,128)S(1)}, f32[10,2,2,128]{3,2,1,0:T(2,128)S(1)}, u32[]{:S(2)}, u32[]{:S(2)}) %collective-permute-start.7) | collective-permute-done | bytes 20512 | tf_op jit(solution)/shard_map/ppermute | solution.py:337
  57.6 5.3 %density.5 = (f32[6,6,128]{2,1,0:T(8,128)S(1)}, f32[128,128]{1,0:T(8,128)}, bf16[40,128,64]{2,1,0:T(8,128)(2,1)S(1)}, bf16[10,10,32,128]{3,2,1,0:T(8,128)(2,1)S(1)}) custom-call(f32[10,10,2,128]{3,2,1,0:T(2,128)S(1)} %pad_maximum_fusion.1.pos_ref, f32[6,6,128]{2,1,0:T(8,128)S(1)} %slice_bitcast_fusion.3.code_ref, bf16[9,32,128]{2,1,0:T(8,128)(2,1)S(1)} %copy-done), custom_call_target="tpu_custom_call" | custom-call | flops 40000000 | bytes 200000 | tf_op jit(solution)/shard_map/density/pallas_call | solution.py:267
  62.9 10.4 %all-to-all-start.1 = ((f32[128,1,128]{2,1,0:T(1,128)}), f32[128,1,128]{2,1,0:T(1,128)S(1)}, u32[]{:S(2)}, u32[]{:S(2)}) async-start(f32[128,1,128]{2,1,0:T(1,128)} %bitcast.9), calls=%async_computation.1 | async-start | bytes 131072 | tf_op jit(solution)/shard_map/all_to_all | solution.py:366
  73.3 13.4 %force.5 = (f32[3,6,6,2,128]{4,3,2,1,0:T(2,128)S(1)}, f32[8,8,128]{2,1,0:T(8,128)S(1)}) custom-call(f32[10,10,2,128]{3,2,1,0:T(2,128)S(1)} %pad_maximum_fusion.1.pos_ref, f32[6,6,128]{2,1,0:T(8,128)S(1)} %get-tuple-element.48.dens_ref, f32[8,8,128]{2,1,0:T(8,128)S(1)} %maximum_bitcast_fusion.code_ref.refs_3_, ...), custom_call_target="tpu_custom_call" | custom-call | flops 800000000 | bytes 400000 | tf_op jit(solution)/shard_map/force/pallas_call | solution.py:278
  86.8 0.1 combine.5
  86.9 0.8 collective-permute-start.9
  87.8 0.5 collective-permute-start.10
  88.3 2.3 %collective-permute-done.9 = f32[2,6,2,128]{3,2,1,0:T(2,128)S(1)} collective-permute-done((f32[2,6,2,128]{3,2,1,0:T(2,128)S(1)}, f32[2,6,2,128]{3,2,1,0:T(2,128)S(1)}, u32[]{:S(2)}, u32[]{:S(2)}) %collective-permute-start.9) | collective-permute-done | bytes 12320 | tf_op jit(solution)/shard_map/ppermute | solution.py:337
  90.6 0.3 collective-permute-done.10
  90.9 1.3 collective-permute-start.11
  92.3 1.9 %collective-permute-done.11 = f32[10,2,2,128]{3,2,1,0:T(2,128)S(1)} collective-permute-done((f32[10,2,2,128]{3,2,1,0:T(2,128)S(1)}, f32[10,2,2,128]{3,2,1,0:T(2,128)S(1)}, u32[]{:S(2)}, u32[]{:S(2)}) %collective-permute-start.11) | collective-permute-done | bytes 20512 | tf_op jit(solution)/shard_map/ppermute | solution.py:337
  94.3 5.3 %density.6 = (f32[6,6,128]{2,1,0:T(8,128)S(1)}, f32[128,128]{1,0:T(8,128)}, bf16[40,128,64]{2,1,0:T(8,128)(2,1)S(1)}, bf16[10,10,32,128]{3,2,1,0:T(8,128)(2,1)S(1)}) custom-call(f32[10,10,2,128]{3,2,1,0:T(2,128)S(1)} %pad_maximum_fusion.2.pos_ref, f32[6,6,128]{2,1,0:T(8,128)S(1)} %slice_bitcast_fusion.3.code_ref, bf16[9,32,128]{2,1,0:T(8,128)(2,1)S(1)} %copy-done), custom_call_target="tpu_custom_call" | custom-call | flops 40000000 | bytes 200000 | tf_op jit(solution)/shard_map/density/pallas_call | solution.py:267
  99.6 10.4 %all-to-all-start.2 = ((f32[128,1,128]{2,1,0:T(1,128)}), f32[128,1,128]{2,1,0:T(1,128)S(1)}, u32[]{:S(2)}, u32[]{:S(2)}) async-start(f32[128,1,128]{2,1,0:T(1,128)} %bitcast.12), calls=%async_computation.2 | async-start | bytes 131072 | tf_op jit(solution)/shard_map/all_to_all | solution.py:366
  110.1 13.3 %force.6 = (f32[3,6,6,2,128]{4,3,2,1,0:T(2,128)S(1)}, f32[8,8,128]{2,1,0:T(8,128)S(1)}) custom-call(f32[10,10,2,128]{3,2,1,0:T(2,128)S(1)} %pad_maximum_fusion.2.pos_ref, f32[6,6,128]{2,1,0:T(8,128)S(1)} %get-tuple-element.56.dens_ref, f32[8,8,128]{2,1,0:T(8,128)S(1)} %maximum_bitcast_fusion.code_ref.refs_3_, ...), custom_call_target="tpu_custom_call" | custom-call | flops 800000000 | bytes 400000 | tf_op jit(solution)/shard_map/force/pallas_call | solution.py:278
  123.4 0.1 combine.6
  123.6 0.7 collective-permute-start.13
  124.2 0.5 collective-permute-start.14
  124.8 2.3 %collective-permute-done.13 = f32[2,6,2,128]{3,2,1,0:T(2,128)S(1)} collective-permute-done((f32[2,6,2,128]{3,2,1,0:T(2,128)S(1)}, f32[2,6,2,128]{3,2,1,0:T(2,128)S(1)}, u32[]{:S(2)}, u32[]{:S(2)}) %collective-permute-start.13) | collective-permute-done | bytes 12320 | tf_op jit(solution)/shard_map/ppermute | solution.py:337
  127.1 0.3 collective-permute-done.14
  127.4 1.3 collective-permute-start.15
  128.8 1.9 %collective-permute-done.15 = f32[10,2,2,128]{3,2,1,0:T(2,128)S(1)} collective-permute-done((f32[10,2,2,128]{3,2,1,0:T(2,128)S(1)}, f32[10,2,2,128]{3,2,1,0:T(2,128)S(1)}, u32[]{:S(2)}, u32[]{:S(2)}) %collective-permute-start.15) | collective-permute-done | bytes 20512 | tf_op jit(solution)/shard_map/ppermute | solution.py:337
  130.8 5.3 %density.7 = (f32[6,6,128]{2,1,0:T(8,128)S(1)}, f32[128,128]{1,0:T(8,128)}, bf16[40,128,64]{2,1,0:T(8,128)(2,1)S(1)}, bf16[10,10,32,128]{3,2,1,0:T(8,128)(2,1)S(1)}) custom-call(f32[10,10,2,128]{3,2,1,0:T(2,128)S(1)} %pad_maximum_fusion.3.pos_ref, f32[6,6,128]{2,1,0:T(8,128)S(1)} %slice_bitcast_fusion.3.code_ref, bf16[9,32,128]{2,1,0:T(8,128)(2,1)S(1)} %copy-done), custom_call_target="tpu_custom_call" | custom-call | flops 40000000 | bytes 200000 | tf_op jit(solution)/shard_map/density/pallas_call | solution.py:267
  136.1 10.4 %all-to-all-start.3 = ((f32[128,1,128]{2,1,0:T(1,128)}), f32[128,1,128]{2,1,0:T(1,128)S(1)}, u32[]{:S(2)}, u32[]{:S(2)}) async-start(f32[128,1,128]{2,1,0:T(1,128)} %bitcast.15), calls=%async_computation.3 | async-start | bytes 131072 | tf_op jit(solution)/shard_map/all_to_all | solution.py:366
  146.6 13.3 %force.7 = (f32[3,6,6,2,128]{4,3,2,1,0:T(2,128)S(1)}, f32[8,8,128]{2,1,0:T(8,128)S(1)}) custom-call(f32[10,10,2,128]{3,2,1,0:T(2,128)S(1)} %pad_maximum_fusion.3.pos_ref, f32[6,6,128]{2,1,0:T(8,128)S(1)} %get-tuple-element.64.dens_ref, f32[8,8,128]{2,1,0:T(8,128)S(1)} %maximum_bitcast_fusion.code_ref.refs_3_, ...), custom_call_target="tpu_custom_call" | custom-call | flops 800000000 | bytes 400000 | tf_op jit(solution)/shard_map/force/pallas_call | solution.py:278
  160.0 5.6 %collective-permute-start.17 = (f32[6,6,3,128]{3,1,0,2:T(8,128)S(1)}, f32[6,6,3,128]{3,1,0,2:T(8,128)S(1)}, u32[]{:S(2)}, u32[]{:S(2)}) collective-permute-start(f32[6,6,3,128]{3,1,0,2:T(8,128)S(1)} %pad_maximum_fusion.5), channel_id=1, source_target_pairs={{0,0},{1,1},{2,2},{3,3},{4,4},{5,5},{6,6},{7,7},{30,8},{31,9},{28,... | collective-permute-start | bytes 165896 | tf_op jit(solution)/shard_map/ppermute | solution.py:322
  165.7 0.6 pad_maximum_fusion.18
  166.3 5.2 %collective-permute-done.17 = f32[6,6,3,128]{3,1,0,2:T(8,128)S(1)} collective-permute-done((f32[6,6,3,128]{3,1,0,2:T(8,128)S(1)}, f32[6,6,3,128]{3,1,0,2:T(8,128)S(1)}, u32[]{:S(2)}, u32[]{:S(2)}) %collective-permute-start.17) | collective-permute-done | bytes 55328 | tf_op jit(solution)/shard_map/ppermute | solution.py:322
  171.5 0.6 slice_bitcast_fusion
  172.1 0.6 copy.38
  172.8 0.6 copy.39
  (59 shorter events, 1.1 us)
Async XLA Ops:
  0.6 20.2 %copy-start = (bf16[9,32,128]{2,1,0:T(8,128)(2,1)S(1)}, bf16[9,32,128]{2,1,0:T(8,128)(2,1)}, u32[]{:S(2)}) copy-start(bf16[9,32,128]{2,1,0:T(8,128)(2,1)} %constant.62.clone.masks_ref) | copy-start | bytes 221188
  3.1 10.3 %collective-permute-start = (f32[6,6,3,128]{3,1,0,2:T(8,128)S(1)}, f32[6,6,3,128]{3,1,0,2:T(8,128)S(1)}, u32[]{:S(2)}, u32[]{:S(2)}) collective-permute-start(f32[6,6,3,128]{3,1,0,2:T(8,128)S(1)} %pad_maximum_fusion.4), channel_id=1, source_target_pairs={{0,0},{1,1},{2,2},{3,3},{4,4},{5,5},{6,6},{7,7},{8,30},{9,31},{10,... | collective-permute-start | bytes 165896 | tf_op jit(solution)/shard_map/ppermute | solution.py:318
  13.4 3.3 %collective-permute-start.1 = (f32[2,6,3,128]{3,1,0,2:T(8,128)S(1)}, f32[2,6,3,128]{3,1,0,2:T(8,128)S(1)}, u32[]{:S(2)}, u32[]{:S(2)}) collective-permute-start(f32[2,6,3,128]{3,1,0,2:T(8,128)S(1)} %get-tuple-element.92), channel_id=1, source_target_pairs={{0,17},{1,16},{2,19},{3,18},{4,21},{5,20},{6,23},{7,22},{30,15},{3... | collective-permute-start | bytes 55304 | tf_op jit(solution)/shard_map/ppermute | solution.py:337
  13.4 3.3 %collective-permute-start.2 = (f32[2,6,3,128]{3,1,0,2:T(8,128)S(1)}, f32[2,6,3,128]{3,1,0,2:T(8,128)S(1)}, u32[]{:S(2)}, u32[]{:S(2)}) collective-permute-start(f32[2,6,3,128]{3,1,0,2:T(8,128)S(1)} %get-tuple-element.93), channel_id=1, source_target_pairs={{0,33},{1,32},{2,35},{3,34},{4,37},{5,36},{6,39},{7,38},{30,63},{3... | collective-permute-start | bytes 55304 | tf_op jit(solution)/shard_map/ppermute | solution.py:338
  16.9 1.3 collective-permute-start.4
  17.3 3.3 %collective-permute-start.3 = (f32[10,2,3,128]{3,1,0,2:T(2,128)S(1)}, f32[10,2,3,128]{3,1,0,2:T(2,128)S(1)}, u32[]{:S(2)}, u32[]{:S(2)}) collective-permute-start(f32[10,2,3,128]{3,1,0,2:T(2,128)S(1)} %get-tuple-element.86), channel_id=1, source_target_pairs={{0,25},{1,2},{2,1},{3,4},{4,3},{5,6},{6,5},{7,30},{30,7},{31,28},{... | collective-permute-start | bytes 92168 | tf_op jit(solution)/shard_map/ppermute | solution.py:337
  26.2 24.0 %all-to-all-start = ((f32[128,1,128]{2,1,0:T(1,128)}), f32[128,1,128]{2,1,0:T(1,128)S(1)}, u32[]{:S(2)}, u32[]{:S(2)}) async-start(f32[128,1,128]{2,1,0:T(1,128)} %bitcast.5), calls=%async_computation | async-start | bytes 131072 | tf_op jit(solution)/shard_map/all_to_all | solution.py:366
  50.4 3.5 %collective-permute-start.5 = (f32[2,6,2,128]{3,2,1,0:T(2,128)S(1)}, f32[2,6,2,128]{3,2,1,0:T(2,128)S(1)}, u32[]{:S(2)}, u32[]{:S(2)}) collective-permute-start(f32[2,6,2,128]{3,2,1,0:T(2,128)S(1)} %get-tuple-element.116), channel_id=1, source_target_pairs={{0,17},{1,16},{2,19},{3,18},{4,21},{5,20},{6,23},{7,22},{30,15},{3... | collective-permute-start | bytes 36872 | tf_op jit(solution)/shard_map/ppermute | solution.py:337
  51.0 3.1 %collective-permute-start.6 = (f32[2,6,2,128]{3,2,1,0:T(2,128)S(1)}, f32[2,6,2,128]{3,2,1,0:T(2,128)S(1)}, u32[]{:S(2)}, u32[]{:S(2)}) collective-permute-start(f32[2,6,2,128]{3,2,1,0:T(2,128)S(1)} %get-tuple-element.117), channel_id=1, source_target_pairs={{0,33},{1,32},{2,35},{3,34},{4,37},{5,36},{6,39},{7,38},{30,63},{3... | collective-permute-start | bytes 36872 | tf_op jit(solution)/shard_map/ppermute | solution.py:338
  54.2 3.3 %collective-permute-start.7 = (f32[10,2,2,128]{3,2,1,0:T(2,128)S(1)}, f32[10,2,2,128]{3,2,1,0:T(2,128)S(1)}, u32[]{:S(2)}, u32[]{:S(2)}) collective-permute-start(f32[10,2,2,128]{3,2,1,0:T(2,128)S(1)} %get-tuple-element.98), channel_id=1, source_target_pairs={{0,25},{1,2},{2,1},{3,4},{4,3},{5,6},{6,5},{7,30},{30,7},{31,28},{... | collective-permute-start | bytes 61448 | tf_op jit(solution)/shard_map/ppermute | solution.py:337
  55.6 1.9 %collective-permute-start.8 = (f32[10,2,2,128]{3,2,1,0:T(2,128)S(1)}, f32[10,2,2,128]{3,2,1,0:T(2,128)S(1)}, u32[]{:S(2)}, u32[]{:S(2)}) collective-permute-start(f32[10,2,2,128]{3,2,1,0:T(2,128)S(1)} %get-tuple-element.99), channel_id=1, source_target_pairs={{0,1},{1,0},{2,3},{3,2},{4,5},{5,4},{6,7},{7,6},{30,31},{31,30},{2... | collective-permute-start | bytes 61448 | tf_op jit(solution)/shard_map/ppermute | solution.py:338
  62.9 23.9 %all-to-all-start.1 = ((f32[128,1,128]{2,1,0:T(1,128)}), f32[128,1,128]{2,1,0:T(1,128)S(1)}, u32[]{:S(2)}, u32[]{:S(2)}) async-start(f32[128,1,128]{2,1,0:T(1,128)} %bitcast.9), calls=%async_computation.1 | async-start | bytes 131072 | tf_op jit(solution)/shard_map/all_to_all | solution.py:366
  86.9 3.7 %collective-permute-start.9 = (f32[2,6,2,128]{3,2,1,0:T(2,128)S(1)}, f32[2,6,2,128]{3,2,1,0:T(2,128)S(1)}, u32[]{:S(2)}, u32[]{:S(2)}) collective-permute-start(f32[2,6,2,128]{3,2,1,0:T(2,128)S(1)} %get-tuple-element.114), channel_id=1, source_target_pairs={{0,17},{1,16},{2,19},{3,18},{4,21},{5,20},{6,23},{7,22},{30,15},{3... | collective-permute-start | bytes 36872 | tf_op jit(solution)/shard_map/ppermute | solution.py:337
  87.8 3.1 %collective-permute-start.10 = (f32[2,6,2,128]{3,2,1,0:T(2,128)S(1)}, f32[2,6,2,128]{3,2,1,0:T(2,128)S(1)}, u32[]{:S(2)}, u32[]{:S(2)}) collective-permute-start(f32[2,6,2,128]{3,2,1,0:T(2,128)S(1)} %get-tuple-element.115), channel_id=1, source_target_pairs={{0,33},{1,32},{2,35},{3,34},{4,37},{5,36},{6,39},{7,38},{30,63},{3... | collective-permute-start | bytes 36872 | tf_op jit(solution)/shard_map/ppermute | solution.py:338
  90.9 3.3 %collective-permute-start.11 = (f32[10,2,2,128]{3,2,1,0:T(2,128)S(1)}, f32[10,2,2,128]{3,2,1,0:T(2,128)S(1)}, u32[]{:S(2)}, u32[]{:S(2)}) collective-permute-start(f32[10,2,2,128]{3,2,1,0:T(2,128)S(1)} %get-tuple-element.96), channel_id=1, source_target_pairs={{0,25},{1,2},{2,1},{3,4},{4,3},{5,6},{6,5},{7,30},{30,7},{31,28},{... | collective-permute-start | bytes 61448 | tf_op jit(solution)/shard_map/ppermute | solution.py:337
  92.3 1.9 %collective-permute-start.12 = (f32[10,2,2,128]{3,2,1,0:T(2,128)S(1)}, f32[10,2,2,128]{3,2,1,0:T(2,128)S(1)}, u32[]{:S(2)}, u32[]{:S(2)}) collective-permute-start(f32[10,2,2,128]{3,2,1,0:T(2,128)S(1)} %get-tuple-element.97), channel_id=1, source_target_pairs={{0,1},{1,0},{2,3},{3,2},{4,5},{5,4},{6,7},{7,6},{30,31},{31,30},{2... | collective-permute-start | bytes 61448 | tf_op jit(solution)/shard_map/ppermute | solution.py:338
  99.6 23.8 %all-to-all-start.2 = ((f32[128,1,128]{2,1,0:T(1,128)}), f32[128,1,128]{2,1,0:T(1,128)S(1)}, u32[]{:S(2)}, u32[]{:S(2)}) async-start(f32[128,1,128]{2,1,0:T(1,128)} %bitcast.12), calls=%async_computation.2 | async-start | bytes 131072 | tf_op jit(solution)/shard_map/all_to_all | solution.py:366
  110.1 18.7 %copy-start.4 = (s32[6,6]{1,0:T(8,128)S(1)}, s32[6,6]{1,0:T(8,128)}, u32[]{:S(2)}) copy-start(s32[6,6]{1,0:T(8,128)} %param.10) | copy-start | bytes 436
  123.6 3.5 %collective-permute-start.13 = (f32[2,6,2,128]{3,2,1,0:T(2,128)S(1)}, f32[2,6,2,128]{3,2,1,0:T(2,128)S(1)}, u32[]{:S(2)}, u32[]{:S(2)}) collective-permute-start(f32[2,6,2,128]{3,2,1,0:T(2,128)S(1)} %get-tuple-element.112), channel_id=1, source_target_pairs={{0,17},{1,16},{2,19},{3,18},{4,21},{5,20},{6,23},{7,22},{30,15},{3... | collective-permute-start | bytes 36872 | tf_op jit(solution)/shard_map/ppermute | solution.py:337
  124.2 3.1 %collective-permute-start.14 = (f32[2,6,2,128]{3,2,1,0:T(2,128)S(1)}, f32[2,6,2,128]{3,2,1,0:T(2,128)S(1)}, u32[]{:S(2)}, u32[]{:S(2)}) collective-permute-start(f32[2,6,2,128]{3,2,1,0:T(2,128)S(1)} %get-tuple-element.113), channel_id=1, source_target_pairs={{0,33},{1,32},{2,35},{3,34},{4,37},{5,36},{6,39},{7,38},{30,63},{3... | collective-permute-start | bytes 36872 | tf_op jit(solution)/shard_map/ppermute | solution.py:338
  127.4 3.3 %collective-permute-start.15 = (f32[10,2,2,128]{3,2,1,0:T(2,128)S(1)}, f32[10,2,2,128]{3,2,1,0:T(2,128)S(1)}, u32[]{:S(2)}, u32[]{:S(2)}) collective-permute-start(f32[10,2,2,128]{3,2,1,0:T(2,128)S(1)} %get-tuple-element.94), channel_id=1, source_target_pairs={{0,25},{1,2},{2,1},{3,4},{4,3},{5,6},{6,5},{7,30},{30,7},{31,28},{... | collective-permute-start | bytes 61448 | tf_op jit(solution)/shard_map/ppermute | solution.py:337
  128.7 2.0 %collective-permute-start.16 = (f32[10,2,2,128]{3,2,1,0:T(2,128)S(1)}, f32[10,2,2,128]{3,2,1,0:T(2,128)S(1)}, u32[]{:S(2)}, u32[]{:S(2)}) collective-permute-start(f32[10,2,2,128]{3,2,1,0:T(2,128)S(1)} %get-tuple-element.95), channel_id=1, source_target_pairs={{0,1},{1,0},{2,3},{3,2},{4,5},{5,4},{6,7},{7,6},{30,31},{31,30},{2... | collective-permute-start | bytes 61448 | tf_op jit(solution)/shard_map/ppermute | solution.py:338
  136.1 23.7 %all-to-all-start.3 = ((f32[128,1,128]{2,1,0:T(1,128)}), f32[128,1,128]{2,1,0:T(1,128)S(1)}, u32[]{:S(2)}, u32[]{:S(2)}) async-start(f32[128,1,128]{2,1,0:T(1,128)} %bitcast.15), calls=%async_computation.3 | async-start | bytes 131072 | tf_op jit(solution)/shard_map/all_to_all | solution.py:366
  146.5 25.6 %copy-start.1 = (f32[2,6,6,128]{3,0,2,1:T(2,128)S(1)}, f32[2,6,6,128]{3,0,2,1:T(2,128)}, u32[]{:S(2)}) copy-start(f32[2,6,6,128]{3,0,2,1:T(2,128)} %param.6) | copy-start | bytes 110596
  146.5 25.5 %copy-start.2 = (f32[2,6,6,128]{3,0,2,1:T(2,128)S(1)}, f32[2,6,6,128]{3,0,2,1:T(2,128)}, u32[]{:S(2)}) copy-start(f32[2,6,6,128]{3,0,2,1:T(2,128)} %param.8) | copy-start | bytes 110596
  146.6 25.5 %copy-start.3 = (f32[2,6,6,128]{3,0,2,1:T(2,128)S(1)}, f32[2,6,6,128]{3,0,2,1:T(2,128)}, u32[]{:S(2)}) copy-start(f32[2,6,6,128]{3,0,2,1:T(2,128)} %param.7) | copy-start | bytes 110596
  160.0 11.4 %collective-permute-start.17 = (f32[6,6,3,128]{3,1,0,2:T(8,128)S(1)}, f32[6,6,3,128]{3,1,0,2:T(8,128)S(1)}, u32[]{:S(2)}, u32[]{:S(2)}) collective-permute-start(f32[6,6,3,128]{3,1,0,2:T(8,128)S(1)} %pad_maximum_fusion.5), channel_id=1, source_target_pairs={{0,0},{1,1},{2,2},{3,3},{4,4},{5,5},{6,6},{7,7},{30,8},{31,9},{28,... | collective-permute-start | bytes 165896 | tf_op jit(solution)/shard_map/ppermute | solution.py:322

commit v3 on v2

--- a/solution.py
+++ b/solution.py
@@ -92,39 +92,27 @@
             lt[start + i * cols + j] = both.T.astype(BF16)
 
 
-def density_pair(rs, lt, masks_ref, i1, i2, first, stride):
+def density_pair(rs, lt, masks_ref, i1, i2, first, stride, squares=None, at=0):
     r1, r2 = rs[i1[0], i1[1]], rs[i2[0], i2[1]]
     acc = jnp.zeros((8, 256), F32)
     for k, (ox, oy) in enumerate(OFFS):
         s = pair_s(lt[first + ox * stride + oy], pair_rhs(r1, r2, masks_ref[k]))
         w = jnp.maximum(s, 0.0)
-        w3 = w * w * w
+        w2 = w * w
+        if squares is not None:
+            squares[at * 9 + k] = w2
+        w3 = w2 * w
         acc = acc + w3.reshape(16, 8, 256).sum(axis=0)
     return acc.sum(axis=0, keepdims=True)
+
 
 TIME_STEP = 0.05
 KERNEL_NORM = 4.0 / (3.141592653589793 * 64.0)
 SENTINEL = 1.0e30
 
 
-def density_own(pos_ref, masks_ref, ls, rs, lt, store):
-    fill_slabs(pos_ref, ls, rs, 1, 9, 1, 9)
-    fill_pairs(ls, lt, 0, 5, 8, 3, 0, 1, 1)
-    def body(b, carry):
-        for a in range(3):
-            row = density_pair(rs, lt, masks_ref, (a + 2, b + 2), (a + 5, b + 2), (a + 1) * 8 + b + 1, 8)
-            store(a, b, row[:, :128])
-            store(a + 3, b, row[:, 128:])
-        return carry
-    lax.fori_loop(0, 6, body, 0)
-
-
-def kd_kernel(pos_ref, code_ref, masks_ref, dens_ref, bnd_ref, lt, rs, ls):
-    def store(a, b, row):
-        dens_ref[a, pl.ds(b, 1), :] = row
-    density_own(pos_ref, masks_ref, ls, rs, lt, store)
-    code = code_ref[...]
-    ratio = dens_ref[...] * jnp.where(code == 2.0, KERNEL_NORM / 1.5, KERNEL_NORM / 1.2)
+def bounds_of(dens, code, bnd_ref):
+    ratio = dens * jnp.where(code == 2.0, KERNEL_NORM / 1.5, KERNEL_NORM / 1.2)
     picks = []
     for phase in (1.0, 2.0):
         picks.append(jnp.where(code == phase, ratio, -SENTINEL))
@@ -160,14 +148,22 @@
     return groups
 
 
-def kf_kernel(pos_ref, dens_ref, code_ref, p_ref, masks_ref, lt0, rs, s_ref, q_ref, ls, lt, dn, tt, gt):
-    fill_slabs(pos_ref, ls, None, 0, 10, 0, 0)
-    fill_pairs(ls, lt, 0, 3, 10, 7, 0, 0, 0)
-    fill_pairs(ls, lt, 30, 8, 3, 0, 7, 1, 0)
+def kdf_kernel(pos_ref, base_ref, code_ref, own_ref, p_ref, masks_ref, bnd_ref, s_ref, q_ref, ls, rs, lt, dn, tt, gt, squares):
+    fill_slabs(pos_ref, ls, rs, 0, 10, 1, 9)
+    fill_pairs(ls, lt, 0, 5, 8, 3, 0, 1, 1)
+    fill_pairs(ls, lt, 40, 3, 10, 7, 0, 0, 0)
+    fill_pairs(ls, lt, 70, 8, 3, 0, 7, 1, 0)
+    def own(b, carry):
+        for a in range(3):
+            row = density_pair(rs, lt, masks_ref, (a + 2, b + 2), (a + 5, b + 2), (a + 1) * 8 + b + 1, 8, squares, b * 3 + a)
+            dn[a + 1, pl.ds(b + 1, 1), :] = row[:, :128]
+            dn[a + 4, pl.ds(b + 1, 1), :] = row[:, 128:]
+        return carry
+    lax.fori_loop(0, 6, own, 0)
     def top_bottom(h, carry):
         for u in range(2):
             c = h * 2 + u
-            row = density_pair(rs, lt, masks_ref, (1, c + 1), (8, c + 1), 10 + c + 1, 10)
+            row = density_pair(rs, lt, masks_ref, (1, c + 1), (8, c + 1), 50 + c + 1, 10)
             dn[0, pl.ds(c, 1), :] = row[:, :128]
             dn[7, pl.ds(c, 1), :] = row[:, 128:]
         return carry
@@ -175,13 +171,12 @@
     def left_right(h, carry):
         for u in range(2):
             a = h * 2 + u + 1
-            row = density_pair(rs, lt, masks_ref, (a + 1, 1), (a + 1, 8), 30 + a * 3 + 1, 3)
+            row = density_pair(rs, lt, masks_ref, (a + 1, 1), (a + 1, 8), 70 + a * 3 + 1, 3)
             dn[a, pl.ds(0, 1), :] = row[:, :128]
             dn[a, pl.ds(7, 1), :] = row[:, 128:]
         return carry
     lax.fori_loop(0, 3, left_right, 0)
-    for a in range(6):
-        dn[a + 1, pl.ds(1, 6), :] = dens_ref[a]
+    bounds_of(dn[...], own_ref[...], bnd_ref)
     code = code_ref[...]
     live = code > 0.0
     heavy = code == 2.0
@@ -204,19 +199,21 @@
         return carry
     lax.fori_loop(0, 5, moments, 0)
     row = row_iota()
-    def forces(bcol, carry):
-        for a in range(3):
-            r1, r2 = rs[a + 2, bcol + 2], rs[a + 5, bcol + 2]
-            acc = jnp.zeros((48, 256), F32)
-            for k, (ox, oy) in enumerate(OFFS):
+    def forces(step, carry):
+        accs = [jnp.zeros((48, 256), F32) for _ in range(2)]
+        work = [((2 * step + m) % 3, (2 * step + m) // 3) for m in range(2)]
+        for k, (ox, oy) in enumerate(OFFS):
+            for m in range(2):
+                a, bcol = work[m]
                 p = (a + 1 + ox) * 8 + bcol + 1 + oy
-                s = pair_s(lt0[p], pair_rhs(r1, r2, masks_ref[k]))
-                w = jnp.maximum(s, 0.0)
-                w2 = w * w
+                w2 = squares[(2 * step + m) * 9 + k]
                 hi = w2.astype(BF16)
                 lo = (w2 - hi.astype(F32)).astype(BF16)
                 g = jnp.concatenate([gt[p, 0:16], gt[p, 32 + 16 * ox:48 + 16 * ox], gt[p, 80 + 16 * oy:96 + 16 * oy]], axis=0)
-                acc = acc + jnp.dot(jnp.concatenate([g, g], axis=1), jnp.concatenate([hi, lo], axis=0), preferred_element_type=F32)
+                accs[m] = accs[m] + jnp.dot(jnp.concatenate([g, g], axis=1), jnp.concatenate([hi, lo], axis=0), preferred_element_type=F32)
+        for m in range(2):
+            a, bcol = work[m]
+            acc = accs[m]
             for h in range(2):
                 aa = a + 3 * h
                 lanes = slice(128 * h, 128 * h + 128)
@@ -234,68 +231,56 @@
                 scale = 6.0 * KERNEL_NORM * TIME_STEP * TIME_STEP
                 coef = jnp.where(code_row == 2.0, scale / 1.5, jnp.where(code_row == 1.0, scale, 0.0))
                 out = coef * (term_rows(tt, aa + 1, bcol + 1) * e0 + e)
-                for t in range(3):
+                s_ref[0, aa, bcol, 0:1, :] = base_ref[aa, bcol, 0:1, :] + out[1:2]
+                s_ref[0, aa, bcol, 1:2, :] = base_ref[aa, bcol, 1:2, :] + out[5:6]
+                for t in (1, 2):
                     s_ref[t, aa, bcol, 0:1, :] = out[t + 1:t + 2]
                     s_ref[t, aa, bcol, 1:2, :] = out[t + 5:t + 6]
         return carry
-    lax.fori_loop(0, 6, forces, 0)
-
-
-def kc_kernel(absolute, seen_ref, s_ref, base_ref, code_ref, p_ref, q_ref, pos_ref, pout_ref, row_ref):
+    lax.fori_loop(0, 9, forces, 0)
+
+
+def kc_kernel(seen_ref, s_ref, code_ref, p_ref, q_ref, pos_ref, pout_ref, row_ref):
     top = seen_ref[...].max(axis=0, keepdims=True)
     lane = lax.broadcasted_iota(jnp.int32, (1, 128), 1)
     top0, top1, neg0, neg1 = (jnp.sum(jnp.where(lane == k, top, 0.0), axis=1, keepdims=True) for k in range(4))
-    row_ref[...] = jnp.where(lane < 2, top, -top)
     r0 = 1.0 / (1.0 + top0 + neg0)
     r1 = 1.0 / (1.0 + top1 + neg1)
+    row_ref[...] = jnp.where(lane < 2, top, jnp.where(lane < 4, -top, jnp.where(lane == 4, r0, r1)))
     for a in range(8):
         pout_ref[a] = p_ref[a] + jnp.where(code_ref[a] == 2.0, r1, r0) * q_ref[a]
-    for a in range(6):
-        delta = s_ref[0, a] + r0[None] * s_ref[1, a] + r1[None] * s_ref[2, a]
-        pos_ref[a] = base_ref[a] + delta if absolute else delta
+    for a in range(10):
+        pos_ref[a] = s_ref[0, a] + r0[None] * s_ref[1, a] + r1[None] * s_ref[2, a]
 
 
 VM = pl.BlockSpec(memory_space=pltpu.VMEM)
-LIMIT = 20 * 1024 * 1024
 
 
 def shaped(shape, dtype=F32):
     return jax.ShapeDtypeStruct(shape, dtype)
 
 
-def call_kd(pos, code, masks):
+def call_kdf(pos, base, code8, own8, p8, masks):
     return pl.pallas_call(
-        kd_kernel,
-        out_shape=(shaped((6, 6, 128)), shaped((128, 128)), shaped((40, 128, 64), BF16), shaped((10, 10, 32, 128), BF16)),
-        in_specs=[VM] * 3, out_specs=(VM,) * 4,
-        scratch_shapes=[pltpu.VMEM((10, 10, 32, 128), F32)],
-        compiler_params=pltpu.CompilerParams(vmem_limit_bytes=LIMIT),
-        cost_estimate=pl.CostEstimate(flops=40_000_000, bytes_accessed=200_000, transcendentals=0),
-        name="density")(pos, code, masks)
-
-
-def call_kf(pos, dens, code8, p8, masks, pairs, rights):
+        kdf_kernel,
+        out_shape=(shaped((128, 128)), shaped((3, 6, 6, 2, 128)), shaped((8, 8, 128))),
+        in_specs=[VM] * 6, out_specs=(VM,) * 3,
+        scratch_shapes=[pltpu.VMEM((10, 10, 32, 128), F32), pltpu.VMEM((10, 10, 32, 128), BF16), pltpu.VMEM((94, 128, 64), BF16),
+                        pltpu.VMEM((8, 8, 128), F32), pltpu.VMEM((3, 8, 8, 128), F32), pltpu.VMEM((40, 112, 128), BF16),
+                        pltpu.VMEM((162, 128, 256), F32)],
+        compiler_params=pltpu.CompilerParams(vmem_limit_bytes=40 * 1024 * 1024),
+        cost_estimate=pl.CostEstimate(flops=40_000_000, bytes_accessed=400_000, transcendentals=0),
+        name="sweep")(pos, base, code8, own8, p8, masks)
+
+
+def call_kc(seen, sums, code8, p8, gain):
     return pl.pallas_call(
-        kf_kernel,
-        out_shape=(shaped((3, 6, 6, 2, 128)), shaped((8, 8, 128))),
-        in_specs=[VM] * 7, out_specs=(VM, VM),
-        scratch_shapes=[pltpu.VMEM((10, 10, 32, 128), F32), pltpu.VMEM((54, 128, 64), BF16),
-                        pltpu.VMEM((8, 8, 128), F32), pltpu.VMEM((3, 8, 8, 128), F32), pltpu.VMEM((40, 112, 128), BF16)],
-        compiler_params=pltpu.CompilerParams(vmem_limit_bytes=LIMIT),
-        cost_estimate=pl.CostEstimate(flops=800_000_000, bytes_accessed=400_000, transcendentals=0),
-        name="force")(pos, dens, code8, p8, masks, pairs, rights)
-
-
-def call_kc(seen, sums, base, code8, p8, gain, absolute):
-    def kernel(*refs):
-        kc_kernel(absolute, *refs)
-    return pl.pallas_call(
-        kernel,
-        out_shape=(shaped((6, 6, 2, 128)), shaped((8, 8, 128)), shaped((1, 128))),
-        in_specs=[VM] * 6, out_specs=(VM,) * 3,
-        compiler_params=pltpu.CompilerParams(vmem_limit_bytes=LIMIT),
+        kc_kernel,
+        out_shape=(shaped((10, 10, 2, 128)), shaped((8, 8, 128)), shaped((1, 128))),
+        in_specs=[VM] * 5, out_specs=(VM,) * 3,
+        compiler_params=pltpu.CompilerParams(vmem_limit_bytes=8 * 1024 * 1024),
         cost_estimate=pl.CostEstimate(flops=1_000_000, bytes_accessed=400_000, transcendentals=0),
-        name="combine")(seen.reshape(128, 128), sums, base, code8, p8, gain)
+        name="combine")(seen.reshape(128, 128), sums, code8, p8, gain)
 
 
 FAR = 2.0 ** 20
@@ -307,7 +292,8 @@
 
 
 def work_of(gx, gy):
-    x, flip = (gx, 0) if gx < 4 else (7 - gx, 1)
+    x = gx >> 1
+    flip = (gx ^ x) & 1
     chip = gy >> 1
     high = chip >> 2
     y = chip & 3 if high == 0 else 3 - (chip & 3)
@@ -332,13 +318,13 @@
 
 
 def swapped(block, even, dim):
-    first = lax.slice_in_dim(block, 0, 2, axis=dim)
-    last = lax.slice_in_dim(block, 4, 6, axis=dim)
+    first = lax.slice_in_dim(block, 0, 2, axis=dim + 1)
+    last = lax.slice_in_dim(block, 4, 6, axis=dim + 1)
     far = lax.ppermute(jnp.where(even, first, last), ALL, partners(dim, False))
     near = lax.ppermute(jnp.where(even, last, first), ALL, partners(dim, True))
     low = jnp.where(even, far, near)
     high = jnp.where(even, near, far)
-    return jnp.concatenate([low, block, high], axis=dim)
+    return jnp.concatenate([low, block, high], axis=dim + 1)
 
 
 def padded(block):
@@ -355,25 +341,33 @@
     rest = position - 0.5 + TIME_STEP * (velocity + TIME_STEP * other_accel)
     base = jnp.stack([jnp.where(live, rest[0], FAR), jnp.where(live, rest[1], 0.0)], axis=2)
     packed = to_work(jnp.concatenate([base, code[:, :, None, :]], axis=2))
-    base, code = packed[:, :, :2], packed[:, :, 2]
-    first = padded(packed)
+    base = packed[:, :, :2]
+    first = padded(packed[None])[0]
     near = first[:, :, :2]
     code8 = first[1:9, 1:9, 2]
+    own8 = jnp.pad(packed[:, :, 2], ((1, 1), (1, 1), (0, 0)))
     pressure = jnp.zeros((8, 8, 128), F32)
     rows = []
     for iteration in range(ITERS):
-        dens, bounds, pairs, rights = call_kd(near, code, masks)
+        last = iteration == ITERS - 1
+        bounds, sums, gain = call_kdf(near, jnp.zeros_like(base) if last else base, code8, own8, pressure, masks)
         seen = lax.all_to_all(bounds, ALL, 0, 0, tiled=True)
-        sums, gain = call_kf(near, dens, code8, pressure, masks, pairs, rights)
-        delta, pressure, row = call_kc(seen, sums, base, code8, pressure, gain, iteration < ITERS - 1)
-        rows.append(row[0, :4])
-        if iteration < ITERS - 1:
-            near = padded(delta)
-    result = to_home(jnp.concatenate([delta, pressure[1:7, 1:7, None]], axis=2))
-    change = jnp.stack([result[:, :, 0], result[:, :, 1]]) * (1.0 / TIME_STEP)
-    new_velocity = jnp.where(live, velocity + TIME_STEP * other_accel + change, 0.0)
+        if not last:
+            wide = padded(sums)
+            near, pressure, row = call_kc(seen, wide, code8, pressure, gain)
+            rows.append(row[0, :4])
+    top = seen.reshape(128, 128).max(axis=0)
+    row = jnp.concatenate([top[:2], -top[2:4]])
+    rows.append(row)
+    relax = 1.0 / (1.0 + row[:2] - row[2:])
+    parts = jnp.stack([sums[0, :, :, 0], sums[0, :, :, 1], sums[1, :, :, 0], sums[1, :, :, 1], sums[2, :, :, 0], sums[2, :, :, 1],
+                       pressure[1:7, 1:7], gain[1:7, 1:7]])
+    parts = to_home(parts)
+    delta = parts[0:2] + relax[0] * parts[2:4] + relax[1] * parts[4:6]
+    new_velocity = jnp.where(live, velocity + TIME_STEP * other_accel + delta * (1.0 / TIME_STEP), 0.0)
     new_position = jnp.where(live, position + TIME_STEP * new_velocity, 0.0)
-    return new_position, new_velocity, result[:, :, 2], jnp.stack(rows)
+    new_pressure = parts[6] + jnp.where(phase_ids == 1, relax[1], relax[0]) * parts[7]
+    return new_position, new_velocity, new_pressure, jnp.stack(rows)
 
 
 def solution(mesh):

time: 174 us -> 168 us (0.966); the launches traced: 173 us -> 165 us
  Pallas kernels: 75.4 us -> 59 us
  waiting for transfers between devices: 30.5 us -> 38.2 us
  starting transfers between devices: 60.7 us -> 57.4 us
  other arithmetic: 3.62 us -> 6.2 us
    pallas_call x12 -> x7, Pallas kernels: 75.4 us -> 59 us  [the longest x4 58.5 us: call_kdf(): pl.pallas_call(kdf_kernel, out_shape=(shaped((128, 128)), shaped((3, 6, 6...]
    all_to_all x4, waiting for transfers between devices: 0.01 us -> 16.3 us  [local(): seen = lax.all_to_all(bounds, ALL, 0, 0, tiled=True)]
    all_to_all x4, starting transfers between devices: 41.7 us -> 31.6 us  [local(): seen = lax.all_to_all(bounds, ALL, 0, 0, tiled=True)]
    ppermute x8, starting transfers between devices: 2.17 us -> 8.2 us  [swapped(): near = lax.ppermute(jnp.where(even, last, first), ALL, partners(dim, True))]
    ppermute x8, waiting for transfers between devices: 18.4 us -> 12.6 us  [swapped(): far = lax.ppermute(jnp.where(even, first, last), ALL, partners(dim, False))]
    ppermute x1, waiting for transfers between devices: 5.36 us -> 2.43 us  [to_work(): lax.ppermute(block, ALL, [(home_of(gx, gy), work_of(gx, gy)) for gx, gy i...]
    ppermute x8, waiting for transfers between devices: 1.57 us -> 3.6 us  [swapped(): near = lax.ppermute(jnp.where(even, last, first), ALL, partners(dim, True))]
    ppermute x1, waiting for transfers between devices: 5.19 us -> 3.25 us  [to_home(): lax.ppermute(block, ALL, [(work_of(gx, gy), home_of(gx, gy)) for gx, gy i...]
  transfers between devices with their start and end apart: 22 -> 22, of which waited for: 14 -> 16; matrix products, arithmetic and copies ran while one was open for 0% -> 1% of each run, Pallas kernels for 31% -> 0%
where the time goes in v3:
time: 168 us; the launch traced here: 165 us
  Pallas kernels  59 us (35%)
  starting transfers between devices  57.4 us (34%)
  waiting for transfers between devices  38.2 us (23%)
  other arithmetic  6.2 us (4%)
  local copies, waits for them, and re-layouts  3.59 us (2%)
    pallas_call x4, Pallas kernels, call_kdf(): pl.pallas_call(kdf_kernel, out_shape=(shaped((128, 128)), shaped((3, 6, 6...  58.5 us
    all_to_all x4, starting transfers between devices, local(): seen = lax.all_to_all(bounds, ALL, 0, 0, tiled=True)  31.6 us
    all_to_all x4, waiting for transfers between devices, local(): seen = lax.all_to_all(bounds, ALL, 0, 0, tiled=True)  16.3 us
    ppermute x8, waiting for transfers between devices, swapped(): far = lax.ppermute(jnp.where(even, first, last), ALL, partners(dim, False))  12.6 us
    ppermute x8, starting transfers between devices, swapped(): near = lax.ppermute(jnp.where(even, last, first), ALL, partners(dim, True))  8.2 us
    ppermute x8, starting transfers between devices, swapped(): far = lax.ppermute(jnp.where(even, first, last), ALL, partners(dim, False))  7.47 us
    ppermute x1, starting transfers between devices, to_work(): lax.ppermute(block, ALL, [(home_of(gx, gy), work_of(gx, gy)) for gx, gy i...  5.2 us
    ppermute x1, starting transfers between devices, to_home(): lax.ppermute(block, ALL, [(work_of(gx, gy), home_of(gx, gy)) for gx, gy i...  4.91 us
  transfers between devices with their start and end apart: 22, of which 16 were waited for; matrix products, arithmetic and copies ran while one was open for 1% of the time, Pallas kernels for 0%

profile of v3, /device:TPU:103, one launch (start us, length us, event | category | flops | bytes accessed | tf_op | source)
XLA Modules:
  0.0 165.5 jit_solution(14494258971723075554)
XLA Ops:
  0.6 0.8 fusion.1
  1.6 0.7 copy-done.4
  2.3 5.2 %collective-permute-start = (f32[6,6,3,128]{3,1,0,2:T(8,128)S(1)}, f32[6,6,3,128]{3,1,0,2:T(8,128)S(1)}, u32[]{:S(2)}, u32[]{:S(2)}) collective-permute-start(f32[6,6,3,128]{3,1,0,2:T(8,128)S(1)} %pad_maximum_fusion.3), channel_id=1, source_target_pairs={{0,0},{1,1},{2,2},{3,3},{4,4},{5,5},{6,6},{7,7},{8,30},{9,31},{10,... | collective-permute-start | bytes 165896 | tf_op jit(solution)/shard_map/ppermute | solution.py:304
  7.5 2.4 %collective-permute-done = f32[6,6,3,128]{3,1,0,2:T(8,128)S(1)} collective-permute-done((f32[6,6,3,128]{3,1,0,2:T(8,128)S(1)}, f32[6,6,3,128]{3,1,0,2:T(8,128)S(1)}, u32[]{:S(2)}, u32[]{:S(2)}) %collective-permute-start) | collective-permute-done | bytes 55328 | tf_op jit(solution)/shard_map/ppermute | solution.py:304
  10.0 1.5 collective-permute-start.1
  11.4 0.4 collective-permute-start.2
  11.8 2.6 %collective-permute-done.1 = f32[1,2,6,3,128]{4,2,1,3,0:T(8,128)S(1)} collective-permute-done((f32[1,2,6,3,128]{4,2,1,3,0:T(8,128)S(1)}, f32[1,2,6,3,128]{4,2,1,3,0:T(8,128)S(1)}, u32[]{:S(2)}, u32[]{:S(2)}) %collective-permute-start.1) | collective-permute-done | bytes 18464 | tf_op jit(solution)/shard_map/ppermute | solution.py:323
  14.4 0.2 collective-permute-done.2
  14.8 0.2 collective-permute-start.4
  14.9 0.4 collective-permute-start.3
  15.4 0.7 collective-permute-done.4
  16.0 2.2 %collective-permute-done.3 = f32[1,10,2,3,128]{4,2,1,3,0:T(2,128)S(1)} collective-permute-done((f32[1,10,2,3,128]{4,2,1,3,0:T(2,128)S(1)}, f32[1,10,2,3,128]{4,2,1,3,0:T(2,128)S(1)}, u32[]{:S(2)}, u32[]{:S(2)}) %collective-permute-start.3) | collective-permute-done | bytes 30752 | tf_op jit(solution)/shard_map/ppermute | solution.py:323
  18.5 0.8 copy-done
  19.3 14.6 %sweep.4 = (f32[128,128]{1,0:T(8,128)}, f32[3,6,6,2,128]{4,3,2,1,0:T(2,128)S(1)}, f32[8,8,128]{2,1,0:T(8,128)S(1)}) custom-call(f32[10,10,2,128]{3,2,1,0:T(2,128)S(1)} %copy.29.pos_ref, f32[6,6,2,128]{3,2,1,0:T(2,128)S(1)} %copy.30.base_ref, f32[8,8,128]{2,1,0:T(8,128)S(1)} %slice_bitcast_fusion.code_ref, f32[8,8,128]{2,1,0:T(8,128)S(1)} %pad.4.own_ref, ...), custom_call_target="tpu_custom_call" | custom-call | flops 40000000 | bytes 400000 | tf_op jit(solution)/shard_map/sweep/pallas_call | solution.py:264
  33.9 1.8 %collective-permute-start.5 = (f32[3,2,6,2,128]{4,3,2,1,0:T(2,128)S(1)}, f32[3,2,6,2,128]{4,3,2,1,0:T(2,128)S(1)}, u32[]{:S(2)}, u32[]{:S(2)}) collective-permute-start(f32[3,2,6,2,128]{4,3,2,1,0:T(2,128)S(1)} %get-tuple-element.75), channel_id=1, source_target_pairs={{0,97},{1,96},{2,99},{3,98},{4,101},{5,100},{6,103},{7,102},{30,12... | collective-permute-start | bytes 110600 | tf_op jit(solution)/shard_map/ppermute | solution.py:323
  35.7 2.8 %collective-permute-done.5 = f32[3,2,6,2,128]{4,3,2,1,0:T(2,128)S(1)} collective-permute-done((f32[3,2,6,2,128]{4,3,2,1,0:T(2,128)S(1)}, f32[3,2,6,2,128]{4,3,2,1,0:T(2,128)S(1)}, u32[]{:S(2)}, u32[]{:S(2)}) %collective-permute-start.5) | collective-permute-done | bytes 36896 | tf_op jit(solution)/shard_map/ppermute | solution.py:323
  38.6 0.8 collective-permute-done.6
  39.6 1.4 collective-permute-start.8
  41.0 9.6 %all-to-all-start = ((f32[128,1,128]{2,1,0:T(1,128)}), f32[128,1,128]{2,1,0:T(1,128)S(1)}, u32[]{:S(2)}, u32[]{:S(2)}) async-start(f32[128,1,128]{2,1,0:T(1,128)} %bitcast.8), calls=%async_computation | async-start | bytes 131072 | tf_op jit(solution)/shard_map/all_to_all | solution.py:354
  50.8 5.3 %all-to-all-done = f32[128,1,128]{2,1,0:T(1,128)S(1)} async-done(((f32[128,1,128]{2,1,0:T(1,128)}), f32[128,1,128]{2,1,0:T(1,128)S(1)}, u32[]{:S(2)}, u32[]{:S(2)}) %all-to-all-start) | async-done | bytes 65568 | tf_op jit(solution)/shard_map/all_to_all | solution.py:354
  56.1 0.2 combine.3
  56.3 14.6 %sweep.5 = (f32[128,128]{1,0:T(8,128)}, f32[3,6,6,2,128]{4,3,2,1,0:T(2,128)S(1)}, f32[8,8,128]{2,1,0:T(8,128)S(1)}) custom-call(f32[10,10,2,128]{3,2,1,0:T(2,128)S(1)} %get-tuple-element.28.pos_ref, f32[6,6,2,128]{3,2,1,0:T(2,128)S(1)} %copy.30.base_ref, f32[8,8,128]{2,1,0:T(8,128)S(1)} %slice_bitcast_fusion.code_ref, f32[8,8,128]{2,1,0:T(8,128)S(1)} %pad.4.own_ref, ...), custom_call_target="tpu_custom_call" | custom-call | flops 40000000 | bytes 400000 | tf_op jit(solution)/shard_map/sweep/pallas_call | solution.py:264
  70.9 1.5 collective-permute-start.10
  72.4 1.2 collective-permute-start.9
  73.6 1.3 collective-permute-done.10
  74.9 2.1 %collective-permute-done.9 = f32[3,2,6,2,128]{4,3,2,1,0:T(2,128)S(1)} collective-permute-done((f32[3,2,6,2,128]{4,3,2,1,0:T(2,128)S(1)}, f32[3,2,6,2,128]{4,3,2,1,0:T(2,128)S(1)}, u32[]{:S(2)}, u32[]{:S(2)}) %collective-permute-start.9) | collective-permute-done | bytes 36896 | tf_op jit(solution)/shard_map/ppermute | solution.py:323
  77.2 2.2 %collective-permute-start.12 = (f32[3,10,2,2,128]{4,3,2,1,0:T(2,128)S(1)}, f32[3,10,2,2,128]{4,3,2,1,0:T(2,128)S(1)}, u32[]{:S(2)}, u32[]{:S(2)}) collective-permute-start(f32[3,10,2,2,128]{4,3,2,1,0:T(2,128)S(1)} %get-tuple-element.62), channel_id=1, source_target_pairs={{0,1},{1,0},{2,3},{3,2},{4,5},{5,4},{6,7},{7,6},{30,31},{31,30},{2... | collective-permute-start | bytes 184328 | tf_op jit(solution)/shard_map/ppermute | solution.py:324
  79.4 6.7 %all-to-all-start.1 = ((f32[128,1,128]{2,1,0:T(1,128)}), f32[128,1,128]{2,1,0:T(1,128)S(1)}, u32[]{:S(2)}, u32[]{:S(2)}) async-start(f32[128,1,128]{2,1,0:T(1,128)} %bitcast.11), calls=%async_computation.1 | async-start | bytes 131072 | tf_op jit(solution)/shard_map/all_to_all | solution.py:354
  86.3 5.3 %all-to-all-done.1 = f32[128,1,128]{2,1,0:T(1,128)S(1)} async-done(((f32[128,1,128]{2,1,0:T(1,128)}), f32[128,1,128]{2,1,0:T(1,128)S(1)}, u32[]{:S(2)}, u32[]{:S(2)}) %all-to-all-start.1) | async-done | bytes 65568 | tf_op jit(solution)/shard_map/all_to_all | solution.py:354
  91.6 0.2 combine.4
  91.8 14.6 %sweep.6 = (f32[128,128]{1,0:T(8,128)}, f32[3,6,6,2,128]{4,3,2,1,0:T(2,128)S(1)}, f32[8,8,128]{2,1,0:T(8,128)S(1)}) custom-call(f32[10,10,2,128]{3,2,1,0:T(2,128)S(1)} %get-tuple-element.33.pos_ref, f32[6,6,2,128]{3,2,1,0:T(2,128)S(1)} %copy.30.base_ref, f32[8,8,128]{2,1,0:T(8,128)S(1)} %slice_bitcast_fusion.code_ref, f32[8,8,128]{2,1,0:T(8,128)S(1)} %pad.4.own_ref, ...), custom_call_target="tpu_custom_call" | custom-call | flops 40000000 | bytes 400000 | tf_op jit(solution)/shard_map/sweep/pallas_call | solution.py:264
  106.4 2.4 %collective-permute-start.13 = (f32[3,2,6,2,128]{4,3,2,1,0:T(2,128)S(1)}, f32[3,2,6,2,128]{4,3,2,1,0:T(2,128)S(1)}, u32[]{:S(2)}, u32[]{:S(2)}) collective-permute-start(f32[3,2,6,2,128]{4,3,2,1,0:T(2,128)S(1)} %get-tuple-element.71), channel_id=1, source_target_pairs={{0,97},{1,96},{2,99},{3,98},{4,101},{5,100},{6,103},{7,102},{30,12... | collective-permute-start | bytes 110600 | tf_op jit(solution)/shard_map/ppermute | solution.py:323
  108.8 2.8 %collective-permute-done.13 = f32[3,2,6,2,128]{4,3,2,1,0:T(2,128)S(1)} collective-permute-done((f32[3,2,6,2,128]{4,3,2,1,0:T(2,128)S(1)}, f32[3,2,6,2,128]{4,3,2,1,0:T(2,128)S(1)}, u32[]{:S(2)}, u32[]{:S(2)}) %collective-permute-start.13) | collective-permute-done | bytes 36896 | tf_op jit(solution)/shard_map/ppermute | solution.py:323
  111.6 0.5 collective-permute-done.14
  112.3 2.5 %collective-permute-start.16 = (f32[3,10,2,2,128]{4,3,2,1,0:T(2,128)S(1)}, f32[3,10,2,2,128]{4,3,2,1,0:T(2,128)S(1)}, u32[]{:S(2)}, u32[]{:S(2)}) collective-permute-start(f32[3,10,2,2,128]{4,3,2,1,0:T(2,128)S(1)} %get-tuple-element.60), channel_id=1, source_target_pairs={{0,1},{1,0},{2,3},{3,2},{4,5},{5,4},{6,7},{7,6},{30,31},{31,30},{2... | collective-permute-start | bytes 184328 | tf_op jit(solution)/shard_map/ppermute | solution.py:324
  115.0 6.8 %all-to-all-start.2 = ((f32[128,1,128]{2,1,0:T(1,128)}), f32[128,1,128]{2,1,0:T(1,128)S(1)}, u32[]{:S(2)}, u32[]{:S(2)}) async-start(f32[128,1,128]{2,1,0:T(1,128)} %bitcast.14), calls=%async_computation.2 | async-start | bytes 131072 | tf_op jit(solution)/shard_map/all_to_all | solution.py:354
  122.0 5.3 %all-to-all-done.2 = f32[128,1,128]{2,1,0:T(1,128)S(1)} async-done(((f32[128,1,128]{2,1,0:T(1,128)}), f32[128,1,128]{2,1,0:T(1,128)S(1)}, u32[]{:S(2)}, u32[]{:S(2)}) %all-to-all-start.2) | async-done | bytes 65568 | tf_op jit(solution)/shard_map/all_to_all | solution.py:354
  127.5 14.6 %sweep.7 = (f32[128,128]{1,0:T(8,128)}, f32[3,6,6,2,128]{4,3,2,1,0:T(2,128)S(1)}, f32[8,8,128]{2,1,0:T(8,128)S(1)}) custom-call(f32[10,10,2,128]{3,2,1,0:T(2,128)S(1)} %get-tuple-element.38.pos_ref, f32[6,6,2,128]{3,2,1,0:T(2,128)S(1)} %broadcast_in_dim.50.base_ref, f32[8,8,128]{2,1,0:T(8,128)S(1)} %slice_bitcast_fusion.code_ref, ...), custom_call_target="tpu_custom_call" | custom-call | flops 40000000 | bytes 400000 | tf_op jit(solution)/shard_map/sweep/pallas_call | solution.py:264
  142.1 8.6 %all-to-all-start.3 = ((f32[128,1,128]{2,1,0:T(1,128)}), f32[128,1,128]{2,1,0:T(1,128)S(1)}, u32[]{:S(2)}, u32[]{:S(2)}) async-start(f32[128,1,128]{2,1,0:T(1,128)} %bitcast.25), calls=%async_computation.3 | async-start | bytes 131072 | tf_op jit(solution)/shard_map/all_to_all | solution.py:354
  150.8 4.9 %collective-permute-start.17 = (f32[8,6,6,128]{3,2,1,0:T(8,128)S(1)}, f32[8,6,6,128]{3,2,1,0:T(8,128)S(1)}, u32[]{:S(2)}, u32[]{:S(2)}) collective-permute-start(f32[8,6,6,128]{3,2,1,0:T(8,128)S(1)} %bitcast_dynamic-update-slice_fusion), channel_id=1, source_target_pairs={{0,0},{1,1},{2,2},{3,3},{4,4},{5,5},{6,6},{7,7},{30,8},{31,9},{28,... | collective-permute-start | bytes 442376 | tf_op jit(solution)/shard_map/ppermute | solution.py:308
  155.7 0.4 all-to-all-done.3
  156.5 0.6 pad_maximum_fusion.16
  157.0 0.6 fusion.19
  157.7 3.3 %collective-permute-done.17 = f32[8,6,6,128]{3,2,1,0:T(8,128)S(1)} collective-permute-done((f32[8,6,6,128]{3,2,1,0:T(8,128)S(1)}, f32[8,6,6,128]{3,2,1,0:T(8,128)S(1)}, u32[]{:S(2)}, u32[]{:S(2)}) %collective-permute-start.17) | collective-permute-done | bytes 147488 | tf_op jit(solution)/shard_map/ppermute | solution.py:308
  161.0 1.3 fusion
  162.3 0.6 copy.44
  162.9 0.6 copy.45
  163.6 1.9 %fusion.8 = f32[6,6,128]{2,1,0:T(8,128)} fusion(f32[8,6,6,128]{3,2,1,0:T(8,128)S(1)} %collective-permute-done.17, s32[6,6,128]{2,1,0:T(8,128)S(1)} %copy-done.4, f32[]{:T(128)} %bitcast.26, f32[]{:T(128)} %bitcast.27), kind=kLoop, calls=%fused_computation.61 | loop fusion | flops 18432 | bytes 73736 | tf_op jit(solution)/shard_map/add | solution.py:369
  (68 shorter events, 2.2 us)
Async XLA Ops:
  0.6 0.8 copy-start.5
  1.5 0.7 copy-start.4
  2.3 7.7 %collective-permute-start = (f32[6,6,3,128]{3,1,0,2:T(8,128)S(1)}, f32[6,6,3,128]{3,1,0,2:T(8,128)S(1)}, u32[]{:S(2)}, u32[]{:S(2)}) collective-permute-start(f32[6,6,3,128]{3,1,0,2:T(8,128)S(1)} %pad_maximum_fusion.3), channel_id=1, source_target_pairs={{0,0},{1,1},{2,2},{3,3},{4,4},{5,5},{6,6},{7,7},{8,30},{9,31},{10,... | collective-permute-start | bytes 165896 | tf_op jit(solution)/shard_map/ppermute | solution.py:304
  10.0 4.5 %collective-permute-start.1 = (f32[1,2,6,3,128]{4,2,1,3,0:T(8,128)S(1)}, f32[1,2,6,3,128]{4,2,1,3,0:T(8,128)S(1)}, u32[]{:S(2)}, u32[]{:S(2)}) collective-permute-start(f32[1,2,6,3,128]{4,2,1,3,0:T(8,128)S(1)} %get-tuple-element.83), channel_id=1, source_target_pairs={{0,97},{1,96},{2,99},{3,98},{4,101},{5,100},{6,103},{7,102},{30,12... | collective-permute-start | bytes 55304 | tf_op jit(solution)/shard_map/ppermute | solution.py:323
  11.4 3.3 %collective-permute-start.2 = (f32[1,2,6,3,128]{4,2,1,3,0:T(8,128)S(1)}, f32[1,2,6,3,128]{4,2,1,3,0:T(8,128)S(1)}, u32[]{:S(2)}, u32[]{:S(2)}) collective-permute-start(f32[1,2,6,3,128]{4,2,1,3,0:T(8,128)S(1)} %get-tuple-element.84), channel_id=1, source_target_pairs={{0,17},{1,16},{2,19},{3,18},{4,21},{5,20},{6,23},{7,22},{30,15},{3... | collective-permute-start | bytes 55304 | tf_op jit(solution)/shard_map/ppermute | solution.py:324
  14.8 1.3 collective-permute-start.4
  14.9 3.3 %collective-permute-start.3 = (f32[1,10,2,3,128]{4,2,1,3,0:T(2,128)S(1)}, f32[1,10,2,3,128]{4,2,1,3,0:T(2,128)S(1)}, u32[]{:S(2)}, u32[]{:S(2)}) collective-permute-start(f32[1,10,2,3,128]{4,2,1,3,0:T(2,128)S(1)} %get-tuple-element.56), channel_id=1, source_target_pairs={{0,25},{1,2},{2,1},{3,4},{4,3},{5,6},{6,5},{7,30},{30,7},{31,28},{... | collective-permute-start | bytes 92168 | tf_op jit(solution)/shard_map/ppermute | solution.py:323
  18.4 0.9 copy-start
  33.9 4.7 %collective-permute-start.5 = (f32[3,2,6,2,128]{4,3,2,1,0:T(2,128)S(1)}, f32[3,2,6,2,128]{4,3,2,1,0:T(2,128)S(1)}, u32[]{:S(2)}, u32[]{:S(2)}) collective-permute-start(f32[3,2,6,2,128]{4,3,2,1,0:T(2,128)S(1)} %get-tuple-element.75), channel_id=1, source_target_pairs={{0,97},{1,96},{2,99},{3,98},{4,101},{5,100},{6,103},{7,102},{30,12... | collective-permute-start | bytes 110600 | tf_op jit(solution)/shard_map/ppermute | solution.py:323
  35.7 3.7 %collective-permute-start.6 = (f32[3,2,6,2,128]{4,3,2,1,0:T(2,128)S(1)}, f32[3,2,6,2,128]{4,3,2,1,0:T(2,128)S(1)}, u32[]{:S(2)}, u32[]{:S(2)}) collective-permute-start(f32[3,2,6,2,128]{4,3,2,1,0:T(2,128)S(1)} %get-tuple-element.76), channel_id=1, source_target_pairs={{0,17},{1,16},{2,19},{3,18},{4,21},{5,20},{6,23},{7,22},{30,15},{3... | collective-permute-start | bytes 110600 | tf_op jit(solution)/shard_map/ppermute | solution.py:324
  39.5 11.1 %collective-permute-start.7 = (f32[3,10,2,2,128]{4,3,2,1,0:T(2,128)S(1)}, f32[3,10,2,2,128]{4,3,2,1,0:T(2,128)S(1)}, u32[]{:S(2)}, u32[]{:S(2)}) collective-permute-start(f32[3,10,2,2,128]{4,3,2,1,0:T(2,128)S(1)} %get-tuple-element.63), channel_id=1, source_target_pairs={{0,25},{1,2},{2,1},{3,4},{4,3},{5,6},{6,5},{7,30},{30,7},{31,28},{... | collective-permute-start | bytes 184328 | tf_op jit(solution)/shard_map/ppermute | solution.py:323
  39.6 11.0 %collective-permute-start.8 = (f32[3,10,2,2,128]{4,3,2,1,0:T(2,128)S(1)}, f32[3,10,2,2,128]{4,3,2,1,0:T(2,128)S(1)}, u32[]{:S(2)}, u32[]{:S(2)}) collective-permute-start(f32[3,10,2,2,128]{4,3,2,1,0:T(2,128)S(1)} %get-tuple-element.64), channel_id=1, source_target_pairs={{0,1},{1,0},{2,3},{3,2},{4,5},{5,4},{6,7},{7,6},{30,31},{31,30},{2... | collective-permute-start | bytes 184328 | tf_op jit(solution)/shard_map/ppermute | solution.py:324
  41.0 15.1 %all-to-all-start = ((f32[128,1,128]{2,1,0:T(1,128)}), f32[128,1,128]{2,1,0:T(1,128)S(1)}, u32[]{:S(2)}, u32[]{:S(2)}) async-start(f32[128,1,128]{2,1,0:T(1,128)} %bitcast.8), calls=%async_computation | async-start | bytes 131072 | tf_op jit(solution)/shard_map/all_to_all | solution.py:354
  70.9 4.0 %collective-permute-start.10 = (f32[3,2,6,2,128]{4,3,2,1,0:T(2,128)S(1)}, f32[3,2,6,2,128]{4,3,2,1,0:T(2,128)S(1)}, u32[]{:S(2)}, u32[]{:S(2)}) collective-permute-start(f32[3,2,6,2,128]{4,3,2,1,0:T(2,128)S(1)} %get-tuple-element.74), channel_id=1, source_target_pairs={{0,17},{1,16},{2,19},{3,18},{4,21},{5,20},{6,23},{7,22},{30,15},{3... | collective-permute-start | bytes 110600 | tf_op jit(solution)/shard_map/ppermute | solution.py:324
  72.4 4.6 %collective-permute-start.9 = (f32[3,2,6,2,128]{4,3,2,1,0:T(2,128)S(1)}, f32[3,2,6,2,128]{4,3,2,1,0:T(2,128)S(1)}, u32[]{:S(2)}, u32[]{:S(2)}) collective-permute-start(f32[3,2,6,2,128]{4,3,2,1,0:T(2,128)S(1)} %get-tuple-element.73), channel_id=1, source_target_pairs={{0,97},{1,96},{2,99},{3,98},{4,101},{5,100},{6,103},{7,102},{30,12... | collective-permute-start | bytes 110600 | tf_op jit(solution)/shard_map/ppermute | solution.py:323
  77.1 8.9 %collective-permute-start.11 = (f32[3,10,2,2,128]{4,3,2,1,0:T(2,128)S(1)}, f32[3,10,2,2,128]{4,3,2,1,0:T(2,128)S(1)}, u32[]{:S(2)}, u32[]{:S(2)}) collective-permute-start(f32[3,10,2,2,128]{4,3,2,1,0:T(2,128)S(1)} %get-tuple-element.61), channel_id=1, source_target_pairs={{0,25},{1,2},{2,1},{3,4},{4,3},{5,6},{6,5},{7,30},{30,7},{31,28},{... | collective-permute-start | bytes 184328 | tf_op jit(solution)/shard_map/ppermute | solution.py:323
  77.2 8.9 %collective-permute-start.12 = (f32[3,10,2,2,128]{4,3,2,1,0:T(2,128)S(1)}, f32[3,10,2,2,128]{4,3,2,1,0:T(2,128)S(1)}, u32[]{:S(2)}, u32[]{:S(2)}) collective-permute-start(f32[3,10,2,2,128]{4,3,2,1,0:T(2,128)S(1)} %get-tuple-element.62), channel_id=1, source_target_pairs={{0,1},{1,0},{2,3},{3,2},{4,5},{5,4},{6,7},{7,6},{30,31},{31,30},{2... | collective-permute-start | bytes 184328 | tf_op jit(solution)/shard_map/ppermute | solution.py:324
  79.4 12.2 %all-to-all-start.1 = ((f32[128,1,128]{2,1,0:T(1,128)}), f32[128,1,128]{2,1,0:T(1,128)S(1)}, u32[]{:S(2)}, u32[]{:S(2)}) async-start(f32[128,1,128]{2,1,0:T(1,128)} %bitcast.11), calls=%async_computation.1 | async-start | bytes 131072 | tf_op jit(solution)/shard_map/all_to_all | solution.py:354
  106.4 5.2 %collective-permute-start.13 = (f32[3,2,6,2,128]{4,3,2,1,0:T(2,128)S(1)}, f32[3,2,6,2,128]{4,3,2,1,0:T(2,128)S(1)}, u32[]{:S(2)}, u32[]{:S(2)}) collective-permute-start(f32[3,2,6,2,128]{4,3,2,1,0:T(2,128)S(1)} %get-tuple-element.71), channel_id=1, source_target_pairs={{0,97},{1,96},{2,99},{3,98},{4,101},{5,100},{6,103},{7,102},{30,12... | collective-permute-start | bytes 110600 | tf_op jit(solution)/shard_map/ppermute | solution.py:323
  108.8 3.4 %collective-permute-start.14 = (f32[3,2,6,2,128]{4,3,2,1,0:T(2,128)S(1)}, f32[3,2,6,2,128]{4,3,2,1,0:T(2,128)S(1)}, u32[]{:S(2)}, u32[]{:S(2)}) collective-permute-start(f32[3,2,6,2,128]{4,3,2,1,0:T(2,128)S(1)} %get-tuple-element.72), channel_id=1, source_target_pairs={{0,17},{1,16},{2,19},{3,18},{4,21},{5,20},{6,23},{7,22},{30,15},{3... | collective-permute-start | bytes 110600 | tf_op jit(solution)/shard_map/ppermute | solution.py:324
  112.3 9.5 %collective-permute-start.15 = (f32[3,10,2,2,128]{4,3,2,1,0:T(2,128)S(1)}, f32[3,10,2,2,128]{4,3,2,1,0:T(2,128)S(1)}, u32[]{:S(2)}, u32[]{:S(2)}) collective-permute-start(f32[3,10,2,2,128]{4,3,2,1,0:T(2,128)S(1)} %get-tuple-element.59), channel_id=1, source_target_pairs={{0,25},{1,2},{2,1},{3,4},{4,3},{5,6},{6,5},{7,30},{30,7},{31,28},{... | collective-permute-start | bytes 184328 | tf_op jit(solution)/shard_map/ppermute | solution.py:323
  112.3 9.4 %collective-permute-start.16 = (f32[3,10,2,2,128]{4,3,2,1,0:T(2,128)S(1)}, f32[3,10,2,2,128]{4,3,2,1,0:T(2,128)S(1)}, u32[]{:S(2)}, u32[]{:S(2)}) collective-permute-start(f32[3,10,2,2,128]{4,3,2,1,0:T(2,128)S(1)} %get-tuple-element.60), channel_id=1, source_target_pairs={{0,1},{1,0},{2,3},{3,2},{4,5},{5,4},{6,7},{7,6},{30,31},{31,30},{2... | collective-permute-start | bytes 184328 | tf_op jit(solution)/shard_map/ppermute | solution.py:324
  115.0 12.3 %all-to-all-start.2 = ((f32[128,1,128]{2,1,0:T(1,128)}), f32[128,1,128]{2,1,0:T(1,128)S(1)}, u32[]{:S(2)}, u32[]{:S(2)}) async-start(f32[128,1,128]{2,1,0:T(1,128)} %bitcast.14), calls=%async_computation.2 | async-start | bytes 131072 | tf_op jit(solution)/shard_map/all_to_all | solution.py:354
  142.1 14.1 %all-to-all-start.3 = ((f32[128,1,128]{2,1,0:T(1,128)}), f32[128,1,128]{2,1,0:T(1,128)S(1)}, u32[]{:S(2)}, u32[]{:S(2)}) async-start(f32[128,1,128]{2,1,0:T(1,128)} %bitcast.25), calls=%async_computation.3 | async-start | bytes 131072 | tf_op jit(solution)/shard_map/all_to_all | solution.py:354
  150.8 10.2 %copy-start.3 = (f32[2,6,6,128]{3,0,2,1:T(2,128)S(1)}, f32[2,6,6,128]{3,0,2,1:T(2,128)}, u32[]{:S(2)}) copy-start(f32[2,6,6,128]{3,0,2,1:T(2,128)} %param.7) | copy-start | bytes 110596
  150.8 10.2 %copy-start.1 = (f32[2,6,6,128]{3,0,2,1:T(2,128)S(1)}, f32[2,6,6,128]{3,0,2,1:T(2,128)}, u32[]{:S(2)}) copy-start(f32[2,6,6,128]{3,0,2,1:T(2,128)} %param.6) | copy-start | bytes 110596
  150.8 10.2 %copy-start.2 = (f32[2,6,6,128]{3,0,2,1:T(2,128)S(1)}, f32[2,6,6,128]{3,0,2,1:T(2,128)}, u32[]{:S(2)}) copy-start(f32[2,6,6,128]{3,0,2,1:T(2,128)} %param.8) | copy-start | bytes 110596
  150.8 10.1 %collective-permute-start.17 = (f32[8,6,6,128]{3,2,1,0:T(8,128)S(1)}, f32[8,6,6,128]{3,2,1,0:T(8,128)S(1)}, u32[]{:S(2)}, u32[]{:S(2)}) collective-permute-start(f32[8,6,6,128]{3,2,1,0:T(8,128)S(1)} %bitcast_dynamic-update-slice_fusion), channel_id=1, source_target_pairs={{0,0},{1,1},{2,2},{3,3},{4,4},{5,5},{6,6},{7,7},{30,8},{31,9},{28,... | collective-permute-start | bytes 442376 | tf_op jit(solution)/shard_map/ppermute | solution.py:308

commit v4 on v3

--- a/solution.py
+++ b/solution.py
@@ -106,6 +106,7 @@
     return acc.sum(axis=0, keepdims=True)
 
 
+OWN, TB, LR, FP = 9, 8, 6, 6
 TIME_STEP = 0.05
 KERNEL_NORM = 4.0 / (3.141592653589793 * 64.0)
 SENTINEL = 1.0e30
@@ -153,29 +154,31 @@
     fill_pairs(ls, lt, 0, 5, 8, 3, 0, 1, 1)
     fill_pairs(ls, lt, 40, 3, 10, 7, 0, 0, 0)
     fill_pairs(ls, lt, 70, 8, 3, 0, 7, 1, 0)
-    def own(b, carry):
-        for a in range(3):
-            row = density_pair(rs, lt, masks_ref, (a + 2, b + 2), (a + 5, b + 2), (a + 1) * 8 + b + 1, 8, squares, b * 3 + a)
+    def own(step, carry):
+        for u in range(OWN):
+            n = step * OWN + u
+            a, b = (u % 3, step * (OWN // 3) + u // 3) if OWN % 3 == 0 else (n % 3, n // 3)
+            row = density_pair(rs, lt, masks_ref, (a + 2, b + 2), (a + 5, b + 2), (a + 1) * 8 + b + 1, 8, squares, n)
             dn[a + 1, pl.ds(b + 1, 1), :] = row[:, :128]
             dn[a + 4, pl.ds(b + 1, 1), :] = row[:, 128:]
         return carry
-    lax.fori_loop(0, 6, own, 0)
+    lax.fori_loop(0, 18 // OWN, own, 0)
     def top_bottom(h, carry):
-        for u in range(2):
-            c = h * 2 + u
+        for u in range(TB):
+            c = h * TB + u
             row = density_pair(rs, lt, masks_ref, (1, c + 1), (8, c + 1), 50 + c + 1, 10)
             dn[0, pl.ds(c, 1), :] = row[:, :128]
             dn[7, pl.ds(c, 1), :] = row[:, 128:]
         return carry
-    lax.fori_loop(0, 4, top_bottom, 0)
+    lax.fori_loop(0, 8 // TB, top_bottom, 0)
     def left_right(h, carry):
-        for u in range(2):
-            a = h * 2 + u + 1
+        for u in range(LR):
+            a = h * LR + u + 1
             row = density_pair(rs, lt, masks_ref, (a + 1, 1), (a + 1, 8), 70 + a * 3 + 1, 3)
             dn[a, pl.ds(0, 1), :] = row[:, :128]
             dn[a, pl.ds(7, 1), :] = row[:, 128:]
         return carry
-    lax.fori_loop(0, 3, left_right, 0)
+    lax.fori_loop(0, 6 // LR, left_right, 0)
     bounds_of(dn[...], own_ref[...], bnd_ref)
     code = code_ref[...]
     live = code > 0.0
@@ -200,18 +203,18 @@
     lax.fori_loop(0, 5, moments, 0)
     row = row_iota()
     def forces(step, carry):
-        accs = [jnp.zeros((48, 256), F32) for _ in range(2)]
-        work = [((2 * step + m) % 3, (2 * step + m) // 3) for m in range(2)]
+        accs = [jnp.zeros((48, 256), F32) for _ in range(FP)]
+        work = [((FP * step + m) % 3, (FP * step + m) // 3) for m in range(FP)]
         for k, (ox, oy) in enumerate(OFFS):
-            for m in range(2):
+            for m in range(FP):
                 a, bcol = work[m]
                 p = (a + 1 + ox) * 8 + bcol + 1 + oy
-                w2 = squares[(2 * step + m) * 9 + k]
+                w2 = squares[(FP * step + m) * 9 + k]
                 hi = w2.astype(BF16)
                 lo = (w2 - hi.astype(F32)).astype(BF16)
                 g = jnp.concatenate([gt[p, 0:16], gt[p, 32 + 16 * ox:48 + 16 * ox], gt[p, 80 + 16 * oy:96 + 16 * oy]], axis=0)
                 accs[m] = accs[m] + jnp.dot(jnp.concatenate([g, g], axis=1), jnp.concatenate([hi, lo], axis=0), preferred_element_type=F32)
-        for m in range(2):
+        for m in range(FP):
             a, bcol = work[m]
             acc = accs[m]
             for h in range(2):
@@ -237,7 +240,7 @@
                     s_ref[t, aa, bcol, 0:1, :] = out[t + 1:t + 2]
                     s_ref[t, aa, bcol, 1:2, :] = out[t + 5:t + 6]
         return carry
-    lax.fori_loop(0, 9, forces, 0)
+    lax.fori_loop(0, 18 // FP, forces, 0)
 
 
 def kc_kernel(seen_ref, s_ref, code_ref, p_ref, q_ref, pos_ref, pout_ref, row_ref):
@@ -330,7 +333,8 @@
 def padded(block):
     odd_x = lax.axis_index("gx_0") + lax.axis_index("gx_1") + lax.axis_index("gy_0")
     odd_y = odd_x + lax.axis_index("gy_2")
-    return swapped(swapped(block, odd_x % 2 == 0, 0), odd_y % 2 == 0, 1)
+    block = swapped(block, odd_x % 2 == 0, 0)
+    return swapped(block, odd_y % 2 == 0, 1)
 
 
 def local(position, velocity, other_accel, phase_ids, counts):

time: 168 us -> 161 us (0.958)
  Pallas kernels: 59 us -> 51.7 us
    pallas_call x4, Pallas kernels: 58.5 us -> 51.2 us  [call_kdf(): pl.pallas_call(kdf_kernel, out_shape=(shaped((128, 128)), shaped((3, 6, 6...]
where the time goes in v4:
time: 161 us; the launch traced here: 158 us
  starting transfers between devices  57.4 us (36%)
  Pallas kernels  51.7 us (32%)
  waiting for transfers between devices  38.2 us (24%)
  other arithmetic  6.2 us (4%)
  local copies, waits for them, and re-layouts  3.59 us (2%)
    pallas_call x4, Pallas kernels, call_kdf(): pl.pallas_call(kdf_kernel, out_shape=(shaped((128, 128)), shaped((3, 6, 6...  51.2 us
    all_to_all x4, starting transfers between devices, local(): seen = lax.all_to_all(bounds, ALL, 0, 0, tiled=True)  31.6 us
    all_to_all x4, waiting for transfers between devices, local(): seen = lax.all_to_all(bounds, ALL, 0, 0, tiled=True)  16.3 us
    ppermute x8, waiting for transfers between devices, swapped(): far = lax.ppermute(jnp.where(even, first, last), ALL, partners(dim, False))  12.6 us
    ppermute x8, starting transfers between devices, swapped(): near = lax.ppermute(jnp.where(even, last, first), ALL, partners(dim, True))  8.19 us
    ppermute x8, starting transfers between devices, swapped(): far = lax.ppermute(jnp.where(even, first, last), ALL, partners(dim, False))  7.49 us
    ppermute x1, starting transfers between devices, to_work(): lax.ppermute(block, ALL, [(home_of(gx, gy), work_of(gx, gy)) for gx, gy i...  5.2 us
    ppermute x1, starting transfers between devices, to_home(): lax.ppermute(block, ALL, [(work_of(gx, gy), home_of(gx, gy)) for gx, gy i...  4.91 us
  transfers between devices with their start and end apart: 22, of which 16 were waited for; matrix products, arithmetic and copies ran while one was open for 1% of the time, Pallas kernels for 0%

profile of v4, /device:TPU:103, one launch (start us, length us, event | category | flops | bytes accessed | tf_op | source)
XLA Modules:
  0.0 158.2 jit_solution(11517091290428345707)
XLA Ops:
  0.6 0.8 fusion.1
  1.6 0.7 copy-done.4
  2.3 5.2 %collective-permute-start = (f32[6,6,3,128]{3,1,0,2:T(8,128)S(1)}, f32[6,6,3,128]{3,1,0,2:T(8,128)S(1)}, u32[]{:S(2)}, u32[]{:S(2)}) collective-permute-start(f32[6,6,3,128]{3,1,0,2:T(8,128)S(1)} %pad_maximum_fusion.3), channel_id=1, source_target_pairs={{0,0},{1,1},{2,2},{3,3},{4,4},{5,5},{6,6},{7,7},{8,30},{9,31},{10,... | collective-permute-start | bytes 165896 | tf_op jit(solution)/shard_map/ppermute | solution.py:307
  7.5 2.4 %collective-permute-done = f32[6,6,3,128]{3,1,0,2:T(8,128)S(1)} collective-permute-done((f32[6,6,3,128]{3,1,0,2:T(8,128)S(1)}, f32[6,6,3,128]{3,1,0,2:T(8,128)S(1)}, u32[]{:S(2)}, u32[]{:S(2)}) %collective-permute-start) | collective-permute-done | bytes 55328 | tf_op jit(solution)/shard_map/ppermute | solution.py:307
  10.0 1.5 collective-permute-start.1
  11.4 0.4 collective-permute-start.2
  11.8 2.6 %collective-permute-done.1 = f32[1,2,6,3,128]{4,2,1,3,0:T(8,128)S(1)} collective-permute-done((f32[1,2,6,3,128]{4,2,1,3,0:T(8,128)S(1)}, f32[1,2,6,3,128]{4,2,1,3,0:T(8,128)S(1)}, u32[]{:S(2)}, u32[]{:S(2)}) %collective-permute-start.1) | collective-permute-done | bytes 18464 | tf_op jit(solution)/shard_map/ppermute | solution.py:326
  14.4 0.2 collective-permute-done.2
  14.8 0.2 collective-permute-start.4
  14.9 0.4 collective-permute-start.3
  15.4 0.7 collective-permute-done.4
  16.0 2.2 %collective-permute-done.3 = f32[1,10,2,3,128]{4,2,1,3,0:T(2,128)S(1)} collective-permute-done((f32[1,10,2,3,128]{4,2,1,3,0:T(2,128)S(1)}, f32[1,10,2,3,128]{4,2,1,3,0:T(2,128)S(1)}, u32[]{:S(2)}, u32[]{:S(2)}) %collective-permute-start.3) | collective-permute-done | bytes 30752 | tf_op jit(solution)/shard_map/ppermute | solution.py:326
  18.5 0.8 copy-done
  19.3 12.8 %sweep.4 = (f32[128,128]{1,0:T(8,128)}, f32[3,6,6,2,128]{4,3,2,1,0:T(2,128)S(1)}, f32[8,8,128]{2,1,0:T(8,128)S(1)}) custom-call(f32[10,10,2,128]{3,2,1,0:T(2,128)S(1)} %copy.29.pos_ref, f32[6,6,2,128]{3,2,1,0:T(2,128)S(1)} %copy.30.base_ref, f32[8,8,128]{2,1,0:T(8,128)S(1)} %slice_bitcast_fusion.code_ref, f32[8,8,128]{2,1,0:T(8,128)S(1)} %pad.4.own_ref, ...), custom_call_target="tpu_custom_call" | custom-call | flops 40000000 | bytes 400000 | tf_op jit(solution)/shard_map/sweep/pallas_call | solution.py:267
  32.1 1.8 %collective-permute-start.5 = (f32[3,2,6,2,128]{4,3,2,1,0:T(2,128)S(1)}, f32[3,2,6,2,128]{4,3,2,1,0:T(2,128)S(1)}, u32[]{:S(2)}, u32[]{:S(2)}) collective-permute-start(f32[3,2,6,2,128]{4,3,2,1,0:T(2,128)S(1)} %get-tuple-element.75), channel_id=1, source_target_pairs={{0,97},{1,96},{2,99},{3,98},{4,101},{5,100},{6,103},{7,102},{30,12... | collective-permute-start | bytes 110600 | tf_op jit(solution)/shard_map/ppermute | solution.py:326
  33.9 2.9 %collective-permute-done.5 = f32[3,2,6,2,128]{4,3,2,1,0:T(2,128)S(1)} collective-permute-done((f32[3,2,6,2,128]{4,3,2,1,0:T(2,128)S(1)}, f32[3,2,6,2,128]{4,3,2,1,0:T(2,128)S(1)}, u32[]{:S(2)}, u32[]{:S(2)}) %collective-permute-start.5) | collective-permute-done | bytes 36896 | tf_op jit(solution)/shard_map/ppermute | solution.py:326
  36.8 0.8 collective-permute-done.6
  37.8 1.4 collective-permute-start.8
  39.2 9.6 %all-to-all-start = ((f32[128,1,128]{2,1,0:T(1,128)}), f32[128,1,128]{2,1,0:T(1,128)S(1)}, u32[]{:S(2)}, u32[]{:S(2)}) async-start(f32[128,1,128]{2,1,0:T(1,128)} %bitcast.8), calls=%async_computation | async-start | bytes 131072 | tf_op jit(solution)/shard_map/all_to_all | solution.py:358
  49.0 5.3 %all-to-all-done = f32[128,1,128]{2,1,0:T(1,128)S(1)} async-done(((f32[128,1,128]{2,1,0:T(1,128)}), f32[128,1,128]{2,1,0:T(1,128)S(1)}, u32[]{:S(2)}, u32[]{:S(2)}) %all-to-all-start) | async-done | bytes 65568 | tf_op jit(solution)/shard_map/all_to_all | solution.py:358
  54.3 0.2 combine.3
  54.5 12.8 %sweep.5 = (f32[128,128]{1,0:T(8,128)}, f32[3,6,6,2,128]{4,3,2,1,0:T(2,128)S(1)}, f32[8,8,128]{2,1,0:T(8,128)S(1)}) custom-call(f32[10,10,2,128]{3,2,1,0:T(2,128)S(1)} %get-tuple-element.28.pos_ref, f32[6,6,2,128]{3,2,1,0:T(2,128)S(1)} %copy.30.base_ref, f32[8,8,128]{2,1,0:T(8,128)S(1)} %slice_bitcast_fusion.code_ref, f32[8,8,128]{2,1,0:T(8,128)S(1)} %pad.4.own_ref, ...), custom_call_target="tpu_custom_call" | custom-call | flops 40000000 | bytes 400000 | tf_op jit(solution)/shard_map/sweep/pallas_call | solution.py:267
  67.3 1.5 collective-permute-start.10
  68.8 1.2 collective-permute-start.9
  70.0 1.3 collective-permute-done.10
  71.3 2.1 %collective-permute-done.9 = f32[3,2,6,2,128]{4,3,2,1,0:T(2,128)S(1)} collective-permute-done((f32[3,2,6,2,128]{4,3,2,1,0:T(2,128)S(1)}, f32[3,2,6,2,128]{4,3,2,1,0:T(2,128)S(1)}, u32[]{:S(2)}, u32[]{:S(2)}) %collective-permute-start.9) | collective-permute-done | bytes 36896 | tf_op jit(solution)/shard_map/ppermute | solution.py:326
  73.6 2.2 %collective-permute-start.12 = (f32[3,10,2,2,128]{4,3,2,1,0:T(2,128)S(1)}, f32[3,10,2,2,128]{4,3,2,1,0:T(2,128)S(1)}, u32[]{:S(2)}, u32[]{:S(2)}) collective-permute-start(f32[3,10,2,2,128]{4,3,2,1,0:T(2,128)S(1)} %get-tuple-element.62), channel_id=1, source_target_pairs={{0,1},{1,0},{2,3},{3,2},{4,5},{5,4},{6,7},{7,6},{30,31},{31,30},{2... | collective-permute-start | bytes 184328 | tf_op jit(solution)/shard_map/ppermute | solution.py:327
  75.8 6.7 %all-to-all-start.1 = ((f32[128,1,128]{2,1,0:T(1,128)}), f32[128,1,128]{2,1,0:T(1,128)S(1)}, u32[]{:S(2)}, u32[]{:S(2)}) async-start(f32[128,1,128]{2,1,0:T(1,128)} %bitcast.11), calls=%async_computation.1 | async-start | bytes 131072 | tf_op jit(solution)/shard_map/all_to_all | solution.py:358
  82.7 5.3 %all-to-all-done.1 = f32[128,1,128]{2,1,0:T(1,128)S(1)} async-done(((f32[128,1,128]{2,1,0:T(1,128)}), f32[128,1,128]{2,1,0:T(1,128)S(1)}, u32[]{:S(2)}, u32[]{:S(2)}) %all-to-all-start.1) | async-done | bytes 65568 | tf_op jit(solution)/shard_map/all_to_all | solution.py:358
  88.0 0.2 combine.4
  88.1 12.8 %sweep.6 = (f32[128,128]{1,0:T(8,128)}, f32[3,6,6,2,128]{4,3,2,1,0:T(2,128)S(1)}, f32[8,8,128]{2,1,0:T(8,128)S(1)}) custom-call(f32[10,10,2,128]{3,2,1,0:T(2,128)S(1)} %get-tuple-element.33.pos_ref, f32[6,6,2,128]{3,2,1,0:T(2,128)S(1)} %copy.30.base_ref, f32[8,8,128]{2,1,0:T(8,128)S(1)} %slice_bitcast_fusion.code_ref, f32[8,8,128]{2,1,0:T(8,128)S(1)} %pad.4.own_ref, ...), custom_call_target="tpu_custom_call" | custom-call | flops 40000000 | bytes 400000 | tf_op jit(solution)/shard_map/sweep/pallas_call | solution.py:267
  101.0 2.4 %collective-permute-start.13 = (f32[3,2,6,2,128]{4,3,2,1,0:T(2,128)S(1)}, f32[3,2,6,2,128]{4,3,2,1,0:T(2,128)S(1)}, u32[]{:S(2)}, u32[]{:S(2)}) collective-permute-start(f32[3,2,6,2,128]{4,3,2,1,0:T(2,128)S(1)} %get-tuple-element.71), channel_id=1, source_target_pairs={{0,97},{1,96},{2,99},{3,98},{4,101},{5,100},{6,103},{7,102},{30,12... | collective-permute-start | bytes 110600 | tf_op jit(solution)/shard_map/ppermute | solution.py:326
  103.4 2.8 %collective-permute-done.13 = f32[3,2,6,2,128]{4,3,2,1,0:T(2,128)S(1)} collective-permute-done((f32[3,2,6,2,128]{4,3,2,1,0:T(2,128)S(1)}, f32[3,2,6,2,128]{4,3,2,1,0:T(2,128)S(1)}, u32[]{:S(2)}, u32[]{:S(2)}) %collective-permute-start.13) | collective-permute-done | bytes 36896 | tf_op jit(solution)/shard_map/ppermute | solution.py:326
  106.2 0.6 collective-permute-done.14
  106.9 2.5 %collective-permute-start.16 = (f32[3,10,2,2,128]{4,3,2,1,0:T(2,128)S(1)}, f32[3,10,2,2,128]{4,3,2,1,0:T(2,128)S(1)}, u32[]{:S(2)}, u32[]{:S(2)}) collective-permute-start(f32[3,10,2,2,128]{4,3,2,1,0:T(2,128)S(1)} %get-tuple-element.60), channel_id=1, source_target_pairs={{0,1},{1,0},{2,3},{3,2},{4,5},{5,4},{6,7},{7,6},{30,31},{31,30},{2... | collective-permute-start | bytes 184328 | tf_op jit(solution)/shard_map/ppermute | solution.py:327
  109.6 6.8 %all-to-all-start.2 = ((f32[128,1,128]{2,1,0:T(1,128)}), f32[128,1,128]{2,1,0:T(1,128)S(1)}, u32[]{:S(2)}, u32[]{:S(2)}) async-start(f32[128,1,128]{2,1,0:T(1,128)} %bitcast.14), calls=%async_computation.2 | async-start | bytes 131072 | tf_op jit(solution)/shard_map/all_to_all | solution.py:358
  116.6 5.3 %all-to-all-done.2 = f32[128,1,128]{2,1,0:T(1,128)S(1)} async-done(((f32[128,1,128]{2,1,0:T(1,128)}), f32[128,1,128]{2,1,0:T(1,128)S(1)}, u32[]{:S(2)}, u32[]{:S(2)}) %all-to-all-start.2) | async-done | bytes 65568 | tf_op jit(solution)/shard_map/all_to_all | solution.py:358
  122.0 12.8 %sweep.7 = (f32[128,128]{1,0:T(8,128)}, f32[3,6,6,2,128]{4,3,2,1,0:T(2,128)S(1)}, f32[8,8,128]{2,1,0:T(8,128)S(1)}) custom-call(f32[10,10,2,128]{3,2,1,0:T(2,128)S(1)} %get-tuple-element.38.pos_ref, f32[6,6,2,128]{3,2,1,0:T(2,128)S(1)} %broadcast_in_dim.50.base_ref, f32[8,8,128]{2,1,0:T(8,128)S(1)} %slice_bitcast_fusion.code_ref, ...), custom_call_target="tpu_custom_call" | custom-call | flops 40000000 | bytes 400000 | tf_op jit(solution)/shard_map/sweep/pallas_call | solution.py:267
  134.8 8.6 %all-to-all-start.3 = ((f32[128,1,128]{2,1,0:T(1,128)}), f32[128,1,128]{2,1,0:T(1,128)S(1)}, u32[]{:S(2)}, u32[]{:S(2)}) async-start(f32[128,1,128]{2,1,0:T(1,128)} %bitcast.25), calls=%async_computation.3 | async-start | bytes 131072 | tf_op jit(solution)/shard_map/all_to_all | solution.py:358
  143.6 4.9 %collective-permute-start.17 = (f32[8,6,6,128]{3,2,1,0:T(8,128)S(1)}, f32[8,6,6,128]{3,2,1,0:T(8,128)S(1)}, u32[]{:S(2)}, u32[]{:S(2)}) collective-permute-start(f32[8,6,6,128]{3,2,1,0:T(8,128)S(1)} %bitcast_dynamic-update-slice_fusion), channel_id=1, source_target_pairs={{0,0},{1,1},{2,2},{3,3},{4,4},{5,5},{6,6},{7,7},{30,8},{31,9},{28,... | collective-permute-start | bytes 442376 | tf_op jit(solution)/shard_map/ppermute | solution.py:311
  148.5 0.4 all-to-all-done.3
  149.2 0.6 pad_maximum_fusion.16
  149.8 0.6 fusion.19
  150.5 3.3 %collective-permute-done.17 = f32[8,6,6,128]{3,2,1,0:T(8,128)S(1)} collective-permute-done((f32[8,6,6,128]{3,2,1,0:T(8,128)S(1)}, f32[8,6,6,128]{3,2,1,0:T(8,128)S(1)}, u32[]{:S(2)}, u32[]{:S(2)}) %collective-permute-start.17) | collective-permute-done | bytes 147488 | tf_op jit(solution)/shard_map/ppermute | solution.py:311
  153.7 1.3 fusion
  155.1 0.6 copy.44
  155.7 0.6 copy.45
  156.3 1.9 %fusion.8 = f32[6,6,128]{2,1,0:T(8,128)} fusion(f32[8,6,6,128]{3,2,1,0:T(8,128)S(1)} %collective-permute-done.17, s32[6,6,128]{2,1,0:T(8,128)S(1)} %copy-done.4, f32[]{:T(128)} %bitcast.26, f32[]{:T(128)} %bitcast.27), kind=kLoop, calls=%fused_computation.61 | loop fusion | flops 18432 | bytes 73736 | tf_op jit(solution)/shard_map/add | solution.py:373
  (68 shorter events, 2.2 us)
Async XLA Ops:
  0.6 0.8 copy-start.5
  1.5 0.7 copy-start.4
  2.3 7.7 %collective-permute-start = (f32[6,6,3,128]{3,1,0,2:T(8,128)S(1)}, f32[6,6,3,128]{3,1,0,2:T(8,128)S(1)}, u32[]{:S(2)}, u32[]{:S(2)}) collective-permute-start(f32[6,6,3,128]{3,1,0,2:T(8,128)S(1)} %pad_maximum_fusion.3), channel_id=1, source_target_pairs={{0,0},{1,1},{2,2},{3,3},{4,4},{5,5},{6,6},{7,7},{8,30},{9,31},{10,... | collective-permute-start | bytes 165896 | tf_op jit(solution)/shard_map/ppermute | solution.py:307
  10.0 4.5 %collective-permute-start.1 = (f32[1,2,6,3,128]{4,2,1,3,0:T(8,128)S(1)}, f32[1,2,6,3,128]{4,2,1,3,0:T(8,128)S(1)}, u32[]{:S(2)}, u32[]{:S(2)}) collective-permute-start(f32[1,2,6,3,128]{4,2,1,3,0:T(8,128)S(1)} %get-tuple-element.83), channel_id=1, source_target_pairs={{0,97},{1,96},{2,99},{3,98},{4,101},{5,100},{6,103},{7,102},{30,12... | collective-permute-start | bytes 55304 | tf_op jit(solution)/shard_map/ppermute | solution.py:326
  11.4 3.3 %collective-permute-start.2 = (f32[1,2,6,3,128]{4,2,1,3,0:T(8,128)S(1)}, f32[1,2,6,3,128]{4,2,1,3,0:T(8,128)S(1)}, u32[]{:S(2)}, u32[]{:S(2)}) collective-permute-start(f32[1,2,6,3,128]{4,2,1,3,0:T(8,128)S(1)} %get-tuple-element.84), channel_id=1, source_target_pairs={{0,17},{1,16},{2,19},{3,18},{4,21},{5,20},{6,23},{7,22},{30,15},{3... | collective-permute-start | bytes 55304 | tf_op jit(solution)/shard_map/ppermute | solution.py:327
  14.8 1.3 collective-permute-start.4
  14.9 3.3 %collective-permute-start.3 = (f32[1,10,2,3,128]{4,2,1,3,0:T(2,128)S(1)}, f32[1,10,2,3,128]{4,2,1,3,0:T(2,128)S(1)}, u32[]{:S(2)}, u32[]{:S(2)}) collective-permute-start(f32[1,10,2,3,128]{4,2,1,3,0:T(2,128)S(1)} %get-tuple-element.56), channel_id=1, source_target_pairs={{0,25},{1,2},{2,1},{3,4},{4,3},{5,6},{6,5},{7,30},{30,7},{31,28},{... | collective-permute-start | bytes 92168 | tf_op jit(solution)/shard_map/ppermute | solution.py:326
  18.4 0.9 copy-start
  32.1 4.7 %collective-permute-start.5 = (f32[3,2,6,2,128]{4,3,2,1,0:T(2,128)S(1)}, f32[3,2,6,2,128]{4,3,2,1,0:T(2,128)S(1)}, u32[]{:S(2)}, u32[]{:S(2)}) collective-permute-start(f32[3,2,6,2,128]{4,3,2,1,0:T(2,128)S(1)} %get-tuple-element.75), channel_id=1, source_target_pairs={{0,97},{1,96},{2,99},{3,98},{4,101},{5,100},{6,103},{7,102},{30,12... | collective-permute-start | bytes 110600 | tf_op jit(solution)/shard_map/ppermute | solution.py:326
  33.9 3.7 %collective-permute-start.6 = (f32[3,2,6,2,128]{4,3,2,1,0:T(2,128)S(1)}, f32[3,2,6,2,128]{4,3,2,1,0:T(2,128)S(1)}, u32[]{:S(2)}, u32[]{:S(2)}) collective-permute-start(f32[3,2,6,2,128]{4,3,2,1,0:T(2,128)S(1)} %get-tuple-element.76), channel_id=1, source_target_pairs={{0,17},{1,16},{2,19},{3,18},{4,21},{5,20},{6,23},{7,22},{30,15},{3... | collective-permute-start | bytes 110600 | tf_op jit(solution)/shard_map/ppermute | solution.py:327
  37.7 11.1 %collective-permute-start.7 = (f32[3,10,2,2,128]{4,3,2,1,0:T(2,128)S(1)}, f32[3,10,2,2,128]{4,3,2,1,0:T(2,128)S(1)}, u32[]{:S(2)}, u32[]{:S(2)}) collective-permute-start(f32[3,10,2,2,128]{4,3,2,1,0:T(2,128)S(1)} %get-tuple-element.63), channel_id=1, source_target_pairs={{0,25},{1,2},{2,1},{3,4},{4,3},{5,6},{6,5},{7,30},{30,7},{31,28},{... | collective-permute-start | bytes 184328 | tf_op jit(solution)/shard_map/ppermute | solution.py:326
  37.8 11.1 %collective-permute-start.8 = (f32[3,10,2,2,128]{4,3,2,1,0:T(2,128)S(1)}, f32[3,10,2,2,128]{4,3,2,1,0:T(2,128)S(1)}, u32[]{:S(2)}, u32[]{:S(2)}) collective-permute-start(f32[3,10,2,2,128]{4,3,2,1,0:T(2,128)S(1)} %get-tuple-element.64), channel_id=1, source_target_pairs={{0,1},{1,0},{2,3},{3,2},{4,5},{5,4},{6,7},{7,6},{30,31},{31,30},{2... | collective-permute-start | bytes 184328 | tf_op jit(solution)/shard_map/ppermute | solution.py:327
  39.2 15.2 %all-to-all-start = ((f32[128,1,128]{2,1,0:T(1,128)}), f32[128,1,128]{2,1,0:T(1,128)S(1)}, u32[]{:S(2)}, u32[]{:S(2)}) async-start(f32[128,1,128]{2,1,0:T(1,128)} %bitcast.8), calls=%async_computation | async-start | bytes 131072 | tf_op jit(solution)/shard_map/all_to_all | solution.py:358
  67.3 4.0 %collective-permute-start.10 = (f32[3,2,6,2,128]{4,3,2,1,0:T(2,128)S(1)}, f32[3,2,6,2,128]{4,3,2,1,0:T(2,128)S(1)}, u32[]{:S(2)}, u32[]{:S(2)}) collective-permute-start(f32[3,2,6,2,128]{4,3,2,1,0:T(2,128)S(1)} %get-tuple-element.74), channel_id=1, source_target_pairs={{0,17},{1,16},{2,19},{3,18},{4,21},{5,20},{6,23},{7,22},{30,15},{3... | collective-permute-start | bytes 110600 | tf_op jit(solution)/shard_map/ppermute | solution.py:327
  68.8 4.6 %collective-permute-start.9 = (f32[3,2,6,2,128]{4,3,2,1,0:T(2,128)S(1)}, f32[3,2,6,2,128]{4,3,2,1,0:T(2,128)S(1)}, u32[]{:S(2)}, u32[]{:S(2)}) collective-permute-start(f32[3,2,6,2,128]{4,3,2,1,0:T(2,128)S(1)} %get-tuple-element.73), channel_id=1, source_target_pairs={{0,97},{1,96},{2,99},{3,98},{4,101},{5,100},{6,103},{7,102},{30,12... | collective-permute-start | bytes 110600 | tf_op jit(solution)/shard_map/ppermute | solution.py:326
  73.5 8.9 %collective-permute-start.11 = (f32[3,10,2,2,128]{4,3,2,1,0:T(2,128)S(1)}, f32[3,10,2,2,128]{4,3,2,1,0:T(2,128)S(1)}, u32[]{:S(2)}, u32[]{:S(2)}) collective-permute-start(f32[3,10,2,2,128]{4,3,2,1,0:T(2,128)S(1)} %get-tuple-element.61), channel_id=1, source_target_pairs={{0,25},{1,2},{2,1},{3,4},{4,3},{5,6},{6,5},{7,30},{30,7},{31,28},{... | collective-permute-start | bytes 184328 | tf_op jit(solution)/shard_map/ppermute | solution.py:326
  73.6 8.9 %collective-permute-start.12 = (f32[3,10,2,2,128]{4,3,2,1,0:T(2,128)S(1)}, f32[3,10,2,2,128]{4,3,2,1,0:T(2,128)S(1)}, u32[]{:S(2)}, u32[]{:S(2)}) collective-permute-start(f32[3,10,2,2,128]{4,3,2,1,0:T(2,128)S(1)} %get-tuple-element.62), channel_id=1, source_target_pairs={{0,1},{1,0},{2,3},{3,2},{4,5},{5,4},{6,7},{7,6},{30,31},{31,30},{2... | collective-permute-start | bytes 184328 | tf_op jit(solution)/shard_map/ppermute | solution.py:327
  75.8 12.2 %all-to-all-start.1 = ((f32[128,1,128]{2,1,0:T(1,128)}), f32[128,1,128]{2,1,0:T(1,128)S(1)}, u32[]{:S(2)}, u32[]{:S(2)}) async-start(f32[128,1,128]{2,1,0:T(1,128)} %bitcast.11), calls=%async_computation.1 | async-start | bytes 131072 | tf_op jit(solution)/shard_map/all_to_all | solution.py:358
  101.0 5.2 %collective-permute-start.13 = (f32[3,2,6,2,128]{4,3,2,1,0:T(2,128)S(1)}, f32[3,2,6,2,128]{4,3,2,1,0:T(2,128)S(1)}, u32[]{:S(2)}, u32[]{:S(2)}) collective-permute-start(f32[3,2,6,2,128]{4,3,2,1,0:T(2,128)S(1)} %get-tuple-element.71), channel_id=1, source_target_pairs={{0,97},{1,96},{2,99},{3,98},{4,101},{5,100},{6,103},{7,102},{30,12... | collective-permute-start | bytes 110600 | tf_op jit(solution)/shard_map/ppermute | solution.py:326
  103.4 3.4 %collective-permute-start.14 = (f32[3,2,6,2,128]{4,3,2,1,0:T(2,128)S(1)}, f32[3,2,6,2,128]{4,3,2,1,0:T(2,128)S(1)}, u32[]{:S(2)}, u32[]{:S(2)}) collective-permute-start(f32[3,2,6,2,128]{4,3,2,1,0:T(2,128)S(1)} %get-tuple-element.72), channel_id=1, source_target_pairs={{0,17},{1,16},{2,19},{3,18},{4,21},{5,20},{6,23},{7,22},{30,15},{3... | collective-permute-start | bytes 110600 | tf_op jit(solution)/shard_map/ppermute | solution.py:327
  106.8 9.5 %collective-permute-start.15 = (f32[3,10,2,2,128]{4,3,2,1,0:T(2,128)S(1)}, f32[3,10,2,2,128]{4,3,2,1,0:T(2,128)S(1)}, u32[]{:S(2)}, u32[]{:S(2)}) collective-permute-start(f32[3,10,2,2,128]{4,3,2,1,0:T(2,128)S(1)} %get-tuple-element.59), channel_id=1, source_target_pairs={{0,25},{1,2},{2,1},{3,4},{4,3},{5,6},{6,5},{7,30},{30,7},{31,28},{... | collective-permute-start | bytes 184328 | tf_op jit(solution)/shard_map/ppermute | solution.py:326
  106.9 9.4 %collective-permute-start.16 = (f32[3,10,2,2,128]{4,3,2,1,0:T(2,128)S(1)}, f32[3,10,2,2,128]{4,3,2,1,0:T(2,128)S(1)}, u32[]{:S(2)}, u32[]{:S(2)}) collective-permute-start(f32[3,10,2,2,128]{4,3,2,1,0:T(2,128)S(1)} %get-tuple-element.60), channel_id=1, source_target_pairs={{0,1},{1,0},{2,3},{3,2},{4,5},{5,4},{6,7},{7,6},{30,31},{31,30},{2... | collective-permute-start | bytes 184328 | tf_op jit(solution)/shard_map/ppermute | solution.py:327
  109.6 12.3 %all-to-all-start.2 = ((f32[128,1,128]{2,1,0:T(1,128)}), f32[128,1,128]{2,1,0:T(1,128)S(1)}, u32[]{:S(2)}, u32[]{:S(2)}) async-start(f32[128,1,128]{2,1,0:T(1,128)} %bitcast.14), calls=%async_computation.2 | async-start | bytes 131072 | tf_op jit(solution)/shard_map/all_to_all | solution.py:358
  134.8 14.1 %all-to-all-start.3 = ((f32[128,1,128]{2,1,0:T(1,128)}), f32[128,1,128]{2,1,0:T(1,128)S(1)}, u32[]{:S(2)}, u32[]{:S(2)}) async-start(f32[128,1,128]{2,1,0:T(1,128)} %bitcast.25), calls=%async_computation.3 | async-start | bytes 131072 | tf_op jit(solution)/shard_map/all_to_all | solution.py:358
  143.5 10.2 %copy-start.3 = (f32[2,6,6,128]{3,0,2,1:T(2,128)S(1)}, f32[2,6,6,128]{3,0,2,1:T(2,128)}, u32[]{:S(2)}) copy-start(f32[2,6,6,128]{3,0,2,1:T(2,128)} %param.7) | copy-start | bytes 110596
  143.6 10.2 %copy-start.1 = (f32[2,6,6,128]{3,0,2,1:T(2,128)S(1)}, f32[2,6,6,128]{3,0,2,1:T(2,128)}, u32[]{:S(2)}) copy-start(f32[2,6,6,128]{3,0,2,1:T(2,128)} %param.6) | copy-start | bytes 110596
  143.6 10.2 %copy-start.2 = (f32[2,6,6,128]{3,0,2,1:T(2,128)S(1)}, f32[2,6,6,128]{3,0,2,1:T(2,128)}, u32[]{:S(2)}) copy-start(f32[2,6,6,128]{3,0,2,1:T(2,128)} %param.8) | copy-start | bytes 110596
  143.6 10.1 %collective-permute-start.17 = (f32[8,6,6,128]{3,2,1,0:T(8,128)S(1)}, f32[8,6,6,128]{3,2,1,0:T(8,128)S(1)}, u32[]{:S(2)}, u32[]{:S(2)}) collective-permute-start(f32[8,6,6,128]{3,2,1,0:T(8,128)S(1)} %bitcast_dynamic-update-slice_fusion), channel_id=1, source_target_pairs={{0,0},{1,1},{2,2},{3,3},{4,4},{5,5},{6,6},{7,7},{30,8},{31,9},{28,... | collective-permute-start | bytes 442376 | tf_op jit(solution)/shard_map/ppermute | solution.py:311

commit v5 on v4

--- a/solution.py
+++ b/solution.py
@@ -106,7 +106,7 @@
     return acc.sum(axis=0, keepdims=True)
 
 
-OWN, TB, LR, FP = 9, 8, 6, 6
+OWN, RING, FP = 9, 7, 6
 TIME_STEP = 0.05
 KERNEL_NORM = 4.0 / (3.141592653589793 * 64.0)
 SENTINEL = 1.0e30
@@ -163,22 +163,16 @@
             dn[a + 4, pl.ds(b + 1, 1), :] = row[:, 128:]
         return carry
     lax.fori_loop(0, 18 // OWN, own, 0)
-    def top_bottom(h, carry):
-        for u in range(TB):
-            c = h * TB + u
-            row = density_pair(rs, lt, masks_ref, (1, c + 1), (8, c + 1), 50 + c + 1, 10)
-            dn[0, pl.ds(c, 1), :] = row[:, :128]
-            dn[7, pl.ds(c, 1), :] = row[:, 128:]
+    def ring(step, carry):
+        for u in range(RING):
+            n = step * RING + u
+            flat = n < 8
+            r1, r2, c1, c2 = (jnp.where(flat, p, q) for p, q in ((1, n - 6), (8, n - 6), (n + 1, 1), (n + 1, 8)))
+            row = density_pair(rs, lt, masks_ref, (r1, c1), (r2, c2), jnp.where(flat, n + 51, 3 * n + 50), jnp.where(flat, 10, 3))
+            dn[r1 - 1, pl.ds(c1 - 1, 1), :] = row[:, :128]
+            dn[r2 - 1, pl.ds(c2 - 1, 1), :] = row[:, 128:]
         return carry
-    lax.fori_loop(0, 8 // TB, top_bottom, 0)
-    def left_right(h, carry):
-        for u in range(LR):
-            a = h * LR + u + 1
-            row = density_pair(rs, lt, masks_ref, (a + 1, 1), (a + 1, 8), 70 + a * 3 + 1, 3)
-            dn[a, pl.ds(0, 1), :] = row[:, :128]
-            dn[a, pl.ds(7, 1), :] = row[:, 128:]
-        return carry
-    lax.fori_loop(0, 6 // LR, left_right, 0)
+    lax.fori_loop(0, 14 // RING, ring, 0)
     bounds_of(dn[...], own_ref[...], bnd_ref)
     code = code_ref[...]
     live = code > 0.0
@@ -286,6 +280,34 @@
         name="combine")(seen.reshape(128, 128), sums, code8, p8, gain)
 
 
+def kz_kernel(seen_ref, parts_ref, pos_ref, vel_ref, acc_ref, code_ref, a_ref, b_ref, c_ref, npos_ref, nvel_ref, press_ref, mon_ref):
+    top = seen_ref[...].max(axis=0, keepdims=True)
+    lane = lax.broadcasted_iota(jnp.int32, (1, 128), 1)
+    top0, top1, neg0, neg1 = (jnp.sum(jnp.where(lane == k, top, 0.0), axis=1, keepdims=True) for k in range(4))
+    r0 = (1.0 / (1.0 + top0 + neg0))[None]
+    r1 = (1.0 / (1.0 + top1 + neg1))[None]
+    row = jnp.where(lane < 2, top, -top)
+    mon_ref[...] = jnp.concatenate([a_ref[...], b_ref[...], c_ref[...], row], axis=0)[:, :4]
+    code = code_ref[...]
+    live = code > 0.0
+    for c in range(2):
+        delta = parts_ref[c] + r0 * parts_ref[2 + c] + r1 * parts_ref[4 + c]
+        speed = jnp.where(live, vel_ref[c] + TIME_STEP * acc_ref[c] + delta * (1.0 / TIME_STEP), 0.0)
+        nvel_ref[c] = speed
+        npos_ref[c] = jnp.where(live, pos_ref[c] + TIME_STEP * speed, 0.0)
+    press_ref[...] = parts_ref[6] + jnp.where(code == 2.0, r1, r0) * parts_ref[7]
+
+
+def call_kz(seen, parts, position, velocity, other_accel, code, rows):
+    return pl.pallas_call(
+        kz_kernel,
+        out_shape=(shaped((2, 6, 6, 128)), shaped((2, 6, 6, 128)), shaped((6, 6, 128)), shaped((4, 4))),
+        in_specs=[VM] * 9, out_specs=(VM,) * 4,
+        compiler_params=pltpu.CompilerParams(vmem_limit_bytes=8 * 1024 * 1024),
+        cost_estimate=pl.CostEstimate(flops=1_000_000, bytes_accessed=400_000, transcendentals=0),
+        name="finish")(seen.reshape(128, 128), parts, position, velocity, other_accel, code, *rows)
+
+
 FAR = 2.0 ** 20
 TILES = [(gx, gy) for gx in range(8) for gy in range(16)]
 
@@ -359,19 +381,11 @@
         if not last:
             wide = padded(sums)
             near, pressure, row = call_kc(seen, wide, code8, pressure, gain)
-            rows.append(row[0, :4])
-    top = seen.reshape(128, 128).max(axis=0)
-    row = jnp.concatenate([top[:2], -top[2:4]])
-    rows.append(row)
-    relax = 1.0 / (1.0 + row[:2] - row[2:])
+            rows.append(row)
     parts = jnp.stack([sums[0, :, :, 0], sums[0, :, :, 1], sums[1, :, :, 0], sums[1, :, :, 1], sums[2, :, :, 0], sums[2, :, :, 1],
                        pressure[1:7, 1:7], gain[1:7, 1:7]])
     parts = to_home(parts)
-    delta = parts[0:2] + relax[0] * parts[2:4] + relax[1] * parts[4:6]
-    new_velocity = jnp.where(live, velocity + TIME_STEP * other_accel + delta * (1.0 / TIME_STEP), 0.0)
-    new_position = jnp.where(live, position + TIME_STEP * new_velocity, 0.0)
-    new_pressure = parts[6] + jnp.where(phase_ids == 1, relax[1], relax[0]) * parts[7]
-    return new_position, new_velocity, new_pressure, jnp.stack(rows)
+    return call_kz(seen, parts, position, velocity, other_accel, code, rows)
 
 
 def solution(mesh):

time: 161 us -> 161 us (level)
  the two profiles are of different devices: /device:TPU:103 before, /device:TPU:1 now
where the time goes in v5:
time: 161 us
  waiting for transfers between devices  54.7 us (34%)
  Pallas kernels  52.6 us (33%)
  starting transfers between devices  47.3 us (29%)
  local copies, waits for them, and re-layouts  2.92 us (2%)
  other arithmetic  2.08 us (1%)
    pallas_call x4, Pallas kernels, call_kdf(): pl.pallas_call(kdf_kernel, out_shape=(shaped((128, 128)), shaped((3, 6, 6...  51.4 us
    all_to_all x4, waiting for transfers between devices, local(): seen = lax.all_to_all(bounds, ALL, 0, 0, tiled=True)  38.5 us
    all_to_all x4, starting transfers between devices, local(): seen = lax.all_to_all(bounds, ALL, 0, 0, tiled=True)  21.4 us
    ppermute x8, starting transfers between devices, swapped(): far = lax.ppermute(jnp.where(even, first, last), ALL, partners(dim, False))  16.3 us
    ppermute x8, waiting for transfers between devices, swapped(): far = lax.ppermute(jnp.where(even, first, last), ALL, partners(dim, False))  12.3 us
    ppermute x8, starting transfers between devices, swapped(): near = lax.ppermute(jnp.where(even, last, first), ALL, partners(dim, True))  8.29 us
    ppermute x8, waiting for transfers between devices, swapped(): near = lax.ppermute(jnp.where(even, last, first), ALL, partners(dim, True))  3.94 us
  transfers between devices with their start and end apart: 22, of which 11 were waited for; matrix products, arithmetic and copies ran while one was open for 0% of the time, Pallas kernels for 0%

profile of v5, /device:TPU:1, one launch (start us, length us, event | category | flops | bytes accessed | tf_op | source)
XLA Modules:
  0.0 160.7 jit_solution(6297604179044052416)
XLA Ops:
  0.6 0.8 fusion.8
  1.6 0.7 copy-done.1
  2.3 0.7 collective-permute-start
  3.0 9.1 %collective-permute-start.1 = (f32[1,2,6,3,128]{4,2,1,3,0:T(8,128)S(1)}, f32[1,2,6,3,128]{4,2,1,3,0:T(8,128)S(1)}, u32[]{:S(2)}, u32[]{:S(2)}) collective-permute-start(f32[1,2,6,3,128]{4,2,1,3,0:T(8,128)S(1)} %get-tuple-element.81), channel_id=1, source_target_pairs={{0,97},{1,96},{2,99},{3,98},{4,101},{5,100},{6,103},{7,102},{30,12... | collective-permute-start | bytes 55304 | tf_op jit(solution)/shard_map/ppermute | solution.py:348
  12.2 1.5 collective-permute-done.1
  13.7 1.7 %collective-permute-done.2 = f32[1,2,6,3,128]{4,2,1,3,0:T(8,128)S(1)} collective-permute-done((f32[1,2,6,3,128]{4,2,1,3,0:T(8,128)S(1)}, f32[1,2,6,3,128]{4,2,1,3,0:T(8,128)S(1)}, u32[]{:S(2)}, u32[]{:S(2)}) %collective-permute-start.2) | collective-permute-done | bytes 18464 | tf_op jit(solution)/shard_map/ppermute | solution.py:349
  15.5 0.4 collective-permute-start.4
  15.9 1.4 collective-permute-start.3
  17.3 1.9 %collective-permute-done.3 = f32[1,10,2,3,128]{4,2,1,3,0:T(2,128)S(1)} collective-permute-done((f32[1,10,2,3,128]{4,2,1,3,0:T(2,128)S(1)}, f32[1,10,2,3,128]{4,2,1,3,0:T(2,128)S(1)}, u32[]{:S(2)}, u32[]{:S(2)}) %collective-permute-start.3) | collective-permute-done | bytes 30752 | tf_op jit(solution)/shard_map/ppermute | solution.py:348
  19.3 0.1 copy.31.pos_ref
  19.4 0.8 copy-done
  20.2 12.8 %sweep.4 = (f32[128,128]{1,0:T(8,128)}, f32[3,6,6,2,128]{4,3,2,1,0:T(2,128)S(1)}, f32[8,8,128]{2,1,0:T(8,128)S(1)}) custom-call(f32[10,10,2,128]{3,2,1,0:T(2,128)S(1)} %copy.31.pos_ref, f32[6,6,2,128]{3,2,1,0:T(2,128)S(1)} %copy.32.base_ref, f32[8,8,128]{2,1,0:T(8,128)S(1)} %slice_bitcast_fusion.code_ref, f32[8,8,128]{2,1,0:T(8,128)S(1)} %pad.4.own_ref, ...), custom_call_target="tpu_custom_call" | custom-call | flops 40000000 | bytes 400000 | tf_op jit(solution)/shard_map/sweep/pallas_call | solution.py:261
  33.1 1.3 collective-permute-start.5
  34.4 3.4 %collective-permute-done.5 = f32[3,2,6,2,128]{4,3,2,1,0:T(2,128)S(1)} collective-permute-done((f32[3,2,6,2,128]{4,3,2,1,0:T(2,128)S(1)}, f32[3,2,6,2,128]{4,3,2,1,0:T(2,128)S(1)}, u32[]{:S(2)}, u32[]{:S(2)}) %collective-permute-start.5) | collective-permute-done | bytes 36896 | tf_op jit(solution)/shard_map/ppermute | solution.py:348
  37.8 1.5 collective-permute-start.7
  39.3 5.4 %collective-permute-start.8 = (f32[3,10,2,2,128]{4,3,2,1,0:T(2,128)S(1)}, f32[3,10,2,2,128]{4,3,2,1,0:T(2,128)S(1)}, u32[]{:S(2)}, u32[]{:S(2)}) collective-permute-start(f32[3,10,2,2,128]{4,3,2,1,0:T(2,128)S(1)} %get-tuple-element.62), channel_id=1, source_target_pairs={{0,1},{1,0},{2,3},{3,2},{4,5},{5,4},{6,7},{7,6},{30,31},{31,30},{2... | collective-permute-start | bytes 184328 | tf_op jit(solution)/shard_map/ppermute | solution.py:349
  44.7 5.5 %all-to-all-start = ((f32[128,1,128]{2,1,0:T(1,128)}), f32[128,1,128]{2,1,0:T(1,128)S(1)}, u32[]{:S(2)}, u32[]{:S(2)}) async-start(f32[128,1,128]{2,1,0:T(1,128)} %bitcast.8), calls=%async_computation | async-start | bytes 131072 | tf_op jit(solution)/shard_map/all_to_all | solution.py:380
  50.3 0.1 pad_maximum_fusion.s_ref
  50.4 9.6 %all-to-all-done = f32[128,1,128]{2,1,0:T(1,128)S(1)} async-done(((f32[128,1,128]{2,1,0:T(1,128)}), f32[128,1,128]{2,1,0:T(1,128)S(1)}, u32[]{:S(2)}, u32[]{:S(2)}) %all-to-all-start) | async-done | bytes 65568 | tf_op jit(solution)/shard_map/all_to_all | solution.py:380
  60.0 0.2 combine.3
  60.2 12.8 %sweep.5 = (f32[128,128]{1,0:T(8,128)}, f32[3,6,6,2,128]{4,3,2,1,0:T(2,128)S(1)}, f32[8,8,128]{2,1,0:T(8,128)S(1)}) custom-call(f32[10,10,2,128]{3,2,1,0:T(2,128)S(1)} %get-tuple-element.28.pos_ref, f32[6,6,2,128]{3,2,1,0:T(2,128)S(1)} %copy.32.base_ref, f32[8,8,128]{2,1,0:T(8,128)S(1)} %slice_bitcast_fusion.code_ref, f32[8,8,128]{2,1,0:T(8,128)S(1)} %pad.4.own_ref, ...), custom_call_target="tpu_custom_call" | custom-call | flops 40000000 | bytes 400000 | tf_op jit(solution)/shard_map/sweep/pallas_call | solution.py:261
  73.1 1.1 collective-permute-start.10
  74.2 0.6 collective-permute-start.9
  74.9 2.2 %collective-permute-done.10 = f32[3,2,6,2,128]{4,3,2,1,0:T(2,128)S(1)} collective-permute-done((f32[3,2,6,2,128]{4,3,2,1,0:T(2,128)S(1)}, f32[3,2,6,2,128]{4,3,2,1,0:T(2,128)S(1)}, u32[]{:S(2)}, u32[]{:S(2)}) %collective-permute-start.10) | collective-permute-done | bytes 36896 | tf_op jit(solution)/shard_map/ppermute | solution.py:349
  77.0 1.8 %collective-permute-done.9 = f32[3,2,6,2,128]{4,3,2,1,0:T(2,128)S(1)} collective-permute-done((f32[3,2,6,2,128]{4,3,2,1,0:T(2,128)S(1)}, f32[3,2,6,2,128]{4,3,2,1,0:T(2,128)S(1)}, u32[]{:S(2)}, u32[]{:S(2)}) %collective-permute-start.9) | collective-permute-done | bytes 36896 | tf_op jit(solution)/shard_map/ppermute | solution.py:348
  78.9 0.2 collective-permute-start.11
  79.1 1.1 collective-permute-start.12
  80.3 3.7 %all-to-all-start.1 = ((f32[128,1,128]{2,1,0:T(1,128)}), f32[128,1,128]{2,1,0:T(1,128)S(1)}, u32[]{:S(2)}, u32[]{:S(2)}) async-start(f32[128,1,128]{2,1,0:T(1,128)} %bitcast.11), calls=%async_computation.1 | async-start | bytes 131072 | tf_op jit(solution)/shard_map/all_to_all | solution.py:380
  84.0 0.1 pad_maximum_fusion.1.s_ref
  84.2 9.6 %all-to-all-done.1 = f32[128,1,128]{2,1,0:T(1,128)S(1)} async-done(((f32[128,1,128]{2,1,0:T(1,128)}), f32[128,1,128]{2,1,0:T(1,128)S(1)}, u32[]{:S(2)}, u32[]{:S(2)}) %all-to-all-start.1) | async-done | bytes 65568 | tf_op jit(solution)/shard_map/all_to_all | solution.py:380
  93.7 0.2 combine.4
  93.9 12.8 %sweep.6 = (f32[128,128]{1,0:T(8,128)}, f32[3,6,6,2,128]{4,3,2,1,0:T(2,128)S(1)}, f32[8,8,128]{2,1,0:T(8,128)S(1)}) custom-call(f32[10,10,2,128]{3,2,1,0:T(2,128)S(1)} %get-tuple-element.33.pos_ref, f32[6,6,2,128]{3,2,1,0:T(2,128)S(1)} %copy.32.base_ref, f32[8,8,128]{2,1,0:T(8,128)S(1)} %slice_bitcast_fusion.code_ref, f32[8,8,128]{2,1,0:T(8,128)S(1)} %pad.4.own_ref, ...), custom_call_target="tpu_custom_call" | custom-call | flops 40000000 | bytes 400000 | tf_op jit(solution)/shard_map/sweep/pallas_call | solution.py:261
  106.8 1.4 collective-permute-start.13
  108.2 3.7 %collective-permute-done.13 = f32[3,2,6,2,128]{4,3,2,1,0:T(2,128)S(1)} collective-permute-done((f32[3,2,6,2,128]{4,3,2,1,0:T(2,128)S(1)}, f32[3,2,6,2,128]{4,3,2,1,0:T(2,128)S(1)}, u32[]{:S(2)}, u32[]{:S(2)}) %collective-permute-start.13) | collective-permute-done | bytes 36896 | tf_op jit(solution)/shard_map/ppermute | solution.py:348
  112.0 0.8 collective-permute-start.15
  112.8 0.2 collective-permute-start.16
  113.0 4.8 %all-to-all-start.2 = ((f32[128,1,128]{2,1,0:T(1,128)}), f32[128,1,128]{2,1,0:T(1,128)S(1)}, u32[]{:S(2)}, u32[]{:S(2)}) async-start(f32[128,1,128]{2,1,0:T(1,128)} %bitcast.14), calls=%async_computation.2 | async-start | bytes 131072 | tf_op jit(solution)/shard_map/all_to_all | solution.py:380
  117.9 0.1 pad_maximum_fusion.2.s_ref
  118.0 9.6 %all-to-all-done.2 = f32[128,1,128]{2,1,0:T(1,128)S(1)} async-done(((f32[128,1,128]{2,1,0:T(1,128)}), f32[128,1,128]{2,1,0:T(1,128)S(1)}, u32[]{:S(2)}, u32[]{:S(2)}) %all-to-all-start.2) | async-done | bytes 65568 | tf_op jit(solution)/shard_map/all_to_all | solution.py:380
  127.6 0.2 combine.5
  127.8 12.8 %sweep.7 = (f32[128,128]{1,0:T(8,128)}, f32[3,6,6,2,128]{4,3,2,1,0:T(2,128)S(1)}, f32[8,8,128]{2,1,0:T(8,128)S(1)}) custom-call(f32[10,10,2,128]{3,2,1,0:T(2,128)S(1)} %get-tuple-element.38.pos_ref, f32[6,6,2,128]{3,2,1,0:T(2,128)S(1)} %broadcast_in_dim.31.base_ref, f32[8,8,128]{2,1,0:T(8,128)S(1)} %slice_bitcast_fusion.code_ref, ...), custom_call_target="tpu_custom_call" | custom-call | flops 40000000 | bytes 400000 | tf_op jit(solution)/shard_map/sweep/pallas_call | solution.py:261
  140.8 0.7 collective-permute-start.17
  141.5 7.4 %all-to-all-start.3 = ((f32[128,1,128]{2,1,0:T(1,128)}), f32[128,1,128]{2,1,0:T(1,128)S(1)}, u32[]{:S(2)}, u32[]{:S(2)}) async-start(f32[128,1,128]{2,1,0:T(1,128)} %bitcast.17), calls=%async_computation.3 | async-start | bytes 131072 | tf_op jit(solution)/shard_map/all_to_all | solution.py:380
  148.9 0.1 select_convert_fusion.code_ref
  148.9 9.7 %all-to-all-done.3 = f32[128,1,128]{2,1,0:T(1,128)S(1)} async-done(((f32[128,1,128]{2,1,0:T(1,128)}), f32[128,1,128]{2,1,0:T(1,128)S(1)}, u32[]{:S(2)}, u32[]{:S(2)}) %all-to-all-start.3) | async-done | bytes 65568 | tf_op jit(solution)/shard_map/all_to_all | solution.py:380
  158.7 0.7 finish.1
  159.4 0.6 copy.48
  160.1 0.6 copy.49
  (56 shorter events, 0.9 us)
Async XLA Ops:
  0.6 0.8 copy-start.2
  1.5 0.7 copy-start.1
  2.3 0.7 collective-permute-start
  3.0 10.6 %collective-permute-start.1 = (f32[1,2,6,3,128]{4,2,1,3,0:T(8,128)S(1)}, f32[1,2,6,3,128]{4,2,1,3,0:T(8,128)S(1)}, u32[]{:S(2)}, u32[]{:S(2)}) collective-permute-start(f32[1,2,6,3,128]{4,2,1,3,0:T(8,128)S(1)} %get-tuple-element.81), channel_id=1, source_target_pairs={{0,97},{1,96},{2,99},{3,98},{4,101},{5,100},{6,103},{7,102},{30,12... | collective-permute-start | bytes 55304 | tf_op jit(solution)/shard_map/ppermute | solution.py:348
  12.2 3.3 %collective-permute-start.2 = (f32[1,2,6,3,128]{4,2,1,3,0:T(8,128)S(1)}, f32[1,2,6,3,128]{4,2,1,3,0:T(8,128)S(1)}, u32[]{:S(2)}, u32[]{:S(2)}) collective-permute-start(f32[1,2,6,3,128]{4,2,1,3,0:T(8,128)S(1)} %get-tuple-element.82), channel_id=1, source_target_pairs={{0,17},{1,16},{2,19},{3,18},{4,21},{5,20},{6,23},{7,22},{30,15},{3... | collective-permute-start | bytes 55304 | tf_op jit(solution)/shard_map/ppermute | solution.py:349
  15.5 1.8 %collective-permute-start.4 = (f32[1,10,2,3,128]{4,2,1,3,0:T(2,128)S(1)}, f32[1,10,2,3,128]{4,2,1,3,0:T(2,128)S(1)}, u32[]{:S(2)}, u32[]{:S(2)}) collective-permute-start(f32[1,10,2,3,128]{4,2,1,3,0:T(2,128)S(1)} %broadcast_select_fusion.26), channel_id=1, source_target_pairs={{0,1},{1,0},{2,3},{3,2},{4,5},{5,4},{6,7},{7,6},{30,31},{31,30},{2... | collective-permute-start | bytes 92168 | tf_op jit(solution)/shard_map/ppermute | solution.py:349
  15.9 3.3 %collective-permute-start.3 = (f32[1,10,2,3,128]{4,2,1,3,0:T(2,128)S(1)}, f32[1,10,2,3,128]{4,2,1,3,0:T(2,128)S(1)}, u32[]{:S(2)}, u32[]{:S(2)}) collective-permute-start(f32[1,10,2,3,128]{4,2,1,3,0:T(2,128)S(1)} %get-tuple-element.54), channel_id=1, source_target_pairs={{0,25},{1,2},{2,1},{3,4},{4,3},{5,6},{6,5},{7,30},{30,7},{31,28},{... | collective-permute-start | bytes 92168 | tf_op jit(solution)/shard_map/ppermute | solution.py:348
  19.3 0.9 copy-start
  33.1 4.7 %collective-permute-start.5 = (f32[3,2,6,2,128]{4,3,2,1,0:T(2,128)S(1)}, f32[3,2,6,2,128]{4,3,2,1,0:T(2,128)S(1)}, u32[]{:S(2)}, u32[]{:S(2)}) collective-permute-start(f32[3,2,6,2,128]{4,3,2,1,0:T(2,128)S(1)} %get-tuple-element.73), channel_id=1, source_target_pairs={{0,97},{1,96},{2,99},{3,98},{4,101},{5,100},{6,103},{7,102},{30,12... | collective-permute-start | bytes 110600 | tf_op jit(solution)/shard_map/ppermute | solution.py:348
  34.4 3.4 %collective-permute-start.6 = (f32[3,2,6,2,128]{4,3,2,1,0:T(2,128)S(1)}, f32[3,2,6,2,128]{4,3,2,1,0:T(2,128)S(1)}, u32[]{:S(2)}, u32[]{:S(2)}) collective-permute-start(f32[3,2,6,2,128]{4,3,2,1,0:T(2,128)S(1)} %get-tuple-element.74), channel_id=1, source_target_pairs={{0,17},{1,16},{2,19},{3,18},{4,21},{5,20},{6,23},{7,22},{30,15},{3... | collective-permute-start | bytes 110600 | tf_op jit(solution)/shard_map/ppermute | solution.py:349
  37.8 12.4 %collective-permute-start.7 = (f32[3,10,2,2,128]{4,3,2,1,0:T(2,128)S(1)}, f32[3,10,2,2,128]{4,3,2,1,0:T(2,128)S(1)}, u32[]{:S(2)}, u32[]{:S(2)}) collective-permute-start(f32[3,10,2,2,128]{4,3,2,1,0:T(2,128)S(1)} %get-tuple-element.61), channel_id=1, source_target_pairs={{0,25},{1,2},{2,1},{3,4},{4,3},{5,6},{6,5},{7,30},{30,7},{31,28},{... | collective-permute-start | bytes 184328 | tf_op jit(solution)/shard_map/ppermute | solution.py:348
  39.3 10.9 %collective-permute-start.8 = (f32[3,10,2,2,128]{4,3,2,1,0:T(2,128)S(1)}, f32[3,10,2,2,128]{4,3,2,1,0:T(2,128)S(1)}, u32[]{:S(2)}, u32[]{:S(2)}) collective-permute-start(f32[3,10,2,2,128]{4,3,2,1,0:T(2,128)S(1)} %get-tuple-element.62), channel_id=1, source_target_pairs={{0,1},{1,0},{2,3},{3,2},{4,5},{5,4},{6,7},{7,6},{30,31},{31,30},{2... | collective-permute-start | bytes 184328 | tf_op jit(solution)/shard_map/ppermute | solution.py:349
  44.7 15.3 %all-to-all-start = ((f32[128,1,128]{2,1,0:T(1,128)}), f32[128,1,128]{2,1,0:T(1,128)S(1)}, u32[]{:S(2)}, u32[]{:S(2)}) async-start(f32[128,1,128]{2,1,0:T(1,128)} %bitcast.8), calls=%async_computation | async-start | bytes 131072 | tf_op jit(solution)/shard_map/all_to_all | solution.py:380
  73.1 4.0 %collective-permute-start.10 = (f32[3,2,6,2,128]{4,3,2,1,0:T(2,128)S(1)}, f32[3,2,6,2,128]{4,3,2,1,0:T(2,128)S(1)}, u32[]{:S(2)}, u32[]{:S(2)}) collective-permute-start(f32[3,2,6,2,128]{4,3,2,1,0:T(2,128)S(1)} %get-tuple-element.72), channel_id=1, source_target_pairs={{0,17},{1,16},{2,19},{3,18},{4,21},{5,20},{6,23},{7,22},{30,15},{3... | collective-permute-start | bytes 110600 | tf_op jit(solution)/shard_map/ppermute | solution.py:349
  74.2 4.6 %collective-permute-start.9 = (f32[3,2,6,2,128]{4,3,2,1,0:T(2,128)S(1)}, f32[3,2,6,2,128]{4,3,2,1,0:T(2,128)S(1)}, u32[]{:S(2)}, u32[]{:S(2)}) collective-permute-start(f32[3,2,6,2,128]{4,3,2,1,0:T(2,128)S(1)} %get-tuple-element.71), channel_id=1, source_target_pairs={{0,97},{1,96},{2,99},{3,98},{4,101},{5,100},{6,103},{7,102},{30,12... | collective-permute-start | bytes 110600 | tf_op jit(solution)/shard_map/ppermute | solution.py:348
  78.9 5.0 %collective-permute-start.11 = (f32[3,10,2,2,128]{4,3,2,1,0:T(2,128)S(1)}, f32[3,10,2,2,128]{4,3,2,1,0:T(2,128)S(1)}, u32[]{:S(2)}, u32[]{:S(2)}) collective-permute-start(f32[3,10,2,2,128]{4,3,2,1,0:T(2,128)S(1)} %get-tuple-element.59), channel_id=1, source_target_pairs={{0,25},{1,2},{2,1},{3,4},{4,3},{5,6},{6,5},{7,30},{30,7},{31,28},{... | collective-permute-start | bytes 184328 | tf_op jit(solution)/shard_map/ppermute | solution.py:348
  79.1 4.8 %collective-permute-start.12 = (f32[3,10,2,2,128]{4,3,2,1,0:T(2,128)S(1)}, f32[3,10,2,2,128]{4,3,2,1,0:T(2,128)S(1)}, u32[]{:S(2)}, u32[]{:S(2)}) collective-permute-start(f32[3,10,2,2,128]{4,3,2,1,0:T(2,128)S(1)} %get-tuple-element.60), channel_id=1, source_target_pairs={{0,1},{1,0},{2,3},{3,2},{4,5},{5,4},{6,7},{7,6},{30,31},{31,30},{2... | collective-permute-start | bytes 184328 | tf_op jit(solution)/shard_map/ppermute | solution.py:349
  80.3 13.5 %all-to-all-start.1 = ((f32[128,1,128]{2,1,0:T(1,128)}), f32[128,1,128]{2,1,0:T(1,128)S(1)}, u32[]{:S(2)}, u32[]{:S(2)}) async-start(f32[128,1,128]{2,1,0:T(1,128)} %bitcast.11), calls=%async_computation.1 | async-start | bytes 131072 | tf_op jit(solution)/shard_map/all_to_all | solution.py:380
  106.8 5.2 %collective-permute-start.13 = (f32[3,2,6,2,128]{4,3,2,1,0:T(2,128)S(1)}, f32[3,2,6,2,128]{4,3,2,1,0:T(2,128)S(1)}, u32[]{:S(2)}, u32[]{:S(2)}) collective-permute-start(f32[3,2,6,2,128]{4,3,2,1,0:T(2,128)S(1)} %get-tuple-element.69), channel_id=1, source_target_pairs={{0,97},{1,96},{2,99},{3,98},{4,101},{5,100},{6,103},{7,102},{30,12... | collective-permute-start | bytes 110600 | tf_op jit(solution)/shard_map/ppermute | solution.py:348
  108.2 3.7 %collective-permute-start.14 = (f32[3,2,6,2,128]{4,3,2,1,0:T(2,128)S(1)}, f32[3,2,6,2,128]{4,3,2,1,0:T(2,128)S(1)}, u32[]{:S(2)}, u32[]{:S(2)}) collective-permute-start(f32[3,2,6,2,128]{4,3,2,1,0:T(2,128)S(1)} %get-tuple-element.70), channel_id=1, source_target_pairs={{0,17},{1,16},{2,19},{3,18},{4,21},{5,20},{6,23},{7,22},{30,15},{3... | collective-permute-start | bytes 110600 | tf_op jit(solution)/shard_map/ppermute | solution.py:349
  112.0 5.8 %collective-permute-start.15 = (f32[3,10,2,2,128]{4,3,2,1,0:T(2,128)S(1)}, f32[3,10,2,2,128]{4,3,2,1,0:T(2,128)S(1)}, u32[]{:S(2)}, u32[]{:S(2)}) collective-permute-start(f32[3,10,2,2,128]{4,3,2,1,0:T(2,128)S(1)} %get-tuple-element.57), channel_id=1, source_target_pairs={{0,25},{1,2},{2,1},{3,4},{4,3},{5,6},{6,5},{7,30},{30,7},{31,28},{... | collective-permute-start | bytes 184328 | tf_op jit(solution)/shard_map/ppermute | solution.py:348
  112.8 5.0 %collective-permute-start.16 = (f32[3,10,2,2,128]{4,3,2,1,0:T(2,128)S(1)}, f32[3,10,2,2,128]{4,3,2,1,0:T(2,128)S(1)}, u32[]{:S(2)}, u32[]{:S(2)}) collective-permute-start(f32[3,10,2,2,128]{4,3,2,1,0:T(2,128)S(1)} %get-tuple-element.58), channel_id=1, source_target_pairs={{0,1},{1,0},{2,3},{3,2},{4,5},{5,4},{6,7},{7,6},{30,31},{31,30},{2... | collective-permute-start | bytes 184328 | tf_op jit(solution)/shard_map/ppermute | solution.py:349
  113.0 14.6 %all-to-all-start.2 = ((f32[128,1,128]{2,1,0:T(1,128)}), f32[128,1,128]{2,1,0:T(1,128)S(1)}, u32[]{:S(2)}, u32[]{:S(2)}) async-start(f32[128,1,128]{2,1,0:T(1,128)} %bitcast.14), calls=%async_computation.2 | async-start | bytes 131072 | tf_op jit(solution)/shard_map/all_to_all | solution.py:380
  140.8 17.9 %collective-permute-start.17 = (f32[8,6,6,128]{3,2,1,0:T(8,128)S(1)}, f32[8,6,6,128]{3,2,1,0:T(8,128)S(1)}, u32[]{:S(2)}, u32[]{:S(2)}) collective-permute-start(f32[8,6,6,128]{3,2,1,0:T(8,128)S(1)} %bitcast_dynamic-update-slice_fusion), channel_id=1, source_target_pairs={{0,0},{1,1},{2,2},{3,3},{4,4},{5,5},{6,6},{7,7},{30,8},{31,9},{28,... | collective-permute-start | bytes 442376 | tf_op jit(solution)/shard_map/ppermute | solution.py:333
  141.5 17.2 %all-to-all-start.3 = ((f32[128,1,128]{2,1,0:T(1,128)}), f32[128,1,128]{2,1,0:T(1,128)S(1)}, u32[]{:S(2)}, u32[]{:S(2)}) async-start(f32[128,1,128]{2,1,0:T(1,128)} %bitcast.17), calls=%async_computation.3 | async-start | bytes 131072 | tf_op jit(solution)/shard_map/all_to_all | solution.py:380

commit v6 on v5

--- a/solution.py
+++ b/solution.py
@@ -293,15 +293,18 @@
     for c in range(2):
         delta = parts_ref[c] + r0 * parts_ref[2 + c] + r1 * parts_ref[4 + c]
         speed = jnp.where(live, vel_ref[c] + TIME_STEP * acc_ref[c] + delta * (1.0 / TIME_STEP), 0.0)
-        nvel_ref[c] = speed
-        npos_ref[c] = jnp.where(live, pos_ref[c] + TIME_STEP * speed, 0.0)
+        place = jnp.where(live, pos_ref[c] + TIME_STEP * speed, 0.0)
+        for a in range(6):
+            for b in range(6):
+                nvel_ref[a, b, c:c + 1, :] = speed[a, b:b + 1]
+                npos_ref[a, b, c:c + 1, :] = place[a, b:b + 1]
     press_ref[...] = parts_ref[6] + jnp.where(code == 2.0, r1, r0) * parts_ref[7]
 
 
 def call_kz(seen, parts, position, velocity, other_accel, code, rows):
     return pl.pallas_call(
         kz_kernel,
-        out_shape=(shaped((2, 6, 6, 128)), shaped((2, 6, 6, 128)), shaped((6, 6, 128)), shaped((4, 4))),
+        out_shape=(shaped((6, 6, 2, 128)), shaped((6, 6, 2, 128)), shaped((6, 6, 128)), shaped((4, 4))),
         in_specs=[VM] * 9, out_specs=(VM,) * 4,
         compiler_params=pltpu.CompilerParams(vmem_limit_bytes=8 * 1024 * 1024),
         cost_estimate=pl.CostEstimate(flops=1_000_000, bytes_accessed=400_000, transcendentals=0),
@@ -385,7 +388,8 @@
     parts = jnp.stack([sums[0, :, :, 0], sums[0, :, :, 1], sums[1, :, :, 0], sums[1, :, :, 1], sums[2, :, :, 0], sums[2, :, :, 1],
                        pressure[1:7, 1:7], gain[1:7, 1:7]])
     parts = to_home(parts)
-    return call_kz(seen, parts, position, velocity, other_accel, code, rows)
+    new_position, new_velocity, new_pressure, monitor = call_kz(seen, parts, position, velocity, other_accel, code, rows)
+    return new_position.transpose((2, 0, 1, 3)), new_velocity.transpose((2, 0, 1, 3)), new_pressure, monitor
 
 
 def solution(mesh):

time: 161 us -> 160 us (level)
  no operation moved by 1% of the time
where the time goes in v6:
time: 160 us; the launch traced here: 159 us
  waiting for transfers between devices  54.7 us (34%)
  Pallas kernels  52.6 us (33%)
  starting transfers between devices  47.3 us (30%)
  other arithmetic  2.08 us (1%)
  local copies, waits for them, and re-layouts  1.65 us (1%)
    pallas_call x4, Pallas kernels, call_kdf(): pl.pallas_call(kdf_kernel, out_shape=(shaped((128, 128)), shaped((3, 6, 6...  51.4 us
    all_to_all x4, waiting for transfers between devices, local(): seen = lax.all_to_all(bounds, ALL, 0, 0, tiled=True)  38.5 us
    all_to_all x4, starting transfers between devices, local(): seen = lax.all_to_all(bounds, ALL, 0, 0, tiled=True)  21.4 us
    ppermute x8, starting transfers between devices, swapped(): far = lax.ppermute(jnp.where(even, first, last), ALL, partners(dim, False))  16.3 us
    ppermute x8, waiting for transfers between devices, swapped(): far = lax.ppermute(jnp.where(even, first, last), ALL, partners(dim, False))  12.3 us
    ppermute x8, starting transfers between devices, swapped(): near = lax.ppermute(jnp.where(even, last, first), ALL, partners(dim, True))  8.29 us
    ppermute x8, waiting for transfers between devices, swapped(): near = lax.ppermute(jnp.where(even, last, first), ALL, partners(dim, True))  3.94 us
  transfers between devices with their start and end apart: 22, of which 11 were waited for; matrix products, arithmetic and copies ran while one was open for 0% of the time, Pallas kernels for 0%

profile of v6, /device:TPU:1, one launch (start us, length us, event | category | flops | bytes accessed | tf_op | source)
XLA Modules:
  0.0 159.4 jit_solution(17383221792580684535)
XLA Ops:
  0.6 0.8 fusion.8
  1.5 0.1 fusion.7
  1.6 0.7 copy-done.1
  2.2 0.1 fusion.9
  2.3 0.7 collective-permute-start
  3.0 9.1 %collective-permute-start.1 = (f32[1,2,6,3,128]{4,2,1,3,0:T(8,128)S(1)}, f32[1,2,6,3,128]{4,2,1,3,0:T(8,128)S(1)}, u32[]{:S(2)}, u32[]{:S(2)}) collective-permute-start(f32[1,2,6,3,128]{4,2,1,3,0:T(8,128)S(1)} %get-tuple-element.81), channel_id=1, source_target_pairs={{0,97},{1,96},{2,99},{3,98},{4,101},{5,100},{6,103},{7,102},{30,12... | collective-permute-start | bytes 55304 | tf_op jit(solution)/shard_map/ppermute | solution.py:351
  12.2 1.5 collective-permute-done.1
  13.7 1.7 %collective-permute-done.2 = f32[1,2,6,3,128]{4,2,1,3,0:T(8,128)S(1)} collective-permute-done((f32[1,2,6,3,128]{4,2,1,3,0:T(8,128)S(1)}, f32[1,2,6,3,128]{4,2,1,3,0:T(8,128)S(1)}, u32[]{:S(2)}, u32[]{:S(2)}) %collective-permute-start.2) | collective-permute-done | bytes 18464 | tf_op jit(solution)/shard_map/ppermute | solution.py:352
  15.5 0.4 collective-permute-start.4
  15.9 1.4 collective-permute-start.3
  17.3 1.9 %collective-permute-done.3 = f32[1,10,2,3,128]{4,2,1,3,0:T(2,128)S(1)} collective-permute-done((f32[1,10,2,3,128]{4,2,1,3,0:T(2,128)S(1)}, f32[1,10,2,3,128]{4,2,1,3,0:T(2,128)S(1)}, u32[]{:S(2)}, u32[]{:S(2)}) %collective-permute-start.3) | collective-permute-done | bytes 30752 | tf_op jit(solution)/shard_map/ppermute | solution.py:351
  19.3 0.1 copy.29.pos_ref
  19.4 0.8 copy-done
  20.2 12.8 %sweep.4 = (f32[128,128]{1,0:T(8,128)}, f32[3,6,6,2,128]{4,3,2,1,0:T(2,128)S(1)}, f32[8,8,128]{2,1,0:T(8,128)S(1)}) custom-call(f32[10,10,2,128]{3,2,1,0:T(2,128)S(1)} %copy.29.pos_ref, f32[6,6,2,128]{3,2,1,0:T(2,128)S(1)} %copy.30.base_ref, f32[8,8,128]{2,1,0:T(8,128)S(1)} %slice_bitcast_fusion.code_ref, f32[8,8,128]{2,1,0:T(8,128)S(1)} %pad.4.own_ref, ...), custom_call_target="tpu_custom_call" | custom-call | flops 40000000 | bytes 400000 | tf_op jit(solution)/shard_map/sweep/pallas_call | solution.py:261
  33.1 1.3 collective-permute-start.5
  34.4 3.4 %collective-permute-done.5 = f32[3,2,6,2,128]{4,3,2,1,0:T(2,128)S(1)} collective-permute-done((f32[3,2,6,2,128]{4,3,2,1,0:T(2,128)S(1)}, f32[3,2,6,2,128]{4,3,2,1,0:T(2,128)S(1)}, u32[]{:S(2)}, u32[]{:S(2)}) %collective-permute-start.5) | collective-permute-done | bytes 36896 | tf_op jit(solution)/shard_map/ppermute | solution.py:351
  37.8 1.5 collective-permute-start.7
  39.3 5.4 %collective-permute-start.8 = (f32[3,10,2,2,128]{4,3,2,1,0:T(2,128)S(1)}, f32[3,10,2,2,128]{4,3,2,1,0:T(2,128)S(1)}, u32[]{:S(2)}, u32[]{:S(2)}) collective-permute-start(f32[3,10,2,2,128]{4,3,2,1,0:T(2,128)S(1)} %get-tuple-element.62), channel_id=1, source_target_pairs={{0,1},{1,0},{2,3},{3,2},{4,5},{5,4},{6,7},{7,6},{30,31},{31,30},{2... | collective-permute-start | bytes 184328 | tf_op jit(solution)/shard_map/ppermute | solution.py:352
  44.7 5.5 %all-to-all-start = ((f32[128,1,128]{2,1,0:T(1,128)}), f32[128,1,128]{2,1,0:T(1,128)S(1)}, u32[]{:S(2)}, u32[]{:S(2)}) async-start(f32[128,1,128]{2,1,0:T(1,128)} %bitcast.8), calls=%async_computation | async-start | bytes 131072 | tf_op jit(solution)/shard_map/all_to_all | solution.py:383
  50.3 0.1 pad_maximum_fusion.s_ref
  50.4 9.6 %all-to-all-done = f32[128,1,128]{2,1,0:T(1,128)S(1)} async-done(((f32[128,1,128]{2,1,0:T(1,128)}), f32[128,1,128]{2,1,0:T(1,128)S(1)}, u32[]{:S(2)}, u32[]{:S(2)}) %all-to-all-start) | async-done | bytes 65568 | tf_op jit(solution)/shard_map/all_to_all | solution.py:383
  60.0 0.2 combine.3
  60.2 12.8 %sweep.5 = (f32[128,128]{1,0:T(8,128)}, f32[3,6,6,2,128]{4,3,2,1,0:T(2,128)S(1)}, f32[8,8,128]{2,1,0:T(8,128)S(1)}) custom-call(f32[10,10,2,128]{3,2,1,0:T(2,128)S(1)} %get-tuple-element.32.pos_ref, f32[6,6,2,128]{3,2,1,0:T(2,128)S(1)} %copy.30.base_ref, f32[8,8,128]{2,1,0:T(8,128)S(1)} %slice_bitcast_fusion.code_ref, f32[8,8,128]{2,1,0:T(8,128)S(1)} %pad.4.own_ref, ...), custom_call_target="tpu_custom_call" | custom-call | flops 40000000 | bytes 400000 | tf_op jit(solution)/shard_map/sweep/pallas_call | solution.py:261
  73.1 1.1 collective-permute-start.10
  74.2 0.6 collective-permute-start.9
  74.9 2.2 %collective-permute-done.10 = f32[3,2,6,2,128]{4,3,2,1,0:T(2,128)S(1)} collective-permute-done((f32[3,2,6,2,128]{4,3,2,1,0:T(2,128)S(1)}, f32[3,2,6,2,128]{4,3,2,1,0:T(2,128)S(1)}, u32[]{:S(2)}, u32[]{:S(2)}) %collective-permute-start.10) | collective-permute-done | bytes 36896 | tf_op jit(solution)/shard_map/ppermute | solution.py:352
  77.0 1.8 %collective-permute-done.9 = f32[3,2,6,2,128]{4,3,2,1,0:T(2,128)S(1)} collective-permute-done((f32[3,2,6,2,128]{4,3,2,1,0:T(2,128)S(1)}, f32[3,2,6,2,128]{4,3,2,1,0:T(2,128)S(1)}, u32[]{:S(2)}, u32[]{:S(2)}) %collective-permute-start.9) | collective-permute-done | bytes 36896 | tf_op jit(solution)/shard_map/ppermute | solution.py:351
  78.9 0.2 collective-permute-start.11
  79.1 1.1 collective-permute-start.12
  80.3 3.7 %all-to-all-start.1 = ((f32[128,1,128]{2,1,0:T(1,128)}), f32[128,1,128]{2,1,0:T(1,128)S(1)}, u32[]{:S(2)}, u32[]{:S(2)}) async-start(f32[128,1,128]{2,1,0:T(1,128)} %bitcast.11), calls=%async_computation.1 | async-start | bytes 131072 | tf_op jit(solution)/shard_map/all_to_all | solution.py:383
  84.0 0.1 pad_maximum_fusion.1.s_ref
  84.2 9.6 %all-to-all-done.1 = f32[128,1,128]{2,1,0:T(1,128)S(1)} async-done(((f32[128,1,128]{2,1,0:T(1,128)}), f32[128,1,128]{2,1,0:T(1,128)S(1)}, u32[]{:S(2)}, u32[]{:S(2)}) %all-to-all-start.1) | async-done | bytes 65568 | tf_op jit(solution)/shard_map/all_to_all | solution.py:383
  93.7 0.2 combine.4
  93.9 12.8 %sweep.6 = (f32[128,128]{1,0:T(8,128)}, f32[3,6,6,2,128]{4,3,2,1,0:T(2,128)S(1)}, f32[8,8,128]{2,1,0:T(8,128)S(1)}) custom-call(f32[10,10,2,128]{3,2,1,0:T(2,128)S(1)} %get-tuple-element.37.pos_ref, f32[6,6,2,128]{3,2,1,0:T(2,128)S(1)} %copy.30.base_ref, f32[8,8,128]{2,1,0:T(8,128)S(1)} %slice_bitcast_fusion.code_ref, f32[8,8,128]{2,1,0:T(8,128)S(1)} %pad.4.own_ref, ...), custom_call_target="tpu_custom_call" | custom-call | flops 40000000 | bytes 400000 | tf_op jit(solution)/shard_map/sweep/pallas_call | solution.py:261
  106.8 1.4 collective-permute-start.13
  108.2 3.7 %collective-permute-done.13 = f32[3,2,6,2,128]{4,3,2,1,0:T(2,128)S(1)} collective-permute-done((f32[3,2,6,2,128]{4,3,2,1,0:T(2,128)S(1)}, f32[3,2,6,2,128]{4,3,2,1,0:T(2,128)S(1)}, u32[]{:S(2)}, u32[]{:S(2)}) %collective-permute-start.13) | collective-permute-done | bytes 36896 | tf_op jit(solution)/shard_map/ppermute | solution.py:351
  112.0 0.8 collective-permute-start.15
  112.8 0.2 collective-permute-start.16
  113.0 4.8 %all-to-all-start.2 = ((f32[128,1,128]{2,1,0:T(1,128)}), f32[128,1,128]{2,1,0:T(1,128)S(1)}, u32[]{:S(2)}, u32[]{:S(2)}) async-start(f32[128,1,128]{2,1,0:T(1,128)} %bitcast.14), calls=%async_computation.2 | async-start | bytes 131072 | tf_op jit(solution)/shard_map/all_to_all | solution.py:383
  117.9 0.1 pad_maximum_fusion.2.s_ref
  118.0 9.6 %all-to-all-done.2 = f32[128,1,128]{2,1,0:T(1,128)S(1)} async-done(((f32[128,1,128]{2,1,0:T(1,128)}), f32[128,1,128]{2,1,0:T(1,128)S(1)}, u32[]{:S(2)}, u32[]{:S(2)}) %all-to-all-start.2) | async-done | bytes 65568 | tf_op jit(solution)/shard_map/all_to_all | solution.py:383
  127.6 0.2 combine.5
  127.8 12.8 %sweep.7 = (f32[128,128]{1,0:T(8,128)}, f32[3,6,6,2,128]{4,3,2,1,0:T(2,128)S(1)}, f32[8,8,128]{2,1,0:T(8,128)S(1)}) custom-call(f32[10,10,2,128]{3,2,1,0:T(2,128)S(1)} %get-tuple-element.42.pos_ref, f32[6,6,2,128]{3,2,1,0:T(2,128)S(1)} %broadcast_in_dim.31.base_ref, f32[8,8,128]{2,1,0:T(8,128)S(1)} %slice_bitcast_fusion.code_ref, ...), custom_call_target="tpu_custom_call" | custom-call | flops 40000000 | bytes 400000 | tf_op jit(solution)/shard_map/sweep/pallas_call | solution.py:261
  140.8 0.7 collective-permute-start.17
  141.5 7.4 %all-to-all-start.3 = ((f32[128,1,128]{2,1,0:T(1,128)}), f32[128,1,128]{2,1,0:T(1,128)S(1)}, u32[]{:S(2)}, u32[]{:S(2)}) async-start(f32[128,1,128]{2,1,0:T(1,128)} %bitcast.17), calls=%async_computation.3 | async-start | bytes 131072 | tf_op jit(solution)/shard_map/all_to_all | solution.py:383
  148.9 0.1 select_convert_fusion.code_ref
  148.9 9.7 %all-to-all-done.3 = f32[128,1,128]{2,1,0:T(1,128)S(1)} async-done(((f32[128,1,128]{2,1,0:T(1,128)}), f32[128,1,128]{2,1,0:T(1,128)S(1)}, u32[]{:S(2)}, u32[]{:S(2)}) %all-to-all-start.3) | async-done | bytes 65568 | tf_op jit(solution)/shard_map/all_to_all | solution.py:383
  158.7 0.8 finish.1
  (54 shorter events, 0.8 us)
Async XLA Ops:
  0.6 0.8 copy-start.2
  1.5 0.7 copy-start.1
  2.3 0.7 collective-permute-start
  3.0 10.6 %collective-permute-start.1 = (f32[1,2,6,3,128]{4,2,1,3,0:T(8,128)S(1)}, f32[1,2,6,3,128]{4,2,1,3,0:T(8,128)S(1)}, u32[]{:S(2)}, u32[]{:S(2)}) collective-permute-start(f32[1,2,6,3,128]{4,2,1,3,0:T(8,128)S(1)} %get-tuple-element.81), channel_id=1, source_target_pairs={{0,97},{1,96},{2,99},{3,98},{4,101},{5,100},{6,103},{7,102},{30,12... | collective-permute-start | bytes 55304 | tf_op jit(solution)/shard_map/ppermute | solution.py:351
  12.2 3.3 %collective-permute-start.2 = (f32[1,2,6,3,128]{4,2,1,3,0:T(8,128)S(1)}, f32[1,2,6,3,128]{4,2,1,3,0:T(8,128)S(1)}, u32[]{:S(2)}, u32[]{:S(2)}) collective-permute-start(f32[1,2,6,3,128]{4,2,1,3,0:T(8,128)S(1)} %get-tuple-element.82), channel_id=1, source_target_pairs={{0,17},{1,16},{2,19},{3,18},{4,21},{5,20},{6,23},{7,22},{30,15},{3... | collective-permute-start | bytes 55304 | tf_op jit(solution)/shard_map/ppermute | solution.py:352
  15.5 1.8 %collective-permute-start.4 = (f32[1,10,2,3,128]{4,2,1,3,0:T(2,128)S(1)}, f32[1,10,2,3,128]{4,2,1,3,0:T(2,128)S(1)}, u32[]{:S(2)}, u32[]{:S(2)}) collective-permute-start(f32[1,10,2,3,128]{4,2,1,3,0:T(2,128)S(1)} %broadcast_select_fusion.26), channel_id=1, source_target_pairs={{0,1},{1,0},{2,3},{3,2},{4,5},{5,4},{6,7},{7,6},{30,31},{31,30},{2... | collective-permute-start | bytes 92168 | tf_op jit(solution)/shard_map/ppermute | solution.py:352
  15.9 3.3 %collective-permute-start.3 = (f32[1,10,2,3,128]{4,2,1,3,0:T(2,128)S(1)}, f32[1,10,2,3,128]{4,2,1,3,0:T(2,128)S(1)}, u32[]{:S(2)}, u32[]{:S(2)}) collective-permute-start(f32[1,10,2,3,128]{4,2,1,3,0:T(2,128)S(1)} %get-tuple-element.54), channel_id=1, source_target_pairs={{0,25},{1,2},{2,1},{3,4},{4,3},{5,6},{6,5},{7,30},{30,7},{31,28},{... | collective-permute-start | bytes 92168 | tf_op jit(solution)/shard_map/ppermute | solution.py:351
  19.3 0.9 copy-start
  33.1 4.7 %collective-permute-start.5 = (f32[3,2,6,2,128]{4,3,2,1,0:T(2,128)S(1)}, f32[3,2,6,2,128]{4,3,2,1,0:T(2,128)S(1)}, u32[]{:S(2)}, u32[]{:S(2)}) collective-permute-start(f32[3,2,6,2,128]{4,3,2,1,0:T(2,128)S(1)} %get-tuple-element.73), channel_id=1, source_target_pairs={{0,97},{1,96},{2,99},{3,98},{4,101},{5,100},{6,103},{7,102},{30,12... | collective-permute-start | bytes 110600 | tf_op jit(solution)/shard_map/ppermute | solution.py:351
  34.4 3.4 %collective-permute-start.6 = (f32[3,2,6,2,128]{4,3,2,1,0:T(2,128)S(1)}, f32[3,2,6,2,128]{4,3,2,1,0:T(2,128)S(1)}, u32[]{:S(2)}, u32[]{:S(2)}) collective-permute-start(f32[3,2,6,2,128]{4,3,2,1,0:T(2,128)S(1)} %get-tuple-element.74), channel_id=1, source_target_pairs={{0,17},{1,16},{2,19},{3,18},{4,21},{5,20},{6,23},{7,22},{30,15},{3... | collective-permute-start | bytes 110600 | tf_op jit(solution)/shard_map/ppermute | solution.py:352
  37.8 12.4 %collective-permute-start.7 = (f32[3,10,2,2,128]{4,3,2,1,0:T(2,128)S(1)}, f32[3,10,2,2,128]{4,3,2,1,0:T(2,128)S(1)}, u32[]{:S(2)}, u32[]{:S(2)}) collective-permute-start(f32[3,10,2,2,128]{4,3,2,1,0:T(2,128)S(1)} %get-tuple-element.61), channel_id=1, source_target_pairs={{0,25},{1,2},{2,1},{3,4},{4,3},{5,6},{6,5},{7,30},{30,7},{31,28},{... | collective-permute-start | bytes 184328 | tf_op jit(solution)/shard_map/ppermute | solution.py:351
  39.3 10.9 %collective-permute-start.8 = (f32[3,10,2,2,128]{4,3,2,1,0:T(2,128)S(1)}, f32[3,10,2,2,128]{4,3,2,1,0:T(2,128)S(1)}, u32[]{:S(2)}, u32[]{:S(2)}) collective-permute-start(f32[3,10,2,2,128]{4,3,2,1,0:T(2,128)S(1)} %get-tuple-element.62), channel_id=1, source_target_pairs={{0,1},{1,0},{2,3},{3,2},{4,5},{5,4},{6,7},{7,6},{30,31},{31,30},{2... | collective-permute-start | bytes 184328 | tf_op jit(solution)/shard_map/ppermute | solution.py:352
  44.7 15.3 %all-to-all-start = ((f32[128,1,128]{2,1,0:T(1,128)}), f32[128,1,128]{2,1,0:T(1,128)S(1)}, u32[]{:S(2)}, u32[]{:S(2)}) async-start(f32[128,1,128]{2,1,0:T(1,128)} %bitcast.8), calls=%async_computation | async-start | bytes 131072 | tf_op jit(solution)/shard_map/all_to_all | solution.py:383
  73.1 4.0 %collective-permute-start.10 = (f32[3,2,6,2,128]{4,3,2,1,0:T(2,128)S(1)}, f32[3,2,6,2,128]{4,3,2,1,0:T(2,128)S(1)}, u32[]{:S(2)}, u32[]{:S(2)}) collective-permute-start(f32[3,2,6,2,128]{4,3,2,1,0:T(2,128)S(1)} %get-tuple-element.72), channel_id=1, source_target_pairs={{0,17},{1,16},{2,19},{3,18},{4,21},{5,20},{6,23},{7,22},{30,15},{3... | collective-permute-start | bytes 110600 | tf_op jit(solution)/shard_map/ppermute | solution.py:352
  74.2 4.6 %collective-permute-start.9 = (f32[3,2,6,2,128]{4,3,2,1,0:T(2,128)S(1)}, f32[3,2,6,2,128]{4,3,2,1,0:T(2,128)S(1)}, u32[]{:S(2)}, u32[]{:S(2)}) collective-permute-start(f32[3,2,6,2,128]{4,3,2,1,0:T(2,128)S(1)} %get-tuple-element.71), channel_id=1, source_target_pairs={{0,97},{1,96},{2,99},{3,98},{4,101},{5,100},{6,103},{7,102},{30,12... | collective-permute-start | bytes 110600 | tf_op jit(solution)/shard_map/ppermute | solution.py:351
  78.9 5.0 %collective-permute-start.11 = (f32[3,10,2,2,128]{4,3,2,1,0:T(2,128)S(1)}, f32[3,10,2,2,128]{4,3,2,1,0:T(2,128)S(1)}, u32[]{:S(2)}, u32[]{:S(2)}) collective-permute-start(f32[3,10,2,2,128]{4,3,2,1,0:T(2,128)S(1)} %get-tuple-element.59), channel_id=1, source_target_pairs={{0,25},{1,2},{2,1},{3,4},{4,3},{5,6},{6,5},{7,30},{30,7},{31,28},{... | collective-permute-start | bytes 184328 | tf_op jit(solution)/shard_map/ppermute | solution.py:351
  79.1 4.8 %collective-permute-start.12 = (f32[3,10,2,2,128]{4,3,2,1,0:T(2,128)S(1)}, f32[3,10,2,2,128]{4,3,2,1,0:T(2,128)S(1)}, u32[]{:S(2)}, u32[]{:S(2)}) collective-permute-start(f32[3,10,2,2,128]{4,3,2,1,0:T(2,128)S(1)} %get-tuple-element.60), channel_id=1, source_target_pairs={{0,1},{1,0},{2,3},{3,2},{4,5},{5,4},{6,7},{7,6},{30,31},{31,30},{2... | collective-permute-start | bytes 184328 | tf_op jit(solution)/shard_map/ppermute | solution.py:352
  80.3 13.5 %all-to-all-start.1 = ((f32[128,1,128]{2,1,0:T(1,128)}), f32[128,1,128]{2,1,0:T(1,128)S(1)}, u32[]{:S(2)}, u32[]{:S(2)}) async-start(f32[128,1,128]{2,1,0:T(1,128)} %bitcast.11), calls=%async_computation.1 | async-start | bytes 131072 | tf_op jit(solution)/shard_map/all_to_all | solution.py:383
  106.8 5.2 %collective-permute-start.13 = (f32[3,2,6,2,128]{4,3,2,1,0:T(2,128)S(1)}, f32[3,2,6,2,128]{4,3,2,1,0:T(2,128)S(1)}, u32[]{:S(2)}, u32[]{:S(2)}) collective-permute-start(f32[3,2,6,2,128]{4,3,2,1,0:T(2,128)S(1)} %get-tuple-element.69), channel_id=1, source_target_pairs={{0,97},{1,96},{2,99},{3,98},{4,101},{5,100},{6,103},{7,102},{30,12... | collective-permute-start | bytes 110600 | tf_op jit(solution)/shard_map/ppermute | solution.py:351
  108.2 3.7 %collective-permute-start.14 = (f32[3,2,6,2,128]{4,3,2,1,0:T(2,128)S(1)}, f32[3,2,6,2,128]{4,3,2,1,0:T(2,128)S(1)}, u32[]{:S(2)}, u32[]{:S(2)}) collective-permute-start(f32[3,2,6,2,128]{4,3,2,1,0:T(2,128)S(1)} %get-tuple-element.70), channel_id=1, source_target_pairs={{0,17},{1,16},{2,19},{3,18},{4,21},{5,20},{6,23},{7,22},{30,15},{3... | collective-permute-start | bytes 110600 | tf_op jit(solution)/shard_map/ppermute | solution.py:352
  112.0 5.8 %collective-permute-start.15 = (f32[3,10,2,2,128]{4,3,2,1,0:T(2,128)S(1)}, f32[3,10,2,2,128]{4,3,2,1,0:T(2,128)S(1)}, u32[]{:S(2)}, u32[]{:S(2)}) collective-permute-start(f32[3,10,2,2,128]{4,3,2,1,0:T(2,128)S(1)} %get-tuple-element.57), channel_id=1, source_target_pairs={{0,25},{1,2},{2,1},{3,4},{4,3},{5,6},{6,5},{7,30},{30,7},{31,28},{... | collective-permute-start | bytes 184328 | tf_op jit(solution)/shard_map/ppermute | solution.py:351
  112.8 5.0 %collective-permute-start.16 = (f32[3,10,2,2,128]{4,3,2,1,0:T(2,128)S(1)}, f32[3,10,2,2,128]{4,3,2,1,0:T(2,128)S(1)}, u32[]{:S(2)}, u32[]{:S(2)}) collective-permute-start(f32[3,10,2,2,128]{4,3,2,1,0:T(2,128)S(1)} %get-tuple-element.58), channel_id=1, source_target_pairs={{0,1},{1,0},{2,3},{3,2},{4,5},{5,4},{6,7},{7,6},{30,31},{31,30},{2... | collective-permute-start | bytes 184328 | tf_op jit(solution)/shard_map/ppermute | solution.py:352
  113.0 14.6 %all-to-all-start.2 = ((f32[128,1,128]{2,1,0:T(1,128)}), f32[128,1,128]{2,1,0:T(1,128)S(1)}, u32[]{:S(2)}, u32[]{:S(2)}) async-start(f32[128,1,128]{2,1,0:T(1,128)} %bitcast.14), calls=%async_computation.2 | async-start | bytes 131072 | tf_op jit(solution)/shard_map/all_to_all | solution.py:383
  140.8 17.9 %collective-permute-start.17 = (f32[8,6,6,128]{3,2,1,0:T(8,128)S(1)}, f32[8,6,6,128]{3,2,1,0:T(8,128)S(1)}, u32[]{:S(2)}, u32[]{:S(2)}) collective-permute-start(f32[8,6,6,128]{3,2,1,0:T(8,128)S(1)} %bitcast_dynamic-update-slice_fusion), channel_id=1, source_target_pairs={{0,0},{1,1},{2,2},{3,3},{4,4},{5,5},{6,6},{7,7},{30,8},{31,9},{28,... | collective-permute-start | bytes 442376 | tf_op jit(solution)/shard_map/ppermute | solution.py:336
  141.5 17.2 %all-to-all-start.3 = ((f32[128,1,128]{2,1,0:T(1,128)}), f32[128,1,128]{2,1,0:T(1,128)S(1)}, u32[]{:S(2)}, u32[]{:S(2)}) async-start(f32[128,1,128]{2,1,0:T(1,128)} %bitcast.17), calls=%async_computation.3 | async-start | bytes 131072 | tf_op jit(solution)/shard_map/all_to_all | solution.py:383
